TPU v7x, 16 devices: a whole 2x2x2 slice. The times are simulated.
16 devices in a mesh: dp: 2 (over z), tp: 8 (over y, x, core).
Axes of the slice: x: 2, y: 2, z: 2, core: 2. Of those that a mesh axis runs over, the one named last changes fastest.
Arguments:
- x_in: bfloat16 [8192, 4096], P(('dp', 'tp')), parts along dimension 0
- grad_out: bfloat16 [8192, 4096], P(('dp', 'tp')), parts along dimension 0
- positions: int32 [8192], P('dp'), parts along dimension 0
- norm_gain: float32 [4096], replicated
- w_query: bfloat16 [4096, 4096], P(None, 'tp')
- w_key: bfloat16 [4096, 1024], replicated
- w_value: bfloat16 [4096, 1024], replicated
- w_out: bfloat16 [4096, 4096], P('tp')
Outputs:
- output 1: bfloat16 [8192, 4096], P(('dp', 'tp')), parts along dimension 0
- output 2: bfloat16 [8192, 4096], P(('dp', 'tp')), parts along dimension 0
- output 3: bfloat16 [8192, 4096], P('dp', 'tp'), parts along dimension 0
- output 4: float32 [8192, 1024], P('dp', 'tp'), parts along dimension 0
- output 5: float32 [8192, 1024], P('dp', 'tp'), parts along dimension 0
- output 6: bfloat16 [8192, 4096], P(('dp', 'tp')), parts along dimension 0
- output 7: float32 [8192], P('dp'), parts along dimension 0
There are 2 independent parts. A program takes and returns all parts, laid end to end along the dimension named above; an argument that names none is the same for every part.
All inputs are finite; a program needn't handle non-finite values.
Results may differ from a plain program's by a relative error of at most 0.0183672.
Values are sent between devices in bfloat16 or wider.
A program may use at most 1 GiB of HBM per device.

v0:
```python
import functools
import jax
import jax.numpy as jnp
from jax import lax
from jax.sharding import PartitionSpec as P

HEAD_DIM = 128
QUERY_BLOCK = 256
SCORE_SCALE = HEAD_DIM ** -0.5
ROPE_THETA = 1000000.0
NORM_EPS = 1e-05


def rope_tables(positions):
    exponents = jnp.arange(0, HEAD_DIM, 2, dtype=jnp.float32) / HEAD_DIM
    angles = positions.astype(jnp.float32)[..., None] * jnp.power(ROPE_THETA, -exponents)
    return jnp.cos(angles), jnp.sin(angles)


def apply_rope(tensor, cos_t, sin_t):
    half_dim = HEAD_DIM // 2
    t_f32 = tensor.astype(jnp.float32)
    lead_half = t_f32[..., :half_dim]
    tail_half = t_f32[..., half_dim:]
    return jnp.concatenate([lead_half * cos_t - tail_half * sin_t, tail_half * cos_t + lead_half * sin_t], axis=-1).astype(jnp.bfloat16)


def norm_forward(x_f32, norm_gain):
    inv_rms = lax.rsqrt(jnp.mean(x_f32 * x_f32, axis=-1, keepdims=True) + NORM_EPS)
    x_hat = x_f32 * inv_rms
    return (x_hat * norm_gain).astype(jnp.bfloat16), x_hat, inv_rms


def norm_backward(d_hidden, x_hat, inv_rms, norm_gain):
    d_f32 = d_hidden.astype(jnp.float32)
    d_gain = jnp.sum(d_f32 * x_hat, axis=-2)
    value_a6 = d_f32 * norm_gain
    d_input = inv_rms * (value_a6 - x_hat * jnp.mean(value_a6 * x_hat, axis=-1, keepdims=True))
    return d_input, d_gain


def attend(positions, q_raw, k_raw, v_raw):
    seq_len, heads_loc = q_raw.shape[0], q_raw.shape[1]
    cos_t, sin_t = rope_tables(positions)
    q_rot = apply_rope(q_raw, cos_t[:, None, :], sin_t[:, None, :])
    k_rot = apply_rope(k_raw, cos_t, sin_t)
    col_idx = lax.iota(jnp.int32, seq_len)
    key_doc = positions - col_idx
    num_blk = seq_len // QUERY_BLOCK

    def one_block(blk_item):
        q_blk, q_pos, row_idx = blk_item
        scores = jnp.einsum('qhd,sd->hqs', q_blk, k_rot, preferred_element_type=jnp.float32) * SCORE_SCALE
        keep_mask = (col_idx[None, :] <= row_idx[:, None]) & (key_doc[None, :] == (q_pos - row_idx)[:, None])
        scores = jnp.where(keep_mask[None], scores, -1e30)
        prob_blk = jax.nn.softmax(scores, axis=-1).astype(jnp.bfloat16)
        return jnp.einsum('hqs,sd->qhd', prob_blk, v_raw, preferred_element_type=jnp.float32).astype(jnp.bfloat16)

    blk_out = lax.map(jax.checkpoint(one_block), (q_rot.reshape(num_blk, QUERY_BLOCK, heads_loc, HEAD_DIM), positions.reshape(num_blk, QUERY_BLOCK), col_idx.reshape(num_blk, QUERY_BLOCK)))
    return blk_out.reshape(seq_len, heads_loc, HEAD_DIM)


def share_sum(part_val, tp_size, kv_repeat):
    summed = part_val
    for offset in range(1, kv_repeat):
        pair_perm = [(src_dev, (src_dev // kv_repeat) * kv_repeat + (src_dev + offset) % kv_repeat) for src_dev in range(tp_size)]
        summed = summed + lax.ppermute(part_val, 'tp', pair_perm)
    return summed


def solution(mesh):
    tp_size = mesh.shape['tp']
    contract_rows = (((0,), (0,)), ((), ()))
    contract_cols = (((1,), (1,)), ((), ()))

    def device_step(x_blk, dy_blk, pos_all, norm_gain, wq_loc, wk_all, wv_all, wo_loc):
        kv_heads = wk_all.shape[1] // HEAD_DIM
        kv_repeat = tp_size // kv_heads
        heads_loc = wq_loc.shape[1] // HEAD_DIM
        kv_index = lax.axis_index('tp') // kv_repeat
        wk_loc = lax.dynamic_slice_in_dim(wk_all, kv_index * HEAD_DIM, HEAD_DIM, axis=1)
        wv_loc = lax.dynamic_slice_in_dim(wv_all, kv_index * HEAD_DIM, HEAD_DIM, axis=1)
        x_f32 = x_blk.astype(jnp.float32)
        hidden, x_hat, inv_rms = norm_forward(x_f32, norm_gain)
        h_full = lax.all_gather(hidden, 'tp', axis=0, tiled=True)
        seq_len = h_full.shape[0]
        q_raw = jnp.dot(h_full, wq_loc, preferred_element_type=jnp.float32).astype(jnp.bfloat16)
        k_raw = jnp.dot(h_full, wk_loc, preferred_element_type=jnp.float32).astype(jnp.bfloat16)
        v_raw = jnp.dot(h_full, wv_loc, preferred_element_type=jnp.float32).astype(jnp.bfloat16)
        attn_out, attn_pull = jax.vjp(functools.partial(attend, pos_all), q_raw.reshape(seq_len, heads_loc, HEAD_DIM), k_raw, v_raw)
        o_flat = attn_out.reshape(seq_len, heads_loc * HEAD_DIM)
        mix_part = jnp.dot(o_flat, wo_loc, preferred_element_type=jnp.float32).astype(jnp.bfloat16)
        mix_rows = lax.psum_scatter(mix_part, 'tp', scatter_dimension=0, tiled=True)
        result = (x_f32 + mix_rows.astype(jnp.float32)).astype(jnp.bfloat16)
        dy_full = lax.all_gather(dy_blk, 'tp', axis=0, tiled=True)
        d_wo = lax.dot_general(o_flat, dy_full, contract_rows, preferred_element_type=jnp.float32).astype(jnp.bfloat16)
        d_o = lax.dot_general(dy_full, wo_loc, contract_cols, preferred_element_type=jnp.float32).astype(jnp.bfloat16)
        d_q, d_k, d_v = attn_pull(d_o.reshape(seq_len, heads_loc, HEAD_DIM))
        dq_flat = d_q.reshape(seq_len, heads_loc * HEAD_DIM)
        d_wq = lax.dot_general(h_full, dq_flat, contract_rows, preferred_element_type=jnp.float32).astype(jnp.bfloat16)
        dwk_part = lax.dot_general(h_full, d_k, contract_rows, preferred_element_type=jnp.float32)
        dwv_part = lax.dot_general(h_full, d_v, contract_rows, preferred_element_type=jnp.float32)
        dh_part = (lax.dot_general(dq_flat, wq_loc, contract_cols, preferred_element_type=jnp.float32) + lax.dot_general(d_k, wk_loc, contract_cols, preferred_element_type=jnp.float32) + lax.dot_general(d_v, wv_loc, contract_cols, preferred_element_type=jnp.float32)).astype(jnp.bfloat16)
        dh_rows = lax.psum_scatter(dh_part, 'tp', scatter_dimension=0, tiled=True)
        d_input, dg_part = norm_backward(dh_rows, x_hat, inv_rms, norm_gain)
        grad_x = (dy_blk.astype(jnp.float32) + d_input).astype(jnp.bfloat16)
        d_gain = lax.psum(dg_part, 'tp')
        d_wk = share_sum(dwk_part, tp_size, kv_repeat)
        d_wv = share_sum(dwv_part, tp_size, kv_repeat)
        return result, grad_x, d_wq, d_wk, d_wv, d_wo, d_gain

    specs_in = (P(('dp', 'tp'), None), P(('dp', 'tp'), None), P('dp'), P(), P(None, 'tp'), P(), P(), P('tp', None))
    specs_out = (P(('dp', 'tp'), None), P(('dp', 'tp'), None), P('dp', 'tp'), P('dp', 'tp'), P('dp', 'tp'), P(('dp', 'tp'), None), P('dp'))
    return jax.shard_map(device_step, mesh=mesh, in_specs=specs_in, out_specs=specs_out, check_vma=False)
```

profile of v0, /device:TPU:0, one launch (start us, length us, event | category | flops | bytes accessed | tf_op | source)
XLA Modules:
  0.0 1951.6 jit_solution(7788641727125081893)
XLA Ops:
  18.1 158.4 %all-gather.3.cloned.1.call-done = bf16[4096,4096]{1,0:T(8,128)(2,1)} async-done(((bf16[512,4096]{1,0:T(8,128)(2,1)}), bf16[4096,4096]{1,0:T(8,128)(2,1)}) %all-gather.3.cloned.1.call-update) | async-done | bytes 33554448 | tf_op jit(solution)/shard_map/all_gather | solution.py:85
  176.6 17.6 fusion.79
  204.4 130.9 %all-gather.5.cloned.1.call-done = bf16[4096,4096]{1,0:T(8,128)(2,1)} async-done(((bf16[512,4096]{1,0:T(8,128)(2,1)}), bf16[4096,4096]{1,0:T(8,128)(2,1)}) %all-gather.5.cloned.1.call-update) | async-done | bytes 33554448 | tf_op jit(solution)/shard_map/all_gather | solution.py:95
  335.3 24.6 %convolution_convert_fusion.5 = bf16[4096,512]{1,0:T(8,128)(2,1)} fusion(bf16[4096,4096]{1,0:T(8,128)(2,1)} %all-gather.5.cloned.1.call-done, bf16[512,4096]{1,0:T(8,128)(2,1)} %param.19), kind=kOutput, calls=%fused_computation.100 | convolution fusion | flops 17181966336 | bytes 41943040 | tf_op jit(solution)/shard_map/dot_general | solution.py:97
  366.8 23.8 %convolution_convert_fusion.6 = bf16[4096,512]{0,1:T(8,128)(2,1)} fusion(bf16[4096,4096]{1,0:T(8,128)(2,1)} %all-gather.3.cloned.1.call-done, bf16[4096,512]{1,0:T(8,128)(2,1)} %param.16), kind=kOutput, calls=%fused_computation.101 | convolution fusion | flops 17181966336 | bytes 41943040 | tf_op jit(solution)/shard_map/dot_general | solution.py:87
  411.1 11.0 subtract_convert_fusion
  444.3 16.3 convolution_convert_fusion.7
  463.7 748.5 %while.32 = (s32[]{:T(128)}, bf16[4096,128]{1,0:T(8,128)(2,1)}, bf16[4096,128]{1,0:T(8,128)(2,1)S(1)}, bf16[16,256,4,128]{3,1,0,2:T(8,128)(2,1)}, bf16[16,256,4,...) while((s32[]{:T(128)}, bf16[4096,128]{1,0:T(8,128)(2,1)}, ...), condition=%wide.region_10.11_spmd.clone, body=%wide.region_6.10_spmd.clone.sunk | while | flops 5503451136 | bytes 223239456 | solution.py:59
  494.1 10.6 fusion.178
  540.8 10.6 fusion.178
  587.6 10.6 fusion.178
  634.3 10.6 fusion.178
  681.0 10.6 fusion.178
  774.5 10.6 fusion.178
  821.3 10.6 fusion.178
  868.0 10.6 fusion.178
  914.8 10.6 fusion.178
  961.5 10.6 fusion.178
  1008.3 10.6 fusion.178
  1101.8 10.6 fusion.178
  1241.4 30.4 %fusion.117 = f32[4096,4096]{1,0:T(8,128)} fusion(bf16[4096,512]{0,1:T(8,128)(2,1)} %bitcast.233, bf16[4096,512]{1,0:T(8,128)(2,1)} %param.16), kind=kOutput, calls=%fused_computation.145 | convolution fusion | flops 17179869184 | bytes 75497472 | tf_op jit(solution)/shard_map/dot_general | solution.py:103
  1271.8 24.4 %fusion.96 = f32[4096,4096]{1,0:T(8,128)} fusion(bf16[4096,1024]{1,0:T(8,128)(2,1)} %param.17, s32[]{:T(128)S(6)} %select_n.46, f32[4096,64]{0,1:T(8,128)S(1)} %get-tuple-element.516, f32[4096,64]{0,1:T(8,128)S(1)} %get-tuple-element.515), kind=kOutput, calls=%fused_computation.127 | convolution fusion | flops 4296015872 | bytes 70254592 | tf_op jit(solution)/shard_map/dot_general | solution.py:103
  1296.2 53.8 %add_convert_fusion = bf16[4096,4096]{1,0:T(8,128)(2,1)} fusion(f32[4096,4096]{1,0:T(8,128)} %fusion.117, f32[4096,4096]{1,0:T(8,128)} %fusion.96, bf16[4096,128]{1,0:T(8,128)(2,1)S(1)} %get-tuple-element.335, bf16[4096,1024]{1,0:T(8,128)(2,1)} %param.18, s32[]{:T(128)S(6)} %select_n.46), kind=kOutput, calls=%fused_computation.74 | convolution fusion | flops 4345298944 | bytes 169869312 | tf_op jit(solution)/shard_map/dot_general | solution.py:103
  1351.5 345.3 %while.31 = (s32[]{:T(128)}, bf16[16,256,4,128]{3,1,2,0:T(8,128)(2,1)}, s32[16,256]{1,0:T(8,128)S(1)}, s32[1,4096]{1,0:T(1,128)S(1)}, s32[16,256]{1,0:T(8,128)S(...) while((s32[]{:T(128)}, ...), condition=%wide.region_4.5_spmd.clone, body=%wide.region_1.4_spmd.clone.sunk | while | flops 2175930624 | bytes 38306928 | solution.py:59
  1352.8 13.4 fusion.167
  1366.1 11.9 fusion.168
  1379.0 13.3 fusion.167
  1404.0 10.9 fusion.167
  1425.4 10.8 fusion.167
  1446.5 10.9 fusion.167
  1467.8 10.8 fusion.167
  1488.9 10.9 fusion.167
  1510.4 10.9 fusion.167
  1531.7 10.8 fusion.167
  1552.7 10.8 fusion.167
  1573.4 10.8 fusion.167
  1594.1 10.8 fusion.167
  1614.8 10.8 fusion.167
  1635.6 10.8 fusion.167
  1656.3 10.8 fusion.167
  1677.1 10.8 fusion.167
  1711.2 22.2 %convolution_convert_fusion.2 = bf16[4096,4096]{1,0:T(8,128)(2,1)} fusion(bf16[4096,512]{0,1:T(8,128)(2,1)S(1)} %bitcast.235, bf16[512,4096]{1,0:T(8,128)(2,1)S(1)} %copy-done.27), kind=kOutput, calls=%fused_computation.75 | convolution fusion | flops 17196646400 | bytes 41943040 | tf_op jit(solution)/shard_map/dot_general | solution.py:92
  1735.0 21.3 %fusion.99 = f32[4096,128]{1,0:T(8,128)} fusion(bf16[4096,4096]{1,0:T(8,128)(2,1)} %all-gather.3.cloned.1.call-done, f32[4096,64]{0,1:T(8,128)S(1)} %copy-done.8, f32[4096,64]{0,1:T(8,128)S(1)} %copy-done.6), kind=kOutput, calls=%fused_computation.130 | convolution fusion | flops 4296015872 | bytes 37748736 | tf_op jit(solution)/shard_map/dot_general | solution.py:101
  1756.3 22.8 %fusion.118 = f32[4096,128]{1,0:T(8,128)} fusion(bf16[4096,4096]{1,0:T(8,128)(2,1)} %all-gather.3.cloned.1.call-done, bf16[4096,128]{1,0:T(8,128)(2,1)S(1)} %copy-done.14), kind=kOutput, calls=%fused_computation.146 | convolution fusion | flops 4294967296 | bytes 36700160 | tf_op jit(solution)/shard_map/dot_general | solution.py:102
  1779.1 24.7 %convolution_convert_fusion.4 = bf16[4096,512]{1,0:T(8,128)(2,1)} fusion(bf16[4096,4096]{1,0:T(8,128)(2,1)} %all-gather.3.cloned.1.call-done, bf16[4096,512]{0,1:T(8,128)(2,1)S(1)} %bitcast.234), kind=kOutput, calls=%fused_computation.99 | convolution fusion | flops 17181966336 | bytes 41943040 | tf_op jit(solution)/shard_map/dot_general | solution.py:100
  1803.9 22.8 %convolution_convert_fusion.3 = bf16[512,4096]{1,0:T(8,128)(2,1)} fusion(bf16[4096,512]{0,1:T(8,128)(2,1)S(1)} %bitcast.236, bf16[4096,4096]{1,0:T(8,128)(2,1)} %all-gather.5.cloned.1.call-done), kind=kOutput, calls=%fused_computation.98 | convolution fusion | flops 17181966336 | bytes 41943040 | tf_op jit(solution)/shard_map/dot_general | solution.py:96
  1832.3 26.7 %psum.7 = f32[4096]{0:T(1024)} all-reduce(f32[4096]{0:T(1024)S(1)} %get-tuple-element.457), channel_id=1, replica_groups=mesh['dp'=2,'tp'=8] {'tp'}, use_global_device_ids=true, to_apply=%region_14.15 | all-reduce | flops 4096 | bytes 32768 | tf_op jit(solution)/shard_map/psum | solution.py:107
  1859.0 75.6 %reduce-scatter.3.cloned.1.call-done = bf16[512,4096]{1,0:T(8,128)(2,1)} async-done(((bf16[4096,4096]{1,0:T(8,128)(2,1)}), bf16[512,4096]{1,0:T(8,128)(2,1)}) %reduce-scatter.3.cloned.1.call-update) | async-done | bytes 4194320 | tf_op jit(solution)/shard_map/reduce_scatter | solution.py:93
  (548 shorter events, 908.8 us)
Async XLA Ops:
  7.2 169.4 %all-gather.3.cloned.1.call-start = ((), (), s32[]{:S(2)}) async-start(), calls=%async_computation.2 | async-start | bytes 37748736 | tf_op jit(solution)/shard_map/all_gather | solution.py:85
  10.9 7.2 copy-start.22
  16.7 318.7 %all-gather.5.cloned.1.call-start = ((), (), s32[]{:S(2)}) async-start(), calls=%async_computation.4 | async-start | bytes 37748736 | tf_op jit(solution)/shard_map/all_gather | solution.py:95
  17.4 1809.3 %reduce-scatter.5.cloned.1.call-start = ((), (), s32[]{:S(2)}) async-start(), calls=%async_computation.5 | async-start | bytes 37748736 | tf_op jit(solution)/shard_map/reduce_scatter | solution.py:104
  18.1 176.1 %copy-start.25 = (f32[64]{0:T(128)}, f32[64]{0:T(128)S(1)}, u32[]{:S(2)}) copy-start(f32[64]{0:T(128)S(1)} %negate_power_fusion) | copy-start | bytes 772
  18.1 176.0 %copy-start.20 = (f32[4096]{0:T(1024)}, f32[4096]{0:T(1024)S(1)}, u32[]{:S(2)}) copy-start(f32[4096]{0:T(1024)S(1)} %get-tuple-element.521) | copy-start | bytes 49156
  202.4 208.7 %copy-start.1 = (f32[4096,64]{1,0:T(8,128)}, f32[4096,64]{1,0:T(8,128)S(1)}, u32[]{:S(2)}) copy-start(f32[4096,64]{1,0:T(8,128)S(1)} %copy.48) | copy-start | bytes 3145732
  444.3 19.4 copy-start.12
  444.3 19.4 copy-start.15
  463.6 750.6 %copy-start.21 = (f32[4096]{0:T(1024)S(1)}, f32[4096]{0:T(1024)}, u32[]{:S(2)}) copy-start(f32[4096]{0:T(1024)} %copy-done.20) | copy-start | bytes 49156
  463.6 750.6 %copy-start.26 = (f32[64]{0:T(128)S(1)}, f32[64]{0:T(128)}, u32[]{:S(2)}) copy-start(f32[64]{0:T(128)} %copy-done.25) | copy-start | bytes 772
  477.4 6.2 copy-start.28
  494.1 10.7 copy-start.17
  524.2 6.2 copy-start.28
  540.8 10.7 copy-start.17
  570.9 6.2 copy-start.28
  587.5 10.7 copy-start.17
  617.7 6.2 copy-start.28
  634.3 10.7 copy-start.17
  664.4 6.2 copy-start.28
  681.0 10.7 copy-start.17
  711.2 6.2 copy-start.28
  727.8 10.7 copy-start.17
  757.9 6.2 copy-start.28
  774.5 10.7 copy-start.17
  804.7 6.2 copy-start.28
  821.3 10.7 copy-start.17
  851.4 6.2 copy-start.28
  868.0 10.7 copy-start.17
  898.2 6.2 copy-start.28
  914.8 10.7 copy-start.17
  961.5 10.7 copy-start.17
  991.6 6.2 copy-start.28
  1008.3 10.7 copy-start.17
  1055.0 10.7 copy-start.17
  1101.7 10.7 copy-start.17
  1148.5 10.7 copy-start.17
  1195.2 10.7 copy-start.17
  1212.2 84.0 %copy-start.13 = (bf16[4096,128]{1,0:T(8,128)(2,1)}, bf16[4096,128]{1,0:T(8,128)(2,1)S(1)}, u32[]{:S(2)}) copy-start(bf16[4096,128]{1,0:T(8,128)(2,1)S(1)} %get-tuple-element.335) | copy-start | bytes 3145732
  1218.4 53.4 %copy-start.5 = (f32[4096,64]{0,1:T(8,128)}, f32[4096,64]{0,1:T(8,128)S(1)}, u32[]{:S(2)}) copy-start(f32[4096,64]{0,1:T(8,128)S(1)} %get-tuple-element.515) | copy-start | bytes 3145732
  1218.4 53.4 %copy-start.7 = (f32[4096,64]{0,1:T(8,128)}, f32[4096,64]{0,1:T(8,128)S(1)}, u32[]{:S(2)}) copy-start(f32[4096,64]{0,1:T(8,128)S(1)} %get-tuple-element.516) | copy-start | bytes 3145732
  1350.0 584.5 %reduce-scatter.3.cloned.1.call-start = ((), (), s32[]{:S(2)}) async-start(), calls=%async_computation.3 | async-start | bytes 37748736 | tf_op jit(solution)/shard_map/reduce_scatter | solution.py:93
  1704.6 6.6 copy-start.27
  1735.0 21.4 %copy-start.14 = (bf16[4096,128]{1,0:T(8,128)(2,1)S(1)}, bf16[4096,128]{1,0:T(8,128)(2,1)}, u32[]{:S(2)}) copy-start(bf16[4096,128]{1,0:T(8,128)(2,1)} %copy-done.13) | copy-start | bytes 3145732
  1756.3 22.8 %copy-start.9 = (bf16[4096,4,128]{0,2,1:T(8,128)(2,1)S(1)}, bf16[4096,4,128]{0,2,1:T(8,128)(2,1)}, u32[]{:S(2)}) copy-start(bf16[4096,4,128]{0,2,1:T(8,128)(2,1)} %copy.58) | copy-start | bytes 12582916
  1779.1 24.7 %copy-start.11 = (bf16[64,8,16,256]{3,1,2,0:T(8,128)(2,1)S(1)}, bf16[64,8,16,256]{3,1,2,0:T(8,128)(2,1)}, u32[]{:S(2)}) copy-start(bf16[64,8,16,256]{3,1,2,0:T(8,128)(2,1)} %copy-done.10) | copy-start | bytes 12582916
  1803.9 22.9 %copy-start.19 = (f32[4096]{0:T(1024)S(1)}, f32[4096]{0:T(1024)}, u32[]{:S(2)}) copy-start(f32[4096]{0:T(1024)} %param.15) | copy-start | bytes 49156
  1803.9 22.9 %copy-start.24 = (f32[512]{0:T(512)S(1)}, f32[512]{0:T(512)}, u32[]{:S(2)}) copy-start(f32[512]{0:T(512)} %copy-done.23) | copy-start | bytes 6148
  (46 other events, 193.8 us)
Sparse Core Ops, SparseCore 0:
  16.8 159.6 all-gather.2
  178.4 156.9 all-gather.4
  1350.1 199.8 reduce-scatter.4
  1733.6 200.9 reduce-scatter.2
where the time goes:
time: 1960 us; the launch traced here: 1950 us
  matrix products  1050 us (54%)
  waiting for transfers between devices  366 us (19%)
  other arithmetic  353 us (18%)
  local copies, waits for them, and re-layouts  136 us (7%)
  blocking collectives  26.7 us (1%)
    dot_general x48, matrix products, one_block(): jnp.einsum('hqs,sd->qhd', prob_blk, v_raw, preferred_element_type=jnp.flo...  415 us
    sub x16, matrix products, one_block(): prob_blk = jax.nn.softmax(scores, axis=-1).astype(jnp.bfloat16)  179 us
    mul x16, other arithmetic, one_block(): jnp.einsum('qhd,sd->hqs', q_blk, k_rot, preferred_element_type=jnp.float32)  170 us
    all_gather x1, waiting for transfers between devices, device_step(): h_full = lax.all_gather(hidden, 'tp', axis=0, tiled=True)  158 us
    dot_general x48, matrix products, one_block(): jnp.einsum('qhd,sd->hqs', q_blk, k_rot, preferred_element_type=jnp.float32)  154 us
    all_gather x1, waiting for transfers between devices, device_step(): dy_full = lax.all_gather(dy_blk, 'tp', axis=0, tiled=True)  131 us
    reduce_scatter x1, waiting for transfers between devices, device_step(): mix_rows = lax.psum_scatter(mix_part, 'tp', scatter_dimension=0, tiled=True)  75.6 us
    reduce_sum x16, other arithmetic, one_block(): prob_blk = jax.nn.softmax(scores, axis=-1).astype(jnp.bfloat16)  70.9 us
  transfers between devices with their start and end apart: 4, of which 3 were waited for; matrix products, arithmetic and copies ran while one was open for 26% of the time, Pallas kernels for 0%

commit v1 on v0

v1 whole, which is shorter than its diff:
```python
import functools
import jax
import jax.numpy as jnp
from jax import lax
from jax.experimental import pallas as pl
from jax.experimental.pallas import tpu as pltpu
from jax.experimental.layout import Layout, with_layout_constraint
from jax.sharding import PartitionSpec as P

HEAD_DIM = 128
SCORE_SCALE = HEAD_DIM ** -0.5
LOG2_SCALE = SCORE_SCALE * 1.4426950408889634
ROPE_THETA = 1000000.0
NORM_EPS = 1e-05
MASKED = -1e30
BQ = 256
BK = 512
VMEM_LIMIT = 60 * 1024 * 1024
NT = (((1,), (1,)), ((), ()))
TN = (((0,), (0,)), ((), ()))
F32 = jnp.float32
BF16 = jnp.bfloat16


def rope_tables(positions):
    exponents = jnp.arange(0, HEAD_DIM, 2, dtype=F32) / HEAD_DIM
    angles = positions.astype(F32)[..., None] * jnp.power(ROPE_THETA, -exponents)
    cos_t, sin_t = jnp.cos(angles), jnp.sin(angles)
    return jnp.concatenate([cos_t, cos_t], axis=-1), jnp.concatenate([-sin_t, sin_t], axis=-1)


def rope(x, cos_t, sin_t):
    x = x.astype(F32)
    return (x * cos_t + pltpu.roll(x, HEAD_DIM // 2, 1) * sin_t).astype(BF16)


def rope_back(x, cos_t, sin_t):
    x = x.astype(F32)
    return (x * cos_t - pltpu.roll(x, HEAD_DIM // 2, 1) * sin_t).astype(BF16)


def stack_heads(x, heads):
    return jnp.concatenate([x[:, h * HEAD_DIM:(h + 1) * HEAD_DIM] for h in range(heads)], axis=0)


def key_loops(i, lo_ref, full_ref, bq, bk, body):
    first = lo_ref[i]
    below = (i * bq) // bk
    last = ((i + 1) * bq + bk - 1) // bk
    mid = jnp.minimum(jnp.maximum(full_ref[i], first), last)
    mid_end = jnp.maximum(mid, jnp.minimum(below, last))
    lax.fori_loop(first, mid, functools.partial(body, True), None)
    lax.fori_loop(mid, mid_end, functools.partial(body, False), None)
    lax.fori_loop(mid_end, last, functools.partial(body, True), None)


def fwd_kernel(heads, lo_ref, full_ref, q_ref, k_ref, v_ref, cos_ref, sin_ref, cosf_ref, sinf_ref, ds_ref, o_ref, lse_ref, k_s, m_s, l_s, acc_s):
    i = pl.program_id(0)
    bq, bk = BQ, BK
    rows = heads * bq

    @pl.when(i == 0)
    def _():
        k_s[...] = rope(k_ref[...], cosf_ref[...], sinf_ref[...])

    cos_t, sin_t = cos_ref[...], sin_ref[...]
    q4 = jnp.concatenate([rope(q_ref[:, h * HEAD_DIM:(h + 1) * HEAD_DIM], cos_t, sin_t) for h in range(heads)], axis=0)
    m_s[...] = jnp.full_like(m_s, MASKED)
    l_s[...] = jnp.zeros_like(l_s)
    acc_s[...] = jnp.zeros_like(acc_s)

    def body(masked, j, _):
        start = pl.multiple_of(j * bk, bk)
        kj = k_s[pl.ds(start, bk), :]
        vj = v_ref[pl.ds(start, bk), :]
        s = lax.dot_general(q4, kj, NT, preferred_element_type=F32) * LOG2_SCALE
        if masked:
            q_idx = i * bq + lax.broadcasted_iota(jnp.int32, (bq, bk), 0)
            k_idx = start + lax.broadcasted_iota(jnp.int32, (bq, bk), 1)
            keep = (k_idx <= q_idx) & (k_idx >= ds_ref[...])
            s = jnp.concatenate([jnp.where(keep, s[h * bq:(h + 1) * bq], MASKED) for h in range(heads)], axis=0)
        m_prev = m_s[...]
        m_new = jnp.maximum(m_prev, jnp.max(s, axis=1, keepdims=True))
        p = jnp.exp2(s - jnp.tile(m_new, (1, bk // HEAD_DIM)))
        alpha = jnp.exp2(m_prev - m_new)
        l_s[...] = l_s[...] * alpha + jnp.sum(p, axis=1, keepdims=True)
        m_s[...] = m_new
        acc_s[...] = acc_s[...] * alpha + jnp.dot(p.astype(BF16), vj, preferred_element_type=F32)

    key_loops(i, lo_ref, full_ref, bq, bk, body)
    l_all = l_s[...]
    o4 = (acc_s[...] / l_all).astype(BF16)
    for h in range(heads):
        o_ref[:, h * HEAD_DIM:(h + 1) * HEAD_DIM] = o4[h * bq:(h + 1) * bq]
    lse = m_s[...] + jnp.log2(l_all)
    lse_ref[0] = lse.T[0:1, :]


def bwd_kernel(heads, n_blk, lo_ref, full_ref, q_ref, k_ref, v_ref, o_ref, do_ref, lse_ref, cos_ref, sin_ref, cosf_ref, sinf_ref, ds_ref, out_ref, k_s, dq_s, dk_s, dv_s):
    i = pl.program_id(0)
    bq, bk = BQ, BK
    rows = heads * bq
    width = heads * HEAD_DIM

    @pl.when(i == 0)
    def _():
        k_s[...] = rope(k_ref[...], cosf_ref[...], sinf_ref[...])
        dk_s[...] = jnp.zeros_like(dk_s)
        dv_s[...] = jnp.zeros_like(dv_s)

    cos_t, sin_t = cos_ref[...], sin_ref[...]
    q4 = jnp.concatenate([rope(q_ref[:, h * HEAD_DIM:(h + 1) * HEAD_DIM], cos_t, sin_t) for h in range(heads)], axis=0)
    do4 = stack_heads(do_ref[...], heads)
    o4 = stack_heads(o_ref[...], heads)
    delta = jnp.sum((do4.astype(F32) * o4.astype(F32)).T, axis=0, keepdims=True)
    lse = lse_ref[0]
    dq_s[...] = jnp.zeros_like(dq_s)

    def body(masked, j, _):
        start = pl.multiple_of(j * bk, bk)
        kj = k_s[pl.ds(start, bk), :]
        vj = v_ref[pl.ds(start, bk), :]
        s = lax.dot_general(kj, q4, NT, preferred_element_type=F32) * LOG2_SCALE
        if masked:
            q_idx = i * bq + lax.broadcasted_iota(jnp.int32, (bk, bq), 1)
            k_idx = start + lax.broadcasted_iota(jnp.int32, (bk, bq), 0)
            keep = (k_idx <= q_idx) & (k_idx >= ds_ref[0])
            s = jnp.concatenate([jnp.where(keep, s[:, h * bq:(h + 1) * bq], MASKED) for h in range(heads)], axis=1)
        p = jnp.exp2(s - lse)
        dp = lax.dot_general(vj, do4, NT, preferred_element_type=F32)
        dv_s[pl.ds(start, bk), :] += jnp.dot(p.astype(BF16), do4, preferred_element_type=F32)
        d_s = (p * (dp - delta)).astype(BF16)
        dk_s[pl.ds(start, bk), :] += jnp.dot(d_s, q4, preferred_element_type=F32)
        dq_s[...] += lax.dot_general(d_s, kj, TN, preferred_element_type=F32)

    key_loops(i, lo_ref, full_ref, bq, bk, body)
    row0 = pl.multiple_of(i * bq, bq)
    for h in range(heads):
        dq = (dq_s[h * bq:(h + 1) * bq, :] * SCORE_SCALE).astype(BF16)
        out_ref[pl.ds(row0, bq), h * HEAD_DIM:(h + 1) * HEAD_DIM] = rope_back(dq, cos_t, sin_t)

    @pl.when(i == n_blk - 1)
    def _():
        dk = (dk_s[...] * SCORE_SCALE).astype(BF16)
        out_ref[:, width:width + HEAD_DIM] = rope_back(dk, cosf_ref[...], sinf_ref[...])
        out_ref[:, width + HEAD_DIM:width + 2 * HEAD_DIM] = dv_s[...].astype(BF16)


def attention_specs(seq, heads):
    width = heads * HEAD_DIM
    q_spec = pl.BlockSpec((BQ, width), lambda i, *_: (i, 0))
    k_spec = pl.BlockSpec((seq, HEAD_DIM), lambda i, *_: (0, heads))
    v_spec = pl.BlockSpec((seq, HEAD_DIM), lambda i, *_: (0, heads + 1))
    tab_spec = pl.BlockSpec((BQ, HEAD_DIM), lambda i, *_: (i, 0))
    tabf_spec = pl.BlockSpec((seq, HEAD_DIM), lambda i, *_: (0, 0))
    row_spec = pl.BlockSpec((1, 1, heads * BQ), lambda i, *_: (i, 0, 0))
    return q_spec, k_spec, v_spec, tab_spec, tabf_spec, row_spec


def attend_forward(lo, full, qkv, cos_t, sin_t, doc_start, heads):
    seq = qkv.shape[0]
    n_blk = seq // BQ
    q_spec, k_spec, v_spec, tab_spec, tabf_spec, row_spec = attention_specs(seq, heads)
    return pl.pallas_call(
        functools.partial(fwd_kernel, heads),
        out_shape=(jax.ShapeDtypeStruct((seq, heads * HEAD_DIM), BF16), jax.ShapeDtypeStruct((n_blk, 1, heads * BQ), F32)),
        grid_spec=pltpu.PrefetchScalarGridSpec(
            num_scalar_prefetch=2, grid=(n_blk,),
            in_specs=[q_spec, k_spec, v_spec, tab_spec, tab_spec, tabf_spec, tabf_spec, pl.BlockSpec((BQ, 1), lambda i, *_: (i, 0))],
            out_specs=[q_spec, row_spec],
            scratch_shapes=[pltpu.VMEM((seq, HEAD_DIM), BF16)] + [pltpu.VMEM((heads * BQ, HEAD_DIM), F32)] * 3),
        compiler_params=pltpu.CompilerParams(dimension_semantics=("arbitrary",), vmem_limit_bytes=VMEM_LIMIT),
        cost_estimate=pl.CostEstimate(flops=4 * heads * seq * seq // 2 * HEAD_DIM, bytes_accessed=16 * 2 ** 20, transcendentals=heads * seq * seq // 2),
        name="attend_fwd",
    )(lo, full, qkv, qkv, qkv, cos_t, sin_t, cos_t, sin_t, doc_start[:, None])


def attend_backward(lo, full, qkv, o, d_o, lse, cos_t, sin_t, doc_start, heads):
    seq = qkv.shape[0]
    n_blk = seq // BQ
    width = heads * HEAD_DIM
    q_spec, k_spec, v_spec, tab_spec, tabf_spec, row_spec = attention_specs(seq, heads)
    return pl.pallas_call(
        functools.partial(bwd_kernel, heads, n_blk),
        out_shape=jax.ShapeDtypeStruct((seq, width + 2 * HEAD_DIM), BF16),
        grid_spec=pltpu.PrefetchScalarGridSpec(
            num_scalar_prefetch=2, grid=(n_blk,),
            in_specs=[q_spec, k_spec, v_spec, q_spec, q_spec, row_spec, tab_spec, tab_spec, tabf_spec, tabf_spec, pl.BlockSpec((1, 1, BQ), lambda i, *_: (i, 0, 0))],
            out_specs=pl.BlockSpec((seq, width + 2 * HEAD_DIM), lambda i, *_: (0, 0)),
            scratch_shapes=[pltpu.VMEM((seq, HEAD_DIM), BF16), pltpu.VMEM((heads * BQ, HEAD_DIM), F32), pltpu.VMEM((seq, HEAD_DIM), F32), pltpu.VMEM((seq, HEAD_DIM), F32)]),
        compiler_params=pltpu.CompilerParams(dimension_semantics=("arbitrary",), vmem_limit_bytes=VMEM_LIMIT),
        cost_estimate=pl.CostEstimate(flops=10 * heads * seq * seq // 2 * HEAD_DIM, bytes_accessed=24 * 2 ** 20, transcendentals=heads * seq * seq // 2),
        name="attend_bwd",
    )(lo, full, qkv, qkv, qkv, o, d_o, lse, cos_t, sin_t, cos_t, sin_t, doc_start.reshape(n_blk, 1, BQ))


def norm_forward(x_f32, norm_gain):
    inv_rms = lax.rsqrt(jnp.mean(x_f32 * x_f32, axis=-1, keepdims=True) + NORM_EPS)
    x_hat = x_f32 * inv_rms
    return (x_hat * norm_gain).astype(BF16), x_hat, inv_rms


def dot32(a, b, dims=(((1,), (0,)), ((), ()))):
    return lax.dot_general(a, b, dims, preferred_element_type=F32)


def row_major(x):
    return with_layout_constraint(x, Layout(major_to_minor=tuple(range(x.ndim))))


def sum_over_tp(value, tp_size):
    step = 1
    while step < tp_size:
        value = value + lax.ppermute(value, 'tp', [(d, d ^ step) for d in range(tp_size)])
        step *= 2
    return value


def solution(mesh):
    tp_size = mesh.shape['tp']
    dp_size = mesh.shape['dp']

    def device_step(x_blk, dy_blk, positions, norm_gain, wq_loc, wk_all, wv_all, wo_loc):
        heads = wq_loc.shape[1] // HEAD_DIM
        width = heads * HEAD_DIM
        rows, d_model = x_blk.shape
        tp_idx, dp_idx = lax.axis_index('tp'), lax.axis_index('dp')
        wk_loc = lax.dynamic_slice_in_dim(wk_all, tp_idx * HEAD_DIM, HEAD_DIM, axis=1)
        wv_loc = lax.dynamic_slice_in_dim(wv_all, tp_idx * HEAD_DIM, HEAD_DIM, axis=1)
        wqkv = jnp.concatenate([wq_loc, wk_loc, wv_loc], axis=1)
        wq_t = wq_loc.T
        share = width // dp_size
        wq_share = lax.dynamic_slice_in_dim(wq_t, dp_idx * share, share, axis=0)
        wo_share = lax.dynamic_slice_in_dim(wo_loc, dp_idx * share, share, axis=0)

        x_f32 = x_blk.astype(F32)
        hidden, x_hat, inv_rms = norm_forward(x_f32, norm_gain)
        h_full = lax.all_gather(hidden, 'tp', axis=0, tiled=True)
        seq = h_full.shape[0]
        dy_in, h_full = lax.optimization_barrier((dy_blk, h_full))
        dy_full = lax.all_gather(dy_in, 'tp', axis=0, tiled=True)

        cos_t, sin_t = rope_tables(positions)
        doc_start = lax.iota(jnp.int32, seq) - positions
        lo = doc_start[::BQ] // BK
        full = (doc_start[BQ - 1::BQ] + BK - 1) // BK

        qkv = dot32(h_full, wqkv).astype(BF16)
        wq_share, qkv = lax.optimization_barrier((wq_share, qkv))
        wq_full_t = lax.all_gather(row_major(wq_share), ('tp', 'dp'), axis=0, tiled=True)
        o, lse = attend_forward(lo, full, qkv, cos_t, sin_t, doc_start, heads)
        o_got = row_major(lax.all_to_all(row_major(o.reshape(tp_size, rows, width)), 'tp', 0, 0))
        dy_full, o_got = lax.optimization_barrier((dy_full, o_got))
        o_rows = row_major(o_got.transpose(1, 0, 2)).reshape(rows, tp_size * width)

        d_o = dot32(dy_full, wo_loc, NT).astype(BF16)
        wo_share, d_o = lax.optimization_barrier((wo_share, d_o))
        wo_full = lax.all_gather(row_major(wo_share), ('tp', 'dp'), axis=0, tiled=True)
        d_qkv = attend_backward(lo, full, qkv, o, d_o, lse, cos_t, sin_t, doc_start, heads)
        got = row_major(lax.all_to_all(row_major(d_qkv.reshape(tp_size, rows, width + 2 * HEAD_DIM)), 'tp', 0, 0))
        got = row_major(got.transpose(1, 0, 2))
        dq_rows = got[:, :, :width].reshape(rows, tp_size * width)
        dk_rows = got[:, :, width:width + HEAD_DIM].reshape(rows, tp_size * HEAD_DIM)
        dv_rows = got[:, :, width + HEAD_DIM:].reshape(rows, tp_size * HEAD_DIM)

        d_wo = dot32(o, dy_full, TN).astype(BF16)
        d_wq = dot32(h_full, d_qkv[:, :width], TN).astype(BF16)
        d_wkv = dot32(h_full, d_qkv[:, width:], TN)
        d_wk, d_wv = d_wkv[:, :HEAD_DIM], d_wkv[:, HEAD_DIM:]

        d_hidden = (dot32(dq_rows, wq_full_t) + (dot32(dk_rows, wk_all, NT) + dot32(dv_rows, wv_all, NT))).astype(BF16)
        d_f32 = d_hidden.astype(F32)
        d_gain = sum_over_tp(jnp.sum(d_f32 * x_hat, axis=0), tp_size)
        scaled = d_f32 * norm_gain
        d_input = inv_rms * (scaled - x_hat * jnp.mean(scaled * x_hat, axis=-1, keepdims=True))
        grad_x = (dy_blk.astype(F32) + d_input).astype(BF16)
        result = (x_f32 + dot32(o_rows, wo_full)).astype(BF16)
        return result, grad_x, d_wq, d_wk, d_wv, d_wo, d_gain

    specs_in = (P(('dp', 'tp'), None), P(('dp', 'tp'), None), P('dp'), P(), P(None, 'tp'), P(), P(), P('tp', None))
    specs_out = (P(('dp', 'tp'), None), P(('dp', 'tp'), None), P('dp', 'tp'), P('dp', 'tp'), P('dp', 'tp'), P(('dp', 'tp'), None), P('dp'))
    return jax.shard_map(device_step, mesh=mesh, in_specs=specs_in, out_specs=specs_out, check_vma=False)
```

time: 1960 us -> 731 us (0.37)
  matrix products: 1050 us -> 199 us
  other arithmetic: 353 us -> 24.5 us
  Pallas kernels: 0 us -> 163 us
  local copies, waits for them, and re-layouts: 136 us -> 34 us
  waiting for transfers between devices: 366 us -> 281 us
  blocking collectives: 26.7 us -> 0 us
    dot_general x108 -> x9, matrix products: 874 us -> 199 us  [dot32(): return lax.dot_general(a, b, dims, preferred_element_type=F32)]
    sub x16 -> x0, matrix products: 179 us -> none  [one_block(): prob_blk = jax.nn.softmax(scores, axis=-1).astype(jnp.bfloat16)]
    mul x16 -> x0, other arithmetic: 170 us -> none  [one_block(): jnp.einsum('qhd,sd->hqs', q_blk, k_rot, preferred_element_type=jnp.float32)]
    pallas_call x0 -> x2, Pallas kernels: none -> 163 us  [the longest x1 99.7 us: attend_backward(): pl.pallas_call(functools.partial(bwd_kernel, heads, n_blk), out_shape=jax...]
    all_gather x1 -> x3, waiting for transfers between devices: 131 us -> 21.2 us  [the longest x1 21.2 us: device_step(): lax.all_gather(row_major(wo_share), ('tp', 'dp'), axis=0, tiled=True)]
    all_to_all x0 -> x2, waiting for transfers between devices: none -> 96 us  [the longest x1 74.9 us: device_step(): lax.all_to_all(row_major(o.reshape(tp_size, rows, width)), 'tp', 0, 0)]
    reduce_sum x17 -> x0, other arithmetic: 76.5 us -> none  [the longest x16 70.9 us: one_block(): prob_blk = jax.nn.softmax(scores, axis=-1).astype(jnp.bfloat16)]
    reduce_scatter x2 -> x0, waiting for transfers between devices: 75.6 us -> none  [the longest x1 75.6 us: device_step(): mix_rows = lax.psum_scatter(mix_part, 'tp', scatter_dimension=0, tiled=True)]
  transfers between devices with their start and end apart: 4 -> 9, of which waited for: 3 -> 5; matrix products, arithmetic and copies ran while one was open for 26% -> 31% of each run, Pallas kernels for 0% -> 22%
where the time goes in v1:
time: 731 us; the launch traced here: 728 us
  waiting for transfers between devices  281 us (38%)
  matrix products  199 us (27%)
  Pallas kernels  163 us (22%)
  local copies, waits for them, and re-layouts  34 us (5%)
  other arithmetic  24.5 us (3%)
  between operations  14.1 us (2%)
  starting transfers between devices  12.5 us (2%)
    dot_general x9, matrix products, dot32(): return lax.dot_general(a, b, dims, preferred_element_type=F32)  199 us
    all_gather x1, waiting for transfers between devices, device_step(): h_full = lax.all_gather(hidden, 'tp', axis=0, tiled=True)  160 us
    pallas_call x1, Pallas kernels, attend_backward(): pl.pallas_call(functools.partial(bwd_kernel, heads, n_blk), out_shape=jax...  99.7 us
    all_to_all x1, waiting for transfers between devices, device_step(): lax.all_to_all(row_major(o.reshape(tp_size, rows, width)), 'tp', 0, 0)  74.9 us
    pallas_call x1, Pallas kernels, attend_forward(): pl.pallas_call(functools.partial(fwd_kernel, heads), out_shape=(jax.Shape...  63.2 us
    all_gather x1, waiting for transfers between devices, device_step(): lax.all_gather(row_major(wo_share), ('tp', 'dp'), axis=0, tiled=True)  21.2 us
    all_to_all x1, waiting for transfers between devices, device_step(): lax.all_to_all(row_major(d_qkv.reshape(tp_size, rows, width + 2 * HEAD_DI...  21 us
  transfers between devices with their start and end apart: 9, of which 5 were waited for; matrix products, arithmetic and copies ran while one was open for 31% of the time, Pallas kernels for 22%

profile of v1, /device:TPU:0, one launch (start us, length us, event | category | flops | bytes accessed | tf_op | source)
XLA Modules:
  0.0 728.1 jit_solution(8812268727714710520)
XLA Ops:
  7.2 0.0 all-gather.5.cloned.1.call-start
  7.2 3.2 fusion.11
  10.5 0.6 copy-done.6
  11.1 4.4 fusion.8
  15.4 0.0 all-gather.5.cloned.1.call-update
  15.4 0.0 all-gather.7.cloned.1.call-start
  15.5 159.8 %all-gather.5.cloned.1.call-done = bf16[4096,4096]{1,0:T(8,128)(2,1)} async-done(((bf16[512,4096]{1,0:T(8,128)(2,1)}), bf16[4096,4096]{1,0:T(8,128)(2,1)}) %all-gather.5.cloned.1.call-update) | async-done | bytes 33554448 | tf_op jit(solution)/shard_map/all_gather | solution.py:238
  175.3 0.0 all-gather.7.cloned.1.call-update
  175.3 0.3 all-gather.11.cloned.1.call-start
  175.7 1.7 constant_dynamic-slice_fusion.3
  177.4 3.0 copy.22
  180.4 2.1 constant_dynamic-slice_fusion.1
  182.5 34.5 %convolution_convert_fusion.q_ref.k_ref.v_ref = bf16[4096,768]{1,0:T(8,128)(2,1)} fusion(bf16[4096,4096]{1,0:T(8,128)(2,1)} %all-gather.5.cloned.1.call-done, bf16[4096,128]{1,0:T(8,128)(2,1)S(1)} %get-tuple-element.41, bf16[4096,128]{1,0:T(8,128)(2,1)S(1)} %get-tuple-element.42, bf16[4096,512]{1,0:T(8,128)(2,1)} %param.12), kind=kOutput, calls=%fused_computation.18 | convolution fusion | flops 25791823872 | bytes 46137344 | tf_op jit(solution)/shard_map/dot_general | solution.py:204
  217.1 0.1 slice.28
  217.2 0.1 slice.27
  217.3 2.0 copy.19.ds_ref
  219.2 0.6 and_select_fusion
  219.8 7.5 %fusion.26 = (f32[4096,64]{1,0:T(8,128)S(1)}, f32[4096,64]{1,0:T(8,128)S(1)}, f32[4096,64]{1,0:T(8,128)S(1)}) fusion(f32[64]{0:T(128)S(1)} %negate_power_fusion, f32[4096]{0:T(1024)S(1)} %get-tuple-element.36), kind=kLoop, calls=%fused_computation.40 | loop fusion | flops 524288 | bytes 3162368 | tf_op jit(solution)/shard_map/neg | solution.py:29
  227.3 3.2 pad_maximum_fusion
  230.4 63.2 %attend_fwd.1 = (bf16[4096,512]{1,0:T(8,128)(2,1)}, f32[16,1,1024]{2,1,0:T(1,128)}) custom-call(s32[16]{0:T(128)} %get-tuple-element.40.lo_ref, s32[16]{0:T(128)} %get-tuple-element.39.full_ref, bf16[4096,768]{1,0:T(8,128)(2,1)} %convolution_convert_fusion.q_ref.k_ref.v_ref, bf16[4096,768]{1,0:T(8,128)(2,1)} %convolution_convert_fusion.q_ref.k_ref.v_ref, ...), custom_call_target="tpu_custom_call" | custom-call | flops 17179869184 | bytes 16777216 | tf_op jit(solution)/shard_map/attend_fwd/pallas_call | solution.py:164
  293.6 4.6 all-to-all-start
  298.2 0.0 all-gather.9.cloned.1.call-start
  298.3 3.2 constant_dynamic-slice_fusion
  301.4 74.9 %all-to-all-done = bf16[8,512,512]{2,1,0:T(8,128)(2,1)} async-done(((bf16[8,512,512]{2,1,0:T(8,128)(2,1)}), bf16[8,512,512]{2,1,0:T(8,128)(2,1)}, u32[]{:S(2)}, u32[]{:S(2)}) %all-to-all-start) | async-done | bytes 4194336 | tf_op jit(solution)/shard_map/all_to_all | solution.py:252
  376.4 24.6 %convolution_convert_fusion.3.do_ref = bf16[4096,512]{1,0:T(8,128)(2,1)} fusion(bf16[4096,4096]{1,0:T(8,128)(2,1)} %all-gather.7.cloned.1.call-done, bf16[512,4096]{1,0:T(8,128)(2,1)} %param.15), kind=kOutput, calls=%fused_computation.27 | convolution fusion | flops 17181966336 | bytes 41943040 | tf_op jit(solution)/shard_map/dot_general | solution.py:204
  400.9 0.0 all-gather.9.cloned.1.call-update
  401.0 99.7 %attend_bwd.1 = bf16[4096,768]{1,0:T(8,128)(2,1)} custom-call(s32[16]{0:T(128)} %get-tuple-element.40.lo_ref, s32[16]{0:T(128)} %get-tuple-element.39.full_ref, bf16[4096,768]{1,0:T(8,128)(2,1)} %convolution_convert_fusion.q_ref.k_ref.v_ref, bf16[4096,768]{1,0:T(8,128)(2,1)} %convolution_convert_fusion.q_ref.k_ref.v_ref, ...), custom_call_target="tpu_custom_call" | custom-call | flops 42949672960 | bytes 25165824 | tf_op jit(solution)/shard_map/attend_bwd/pallas_call | solution.py:183
  500.7 5.8 all-to-all-start.1
  506.4 24.4 %convolution_convert_fusion.1 = bf16[512,4096]{1,0:T(8,128)(2,1)} fusion(bf16[4096,512]{1,0:T(8,128)(2,1)} %get-tuple-element.20.o_ref, bf16[4096,4096]{1,0:T(8,128)(2,1)} %all-gather.7.cloned.1.call-done), kind=kOutput, calls=%fused_computation.25 | convolution fusion | flops 17181966336 | bytes 41943040 | tf_op jit(solution)/shard_map/dot_general | solution.py:204
  530.8 17.7 %fusion.19 = f32[4096,256]{1,0:T(8,128)} fusion(bf16[4096,4096]{1,0:T(8,128)(2,1)} %all-gather.5.cloned.1.call-done, bf16[4096,768]{1,0:T(8,128)(2,1)S(1)} %bitcast.43), kind=kOutput, calls=%fused_computation.31 | convolution fusion | flops 8589934592 | bytes 39845888 | tf_op jit(solution)/shard_map/dot_general | solution.py:204
  548.5 24.1 %convolution_convert_fusion.2 = bf16[4096,512]{1,0:T(8,128)(2,1)} fusion(bf16[4096,4096]{1,0:T(8,128)(2,1)} %all-gather.5.cloned.1.call-done, bf16[4096,768]{1,0:T(8,128)(2,1)S(1)} %bitcast.43), kind=kOutput, calls=%fused_computation.26 | convolution fusion | flops 17181966336 | bytes 41943040 | tf_op jit(solution)/shard_map/dot_general | solution.py:204
  572.6 21.0 %all-to-all-done.1 = bf16[8,512,768]{2,1,0:T(8,128)(2,1)} async-done(((bf16[8,512,768]{2,1,0:T(8,128)(2,1)}), bf16[8,512,768]{2,1,0:T(8,128)(2,1)}, u32[]{:S(2)}, u32[]{:S(2)}) %all-to-all-start.1) | async-done | bytes 6291488 | tf_op jit(solution)/shard_map/all_to_all | solution.py:260
  593.6 6.7 copy.39
  600.3 0.3 slice.36
  600.7 4.4 copy.24
  605.0 0.1 fusion.28
  605.2 7.2 fusion.23
  612.4 25.2 %fusion.31 = f32[512,4096]{1,0:T(8,128)} fusion(bf16[512,4096]{1,0:T(8,128)(2,1)} %bitcast.46, bf16[4096,4096]{1,0:T(8,128)(2,1)} %all-gather.11.cloned.1.call-done), kind=kOutput, calls=%fused_computation.61 | convolution fusion | flops 17179869184 | bytes 46137344 | tf_op jit(solution)/shard_map/dot_general | solution.py:204
  637.6 14.7 %fusion.10 = (f32[4096]{0:T(1024)S(1)}, f32[512]{0:T(512)S(1)}, bf16[512,4096]{1,0:T(8,128)(2,1)}) fusion(bf16[512,4096]{1,0:T(8,128)(2,1)S(1)} %copy-done.1, f32[512]{0:T(512)S(1)} %copy-done.7, f32[4096]{0:T(1024)S(1)} %copy-done.5, f32[512,4096]{1,0:T(8,128)} %fusion.31, f32[512,4096]{1,0:T(8,128)} %fusion.23, bf16[4096,1024]{1,0:T(8,128)(2,1)} %param.14, ...), kind=kOutput, calls=%fused_computation.14 | convolution fusion | flops 4318031360 | bytes 34639872 | tf_op jit(solution)/shard_map/dot_general | solution.py:204
  652.3 4.5 fusion.29
  656.8 5.1 copy.23
  662.0 0.0 collective-permute-start.1
  662.0 4.2 collective-permute-done.1
  666.2 1.7 collective-permute-start.2
  667.9 5.0 fusion.7
  672.9 0.6 add.56
  673.6 21.2 %all-gather.9.cloned.1.call-done = bf16[4096,4096]{1,0:T(8,128)(2,1)} async-done(((bf16[256,4096]{1,0:T(8,128)(2,1)}), bf16[4096,4096]{1,0:T(8,128)(2,1)}) %all-gather.9.cloned.1.call-update) | async-done | bytes 33554448 | tf_op jit(solution)/shard_map/all_gather | solution.py:258
  694.7 26.7 %fusion.12 = bf16[512,4096]{1,0:T(8,128)(2,1)} fusion(bf16[512,4096]{1,0:T(8,128)(2,1)} %param.8, bf16[512,4096]{1,0:T(8,128)(2,1)} %bitcast.45, bf16[4096,4096]{1,0:T(8,128)(2,1)} %all-gather.9.cloned.1.call-done), kind=kOutput, calls=%fused_computation.16 | convolution fusion | flops 17186160640 | bytes 46137344 | tf_op jit(solution)/shard_map/dot_general | solution.py:204
  (39 shorter events, 0.1 us)
Async XLA Ops:
  7.2 168.1 %all-gather.5.cloned.1.call-start = ((), (), s32[]{:S(2)}) async-start(), calls=%async_computation.2 | async-start | bytes 37748736 | tf_op jit(solution)/shard_map/all_gather | solution.py:238
  7.2 3.8 copy-start
  10.5 0.6 copy-start.6
  15.4 361.0 %all-gather.7.cloned.1.call-start = ((), (), s32[]{:S(2)}) async-start(), calls=%async_computation.3 | async-start | bytes 37748736 | tf_op jit(solution)/shard_map/all_gather | solution.py:241
  175.3 437.1 %all-gather.11.cloned.1.call-start = ((), (), s32[]{:S(2)}) async-start(), calls=%async_computation.5 | async-start | bytes 35651584 | tf_op jit(solution)/shard_map/all_gather | solution.py:250
  182.5 34.5 %copy-start.8 = (s32[4096]{0:T(1024)S(1)}, s32[4096]{0:T(1024)}, u32[]{:S(2)}) copy-start(s32[4096]{0:T(1024)} %param.10) | copy-start | bytes 49156
  217.0 13.4 %copy-start.4 = (s32[4096]{0:T(1024)}, s32[4096]{0:T(1024)S(1)}, u32[]{:S(2)}) copy-start(s32[4096]{0:T(1024)S(1)} %get-tuple-element.37) | copy-start | bytes 49156
  293.6 82.8 %all-to-all-start = ((bf16[8,512,512]{2,1,0:T(8,128)(2,1)}), bf16[8,512,512]{2,1,0:T(8,128)(2,1)}, u32[]{:S(2)}, u32[]{:S(2)}) async-start(bf16[8,512,512]{2,1,0:T(8,128)(2,1)} %bitcast.44), calls=%async_computation | async-start | bytes 8388608 | tf_op jit(solution)/shard_map/all_to_all | solution.py:252
  298.2 396.5 %all-gather.9.cloned.1.call-start = ((), (), s32[]{:S(2)}) async-start(), calls=%async_computation.4 | async-start | bytes 35651584 | tf_op jit(solution)/shard_map/all_gather | solution.py:258
  500.7 30.1 %slice-start = ((s8[6291456]{0:T(1024)(128)(4,1)}), s8[2097152]{0:T(1024)(128)(4,1)S(1)}, s32[]{:S(2)}) async-start(s8[6291456]{0:T(1024)(128)(4,1)} %bitcast.42), calls=%async_computation.6 | async-start | bytes 4194304
  500.7 92.9 %all-to-all-start.1 = ((bf16[8,512,768]{2,1,0:T(8,128)(2,1)}), bf16[8,512,768]{2,1,0:T(8,128)(2,1)}, u32[]{:S(2)}, u32[]{:S(2)}) async-start(bf16[8,512,768]{2,1,0:T(8,128)(2,1)} %bitcast.41), calls=%async_computation.1 | async-start | bytes 12582912 | tf_op jit(solution)/shard_map/all_to_all | solution.py:260
  506.4 24.4 %slice-start.1 = ((s8[6291456]{0:T(1024)(128)(4,1)}), s8[4194304]{0:T(1024)(128)(4,1)S(1)}, s32[]{:S(2)}) async-start(s8[6291456]{0:T(1024)(128)(4,1)} %bitcast.42), calls=%async_computation.7 | async-start | bytes 8388608
  600.3 4.9 slice-start.2
  600.7 4.5 slice-start.3
  612.4 25.2 %copy-start.1 = (bf16[512,4096]{1,0:T(8,128)(2,1)S(1)}, bf16[512,4096]{1,0:T(8,128)(2,1)}, u32[]{:S(2)}) copy-start(bf16[512,4096]{1,0:T(8,128)(2,1)} %param.8) | copy-start | bytes 12582916
  612.4 25.2 %copy-start.5 = (f32[4096]{0:T(1024)S(1)}, f32[4096]{0:T(1024)}, u32[]{:S(2)}) copy-start(f32[4096]{0:T(1024)} %param.11) | copy-start | bytes 49156
  612.4 25.2 %copy-start.7 = (f32[512]{0:T(512)S(1)}, f32[512]{0:T(512)}, u32[]{:S(2)}) copy-start(f32[512]{0:T(512)} %copy-done.6) | copy-start | bytes 6148
  652.3 9.6 %collective-permute-start = (f32[4096]{0:T(1024)S(1)}, f32[4096]{0:T(1024)S(1)}, u32[]{:S(2)}, u32[]{:S(2)}) collective-permute-start(f32[4096]{0:T(1024)S(1)} %get-tuple-element.27), channel_id=1, source_target_pairs={{0,1},{1,0},{2,3},{3,2},{4,5},{5,4},{6,7},{7,6},{8,9},{9,8},{10,11... | collective-permute-start | bytes 49160 | tf_op jit(solution)/shard_map/ppermute | solution.py:214
  656.8 11.1 %copy-start.2 = (bf16[512,4096]{1,0:T(8,128)(2,1)S(1)}, bf16[512,4096]{1,0:T(8,128)(2,1)}, u32[]{:S(2)}) copy-start(bf16[512,4096]{1,0:T(8,128)(2,1)} %param.9) | copy-start | bytes 12582916
  656.8 11.1 %copy-start.3 = (bf16[512,4096]{1,0:T(8,128)(2,1)S(1)}, bf16[512,4096]{1,0:T(8,128)(2,1)}, u32[]{:S(2)}) copy-start(bf16[512,4096]{1,0:T(8,128)(2,1)} %get-tuple-element.38) | copy-start | bytes 12582916
  662.0 4.2 collective-permute-start.1
  666.2 6.7 collective-permute-start.2
Sparse Core Ops, SparseCore 0:
  15.6 159.6 all-gather.4
  177.1 190.6 all-gather.6
  370.0 142.5 all-gather.10
  514.7 179.9 all-gather.8

commit v2 on v1

--- a/solution.py
+++ b/solution.py
@@ -216,22 +216,103 @@
     return value
 
 
+def grad_mm_kernel(width, owner_ref, *refs):
+    g_refs, w_refs, (wk_ref, wv_ref, out_ref, x_s, w_s) = refs[:4], refs[4:8], refs[8:]
+    span = width + 2 * HEAD_DIM
+
+    @pl.when(pl.program_id(0) == 0)
+    def _():
+        for p, g_ref in enumerate(g_refs):
+            x_s[:, p * span:(p + 1) * span] = g_ref[0]
+
+    for p, w_ref in enumerate(w_refs):
+        head = pl.ds(pl.multiple_of(owner_ref[p] * HEAD_DIM, HEAD_DIM), HEAD_DIM)
+        w_s[:, p * span:p * span + width] = w_ref[...]
+        w_s[:, p * span + width:p * span + width + HEAD_DIM] = wk_ref[:, head]
+        w_s[:, p * span + width + HEAD_DIM:(p + 1) * span] = wv_ref[:, head]
+    out_ref[...] = lax.dot_general(x_s[...], w_s[...], NT, preferred_element_type=F32).astype(out_ref.dtype)
+
+
+def grad_mm(owners, pieces, half, weights, wk_all, wv_all, dtype):
+    _, rows, span = pieces[0].shape
+    d_model, width = weights[0].shape
+    bn = 512
+    g_spec = pl.BlockSpec((1, rows, span), lambda j, *_: (half, 0, 0))
+    w_spec = pl.BlockSpec((bn, width), lambda j, *_: (j, 0))
+    kv_spec = pl.BlockSpec((bn, wk_all.shape[1]), lambda j, *_: (j, 0))
+    return pl.pallas_call(
+        functools.partial(grad_mm_kernel, width),
+        out_shape=jax.ShapeDtypeStruct((rows, d_model), dtype),
+        grid_spec=pltpu.PrefetchScalarGridSpec(
+            num_scalar_prefetch=1, grid=(d_model // bn,),
+            in_specs=[g_spec] * 4 + [w_spec] * 4 + [kv_spec] * 2,
+            out_specs=pl.BlockSpec((rows, bn), lambda j, *_: (0, j)),
+            scratch_shapes=[pltpu.VMEM((rows, 4 * span), BF16), pltpu.VMEM((bn, 4 * span), BF16)]),
+        compiler_params=pltpu.CompilerParams(dimension_semantics=("arbitrary",), vmem_limit_bytes=VMEM_LIMIT),
+        cost_estimate=pl.CostEstimate(flops=2 * rows * 4 * span * d_model, bytes_accessed=2 * (4 * span + 2 * rows) * d_model, transcendentals=0),
+        name="grad_mm",
+    )(owners, *pieces, *weights, wk_all, wv_all)
+
+
+def mix_mm_kernel(width, *refs):
+    o_refs, w_refs, (out_ref, x_s, w_s) = refs[:4], refs[4:8], refs[8:]
+
+    @pl.when(pl.program_id(0) == 0)
+    def _():
+        for p, o_ref in enumerate(o_refs):
+            x_s[:, p * width:(p + 1) * width] = o_ref[0]
+
+    for p, w_ref in enumerate(w_refs):
+        w_s[p * width:(p + 1) * width, :] = w_ref[...]
+    out_ref[...] = jnp.dot(x_s[...], w_s[...], preferred_element_type=F32).astype(out_ref.dtype)
+
+
+def mix_mm(pieces, half, weights, dtype):
+    _, rows, width = pieces[0].shape
+    d_model = weights[0].shape[1]
+    bn = 512
+    o_spec = pl.BlockSpec((1, rows, width), lambda j: (half, 0, 0))
+    w_spec = pl.BlockSpec((width, bn), lambda j: (0, j))
+    return pl.pallas_call(
+        functools.partial(mix_mm_kernel, width),
+        out_shape=jax.ShapeDtypeStruct((rows, d_model), dtype),
+        grid=(d_model // bn,),
+        in_specs=[o_spec] * 4 + [w_spec] * 4,
+        out_specs=pl.BlockSpec((rows, bn), lambda j: (0, j)),
+        scratch_shapes=[pltpu.VMEM((rows, 4 * width), BF16), pltpu.VMEM((4 * width, bn), BF16)],
+        compiler_params=pltpu.CompilerParams(dimension_semantics=("arbitrary",), vmem_limit_bytes=VMEM_LIMIT),
+        cost_estimate=pl.CostEstimate(flops=2 * rows * 4 * width * d_model, bytes_accessed=2 * (4 * width + 2 * rows) * d_model, transcendentals=0),
+        name="mix_mm",
+    )(*pieces, *weights)
+
+
+def swap(value, bit, tp_size):
+    return lax.ppermute(value, 'tp', [(d, d ^ bit) for d in range(tp_size)])
+
+
+def group_rows(blocks, me, pair_bit, mate_bit, tp_size):
+    def rows_of(owner):
+        return jnp.stack([lax.dynamic_index_in_dim(blocks, owner, 0, False), lax.dynamic_index_in_dim(blocks, owner ^ mate_bit, 0, False)])
+    pieces = [rows_of(me)]
+    for bit in (1, pair_bit, pair_bit | 1):
+        pieces.append(swap(row_major(rows_of(me ^ bit)), bit, tp_size))
+    return pieces
+
+
 def solution(mesh):
     tp_size = mesh.shape['tp']
-    dp_size = mesh.shape['dp']
+    x_bit, y_bit = 2, 4
 
     def device_step(x_blk, dy_blk, positions, norm_gain, wq_loc, wk_all, wv_all, wo_loc):
         heads = wq_loc.shape[1] // HEAD_DIM
         width = heads * HEAD_DIM
         rows, d_model = x_blk.shape
-        tp_idx, dp_idx = lax.axis_index('tp'), lax.axis_index('dp')
-        wk_loc = lax.dynamic_slice_in_dim(wk_all, tp_idx * HEAD_DIM, HEAD_DIM, axis=1)
-        wv_loc = lax.dynamic_slice_in_dim(wv_all, tp_idx * HEAD_DIM, HEAD_DIM, axis=1)
-        wqkv = jnp.concatenate([wq_loc, wk_loc, wv_loc], axis=1)
-        wq_t = wq_loc.T
-        share = width // dp_size
-        wq_share = lax.dynamic_slice_in_dim(wq_t, dp_idx * share, share, axis=0)
-        wo_share = lax.dynamic_slice_in_dim(wo_loc, dp_idx * share, share, axis=0)
+        me = lax.axis_index('tp')
+
+        def head_of(weights, owner):
+            return lax.dynamic_slice_in_dim(weights, owner * HEAD_DIM, HEAD_DIM, axis=1)
+
+        wqkv = jnp.concatenate([wq_loc, head_of(wk_all, me), head_of(wv_all, me)], axis=1)
 
         x_f32 = x_blk.astype(F32)
         hidden, x_hat, inv_rms = norm_forward(x_f32, norm_gain)
@@ -246,35 +327,38 @@
         full = (doc_start[BQ - 1::BQ] + BK - 1) // BK
 
         qkv = dot32(h_full, wqkv).astype(BF16)
-        wq_share, qkv = lax.optimization_barrier((wq_share, qkv))
-        wq_full_t = lax.all_gather(row_major(wq_share), ('tp', 'dp'), axis=0, tiled=True)
         o, lse = attend_forward(lo, full, qkv, cos_t, sin_t, doc_start, heads)
-        o_got = row_major(lax.all_to_all(row_major(o.reshape(tp_size, rows, width)), 'tp', 0, 0))
-        dy_full, o_got = lax.optimization_barrier((dy_full, o_got))
-        o_rows = row_major(o_got.transpose(1, 0, 2)).reshape(rows, tp_size * width)
+        dy_full, o, wo_own, wq_own = lax.optimization_barrier((dy_full, o, wo_loc, wq_loc))
+        wq_near = swap(wq_own, y_bit, tp_size)
+        wo_near = swap(wo_own, x_bit, tp_size)
+        o_pieces = group_rows(o.reshape(tp_size, rows, width), me, x_bit, y_bit, tp_size)
 
         d_o = dot32(dy_full, wo_loc, NT).astype(BF16)
-        wo_share, d_o = lax.optimization_barrier((wo_share, d_o))
-        wo_full = lax.all_gather(row_major(wo_share), ('tp', 'dp'), axis=0, tiled=True)
         d_qkv = attend_backward(lo, full, qkv, o, d_o, lse, cos_t, sin_t, doc_start, heads)
-        got = row_major(lax.all_to_all(row_major(d_qkv.reshape(tp_size, rows, width + 2 * HEAD_DIM)), 'tp', 0, 0))
-        got = row_major(got.transpose(1, 0, 2))
-        dq_rows = got[:, :, :width].reshape(rows, tp_size * width)
-        dk_rows = got[:, :, width:width + HEAD_DIM].reshape(rows, tp_size * HEAD_DIM)
-        dv_rows = got[:, :, width + HEAD_DIM:].reshape(rows, tp_size * HEAD_DIM)
+        dq_pieces = group_rows(d_qkv.reshape(tp_size, rows, width + 2 * HEAD_DIM), me, y_bit, x_bit, tp_size)
+        wq_near, wo_near, wq_own, wo_own, d_qkv = lax.optimization_barrier((wq_near, wo_near, wq_own, wo_own, d_qkv))
+        wq_group = [wq_own, swap(wq_own, 1, tp_size), wq_near, swap(wq_near, 1, tp_size)]
+        wo_group = [wo_own, swap(wo_own, 1, tp_size), wo_near, swap(wo_near, 1, tp_size)]
 
         d_wo = dot32(o, dy_full, TN).astype(BF16)
         d_wq = dot32(h_full, d_qkv[:, :width], TN).astype(BF16)
         d_wkv = dot32(h_full, d_qkv[:, width:], TN)
+        dq_pieces, d_wo, d_wq, d_wkv = lax.optimization_barrier((dq_pieces, d_wo, d_wq, d_wkv))
+        owners = jnp.stack([me ^ bit for bit in (0, 1, y_bit, y_bit | 1)])
+        dh_mate = grad_mm(owners, dq_pieces, 1, wq_group, wk_all, wv_all, BF16)
+        dh_got = swap(dh_mate, x_bit, tp_size)
+        o_pieces, dh_mate = lax.optimization_barrier((o_pieces, dh_mate))
+        mix_got = swap(mix_mm(o_pieces, 1, wo_group, BF16), y_bit, tp_size)
+        dh_own = grad_mm(owners, dq_pieces, 0, wq_group, wk_all, wv_all, F32)
+        mix_own = mix_mm(o_pieces, 0, wo_group, F32)
+
         d_wk, d_wv = d_wkv[:, :HEAD_DIM], d_wkv[:, HEAD_DIM:]
-
-        d_hidden = (dot32(dq_rows, wq_full_t) + (dot32(dk_rows, wk_all, NT) + dot32(dv_rows, wv_all, NT))).astype(BF16)
-        d_f32 = d_hidden.astype(F32)
+        d_f32 = (dh_own + dh_got.astype(F32)).astype(BF16).astype(F32)
         d_gain = sum_over_tp(jnp.sum(d_f32 * x_hat, axis=0), tp_size)
         scaled = d_f32 * norm_gain
         d_input = inv_rms * (scaled - x_hat * jnp.mean(scaled * x_hat, axis=-1, keepdims=True))
         grad_x = (dy_blk.astype(F32) + d_input).astype(BF16)
-        result = (x_f32 + dot32(o_rows, wo_full)).astype(BF16)
+        result = (x_f32 + (mix_own + mix_got.astype(F32))).astype(BF16)
         return result, grad_x, d_wq, d_wk, d_wv, d_wo, d_gain
 
     specs_in = (P(('dp', 'tp'), None), P(('dp', 'tp'), None), P('dp'), P(), P(None, 'tp'), P(), P(), P('tp', None))

time: 731 us -> 807 us (1.10)
  matrix products: 199 us -> 123 us
  Pallas kernels: 163 us -> 239 us
  waiting for transfers between devices: 281 us -> 355 us
  other arithmetic: 24.5 us -> 47.1 us
  local copies, waits for them, and re-layouts: 34 us -> 13.5 us
    ppermute x0 -> x14, waiting for transfers between devices: none -> 147 us  [swap(): return lax.ppermute(value, 'tp', [(d, d ^ bit) for d in range(tp_size)])]
    all_to_all x2 -> x0, waiting for transfers between devices: 96 us -> none  [the longest x1 74.9 us: device_step(): lax.all_to_all(row_major(o.reshape(tp_size, rows, width)), 'tp', 0, 0)]
    dot_general x9 -> x5, matrix products: 199 us -> 123 us  [dot32(): return lax.dot_general(a, b, dims, preferred_element_type=F32)]
    pallas_call x0 -> x4, Pallas kernels: none -> 76.1 us  [the longest x2 45 us: grad_mm(): pl.pallas_call(functools.partial(grad_mm_kernel, width), out_shape=jax.Sh...]
    all_gather x1, waiting for transfers between devices: 0.01 us -> 47.2 us  [device_step(): dy_full = lax.all_gather(dy_in, 'tp', axis=0, tiled=True)]
    all_gather x2 -> x0, waiting for transfers between devices: 21.2 us -> none  [the longest x1 21.2 us: device_step(): lax.all_gather(row_major(wo_share), ('tp', 'dp'), axis=0, tiled=True)]
    unnamed x29 -> x20, local copies, waits for them, and re-layouts: 13.1 us -> 1.6 us
    all_to_all x2 -> x0, starting transfers between devices: 10.3 us -> none  [the longest x1 5.75 us: device_step(): lax.all_to_all(row_major(d_qkv.reshape(tp_size, rows, width + 2 * HEAD_DI...]
  transfers between devices with their start and end apart: 9 -> 19, of which waited for: 5 -> 6; matrix products, arithmetic and copies ran while one was open for 31% -> 19% of each run, Pallas kernels for 22% -> 30%
where the time goes in v2:
time: 807 us; the launch traced here: 804 us
  waiting for transfers between devices  355 us (44%)
  Pallas kernels  239 us (30%)
  matrix products  123 us (15%)
  other arithmetic  47.1 us (6%)
  between operations  14.5 us (2%)
  local copies, waits for them, and re-layouts  13.5 us (2%)
  starting transfers between devices  11.9 us (1%)
    all_gather x1, waiting for transfers between devices, device_step(): h_full = lax.all_gather(hidden, 'tp', axis=0, tiled=True)  159 us
    ppermute x14, waiting for transfers between devices, swap(): return lax.ppermute(value, 'tp', [(d, d ^ bit) for d in range(tp_size)])  147 us
    dot_general x5, matrix products, dot32(): return lax.dot_general(a, b, dims, preferred_element_type=F32)  123 us
    pallas_call x1, Pallas kernels, attend_backward(): pl.pallas_call(functools.partial(bwd_kernel, heads, n_blk), out_shape=jax...  99.3 us
    pallas_call x1, Pallas kernels, attend_forward(): pl.pallas_call(functools.partial(fwd_kernel, heads), out_shape=(jax.Shape...  63 us
    all_gather x1, waiting for transfers between devices, device_step(): dy_full = lax.all_gather(dy_in, 'tp', axis=0, tiled=True)  47.2 us
    pallas_call x2, Pallas kernels, grad_mm(): pl.pallas_call(functools.partial(grad_mm_kernel, width), out_shape=jax.Sh...  45 us
    pallas_call x2, Pallas kernels, mix_mm(): pl.pallas_call(functools.partial(mix_mm_kernel, width), out_shape=jax.Sha...  31.1 us
  transfers between devices with their start and end apart: 19, of which 6 were waited for; matrix products, arithmetic and copies ran while one was open for 19% of the time, Pallas kernels for 30%

profile of v2, /device:TPU:0, one launch (start us, length us, event | category | flops | bytes accessed | tf_op | source)
XLA Modules:
  0.0 803.7 jit_solution(1658321210434837099)
XLA Ops:
  7.2 3.2 fusion.11
  10.5 0.6 copy-done.4
  11.1 4.4 fusion.8
  15.4 0.6 all-gather.5.cloned.1.call-start
  16.0 159.3 %all-gather.3.cloned.1.call-done = bf16[4096,4096]{1,0:T(8,128)(2,1)} async-done(((bf16[512,4096]{1,0:T(8,128)(2,1)}), bf16[4096,4096]{1,0:T(8,128)(2,1)}) %all-gather.3.cloned.1.call-update) | async-done | bytes 33554448 | tf_op jit(solution)/shard_map/all_gather | solution.py:319
  175.6 2.0 copy.15.ds_ref
  177.6 0.6 pad_add_fusion.owner_ref
  178.2 0.5 and_select_fusion
  178.8 1.7 constant_dynamic-slice_fusion.16
  180.5 7.5 fusion.21
  188.0 3.4 pad_maximum_fusion
  191.4 32.5 %convolution_convert_fusion.q_ref.k_ref.v_ref = bf16[4096,768]{1,0:T(8,128)(2,1)} fusion(bf16[4096,4096]{1,0:T(8,128)(2,1)} %all-gather.3.cloned.1.call-done, bf16[4096,128]{1,0:T(8,128)(2,1)S(1)} %get-tuple-element.85, bf16[4096,128]{1,0:T(8,128)(2,1)S(1)} %get-tuple-element.86, bf16[4096,512]{1,0:T(8,128)(2,1)} %refs_4_.3), kind=kOutput, calls=%fused_computation.18 | convolution fusion | flops 25791823872 | bytes 46137344 | tf_op jit(solution)/shard_map/dot_general | solution.py:204
  223.9 63.0 %attend_fwd.1 = (bf16[4096,512]{1,0:T(8,128)(2,1)}, f32[16,1,1024]{2,1,0:T(1,128)}) custom-call(s32[16]{0:T(128)} %get-tuple-element.84.lo_ref, s32[16]{0:T(128)} %get-tuple-element.83.full_ref, bf16[4096,768]{1,0:T(8,128)(2,1)} %convolution_convert_fusion.q_ref.k_ref.v_ref, bf16[4096,768]{1,0:T(8,128)(2,1)} %convolution_convert_fusion.q_ref.k_ref.v_ref, ...), custom_call_target="tpu_custom_call" | custom-call | flops 17179869184 | bytes 16777216 | tf_op jit(solution)/shard_map/attend_fwd/pallas_call | solution.py:164
  286.9 47.2 %all-gather.5.cloned.1.call-done = bf16[4096,4096]{1,0:T(8,128)(2,1)} async-done(((bf16[512,4096]{1,0:T(8,128)(2,1)}), bf16[4096,4096]{1,0:T(8,128)(2,1)}) %all-gather.5.cloned.1.call-update) | async-done | bytes 33554448 | tf_op jit(solution)/shard_map/all_gather | solution.py:322
  334.1 24.6 %convolution_convert_fusion.3.do_ref = bf16[4096,512]{1,0:T(8,128)(2,1)} fusion(bf16[4096,4096]{1,0:T(8,128)(2,1)} %all-gather.5.cloned.1.call-done, bf16[512,4096]{1,0:T(8,128)(2,1)} %refs_4_.2), kind=kOutput, calls=%fused_computation.26 | convolution fusion | flops 17181966336 | bytes 41943040 | tf_op jit(solution)/shard_map/dot_general | solution.py:204
  358.7 0.4 collective-permute-start.6
  359.0 1.7 collective-permute-start.7
  360.7 99.3 %attend_bwd.1 = bf16[4096,768]{1,0:T(8,128)(2,1)} custom-call(s32[16]{0:T(128)} %get-tuple-element.84.lo_ref, s32[16]{0:T(128)} %get-tuple-element.83.full_ref, bf16[4096,768]{1,0:T(8,128)(2,1)} %convolution_convert_fusion.q_ref.k_ref.v_ref, bf16[4096,768]{1,0:T(8,128)(2,1)} %convolution_convert_fusion.q_ref.k_ref.v_ref, ...), custom_call_target="tpu_custom_call" | custom-call | flops 42949672960 | bytes 25165824 | tf_op jit(solution)/shard_map/attend_bwd/pallas_call | solution.py:183
  460.0 3.2 constant_dynamic-slice_fusion.1
  463.6 1.5 collective-permute-start.4
  465.1 1.3 pad_maximum_fusion.5
  466.4 0.4 collective-permute-start.5
  466.8 0.3 constant_dynamic-slice_fusion.9
  467.1 1.1 pad_maximum_fusion.7
  468.3 1.3 pad_maximum_fusion.2.refs_0_
  469.6 23.6 %convolution_convert_fusion.2 = bf16[512,4096]{1,0:T(8,128)(2,1)} fusion(bf16[4096,512]{1,0:T(8,128)(2,1)S(1)} %copy-done.1, bf16[4096,4096]{1,0:T(8,128)(2,1)} %all-gather.5.cloned.1.call-done), kind=kOutput, calls=%fused_computation.25 | convolution fusion | flops 17181966336 | bytes 41943040 | tf_op jit(solution)/shard_map/dot_general | solution.py:204
  493.2 0.3 collective-permute-start.8
  493.7 24.4 %convolution_convert_fusion.1 = bf16[4096,512]{1,0:T(8,128)(2,1)} fusion(bf16[4096,4096]{1,0:T(8,128)(2,1)} %all-gather.3.cloned.1.call-done, bf16[4096,768]{1,0:T(8,128)(2,1)S(1)} %bitcast.17), kind=kOutput, calls=%fused_computation.24 | convolution fusion | flops 17181966336 | bytes 41943040 | tf_op jit(solution)/shard_map/dot_general | solution.py:204
  518.7 17.7 %fusion.19 = f32[4096,256]{1,0:T(8,128)} fusion(bf16[4096,4096]{1,0:T(8,128)(2,1)} %all-gather.3.cloned.1.call-done, bf16[4096,768]{1,0:T(8,128)(2,1)S(1)} %bitcast.17), kind=kOutput, calls=%fused_computation.32 | convolution fusion | flops 8589934592 | bytes 39845888 | tf_op jit(solution)/shard_map/dot_general | solution.py:204
  536.6 0.4 collective-permute-start.1
  537.0 22.0 %grad_mm.2 = bf16[512,4096]{1,0:T(8,128)(2,1)} custom-call(s32[4]{0:T(128)} %pad_add_fusion.owner_ref, bf16[2,512,768]{2,1,0:T(8,128)(2,1)} %pad_maximum_fusion.2.refs_0_, bf16[2,512,768]{2,1,0:T(8,128)(2,1)} %collective-permute-done.3.refs_1_, bf16[2,512,768]{2,1,0:T(8,128)(2,1)} %collective-permute-done.4.refs_2_, ...), custom_call_target="tpu_custom_call" | custom-call | flops 12884901888 | bytes 33554432 | tf_op jit(solution)/shard_map/grad_mm/pallas_call | solution.py:243
  559.0 1.7 collective-permute-start.13
  560.9 1.1 pad_maximum_fusion.6.refs_0_
  562.2 111.2 %collective-permute-done.2.refs_3_ = bf16[2,512,512]{2,1,0:T(8,128)(2,1)S(1)} collective-permute-done((bf16[2,512,512]{2,1,0:T(8,128)(2,1)S(1)}, bf16[2,512,512]{2,1,0:T(8,128)(2,1)S(1)}, u32[]{:S(2)}, u32[]{:S(2)}) %collective-permute-start.2) | collective-permute-done | bytes 1048608 | tf_op jit(solution)/shard_map/ppermute | solution.py:290
  673.4 1.0 copy-done.7
  674.4 15.2 %mix_mm.3 = bf16[512,4096]{1,0:T(8,128)(2,1)} custom-call(bf16[2,512,512]{2,1,0:T(8,128)(2,1)} %pad_maximum_fusion.6.refs_0_, bf16[2,512,512]{2,1,0:T(8,128)(2,1)} %collective-permute-done.refs_1_, bf16[2,512,512]{2,1,0:T(8,128)(2,1)} %collective-permute-done.1.refs_2_, bf16[2,512,512]{2,1,0:T(8,128)(2,1)} %copy-done.7, bf16[512,4096]{1,0:T(8,128)(2,1)} %refs_4_.2, ...), custom_call_target="tpu_custom_call" | custom-call | flops 8589934592 | bytes 25165824 | tf_op jit(solution)/shard_map/mix_mm/pallas_call | solution.py:276
  689.6 1.3 collective-permute-start.12
  690.9 4.5 fusion.23
  695.4 23.0 %grad_mm.3 = f32[512,4096]{1,0:T(8,128)} custom-call(s32[4]{0:T(128)} %pad_add_fusion.owner_ref, bf16[2,512,768]{2,1,0:T(8,128)(2,1)} %pad_maximum_fusion.2.refs_0_, bf16[2,512,768]{2,1,0:T(8,128)(2,1)} %collective-permute-done.3.refs_1_, bf16[2,512,768]{2,1,0:T(8,128)(2,1)} %collective-permute-done.4.refs_2_, ...), custom_call_target="tpu_custom_call" | custom-call | flops 12884901888 | bytes 33554432 | tf_op jit(solution)/shard_map/grad_mm/pallas_call | solution.py:243
  718.5 8.8 %fusion.10 = (f32[4096]{0:T(1024)S(1)}, f32[512]{0:T(512)S(1)}, bf16[512,4096]{1,0:T(8,128)(2,1)}) fusion(bf16[512,4096]{1,0:T(8,128)(2,1)} %param.8, f32[512]{0:T(512)S(1)} %copy-done.5, f32[4096]{0:T(1024)S(1)} %copy-done.2, f32[512,4096]{1,0:T(8,128)} %grad_mm.3, bf16[512,4096]{1,0:T(8,128)(2,1)} %collective-permute-done.13), kind=kLoop, calls=%fused_computation.14 | loop fusion | flops 23064064 | bytes 21008384 | tf_op jit(solution)/shard_map/reduce_sum | solution.py:357
  727.3 0.5 collective-permute-start.14
  727.8 15.9 %mix_mm.2 = f32[512,4096]{1,0:T(8,128)} custom-call(bf16[2,512,512]{2,1,0:T(8,128)(2,1)} %pad_maximum_fusion.6.refs_0_, bf16[2,512,512]{2,1,0:T(8,128)(2,1)} %collective-permute-done.refs_1_, bf16[2,512,512]{2,1,0:T(8,128)(2,1)} %collective-permute-done.1.refs_2_, bf16[2,512,512]{2,1,0:T(8,128)(2,1)} %copy-done.7, bf16[512,4096]{1,0:T(8,128)(2,1)} %refs_4_.2, ...), custom_call_target="tpu_custom_call" | custom-call | flops 8589934592 | bytes 25165824 | tf_op jit(solution)/shard_map/mix_mm/pallas_call | solution.py:276
  743.7 1.5 collective-permute-start.15
  745.3 2.2 collective-permute-done.15
  747.5 0.5 collective-permute-start.16
  748.0 35.2 %collective-permute-done.12 = bf16[512,4096]{1,0:T(8,128)(2,1)} collective-permute-done((bf16[512,4096]{1,0:T(8,128)(2,1)}, bf16[512,4096]{1,0:T(8,128)(2,1)}, u32[]{:S(2)}, u32[]{:S(2)}) %collective-permute-start.12) | collective-permute-done | bytes 4194336 | tf_op jit(solution)/shard_map/ppermute | solution.py:290
  783.2 12.8 %fusion.7 = (bf16[512,4096]{1,0:T(8,128)(2,1)}, bf16[512,4096]{1,0:T(8,128)(2,1)}) fusion(bf16[512,4096]{1,0:T(8,128)(2,1)} %get-tuple-element.57, bf16[512,4096]{1,0:T(8,128)(2,1)} %param.8, bf16[512,4096]{1,0:T(8,128)(2,1)} %param.9, f32[512]{0:T(512)S(1)} %broadcast_multiply_fusion, f32[4096]{0:T(1024)S(1)} %copy-done.2, f32[512]{0:T(512)S(1)} %copy-done.5, ...), kind=kLoop, calls=%fused_computation.11 | loop fusion | flops 29360128 | bytes 33574912 | tf_op jit(solution)/shard_map/convert_element_type | solution.py:360
  796.0 0.6 add.105
  (54 shorter events, 2.2 us)
Async XLA Ops:
  7.2 168.1 %all-gather.3.cloned.1.call-start = ((), (), s32[]{:S(2)}) async-start(), calls=%async_computation | async-start | bytes 37748736 | tf_op jit(solution)/shard_map/all_gather | solution.py:319
  7.2 3.9 copy-start
  10.5 0.6 copy-start.4
  15.4 159.9 %copy-start.6 = (s32[4096]{0:T(1024)S(1)}, s32[4096]{0:T(1024)}, u32[]{:S(2)}) copy-start(s32[4096]{0:T(1024)} %param.10) | copy-start | bytes 49156
  15.4 318.7 %all-gather.5.cloned.1.call-start = ((), (), s32[]{:S(2)}) async-start(), calls=%async_computation.1 | async-start | bytes 37748736 | tf_op jit(solution)/shard_map/all_gather | solution.py:322
  175.4 12.6 %copy-start.3 = (s32[4096]{0:T(1024)}, s32[4096]{0:T(1024)S(1)}, u32[]{:S(2)}) copy-start(s32[4096]{0:T(1024)S(1)} %get-tuple-element.82) | copy-start | bytes 49156
  358.7 134.5 %collective-permute-start.6 = (bf16[4096,512]{1,0:T(8,128)(2,1)}, bf16[4096,512]{1,0:T(8,128)(2,1)}, u32[]{:S(2)}, u32[]{:S(2)}) collective-permute-start(bf16[4096,512]{1,0:T(8,128)(2,1)} %refs_4_.3), channel_id=1, source_target_pairs={{0,4},{1,5},{2,6},{3,7},{4,0},{5,1},{6,2},{7,3},{8,12},{9,13},{10,... | collective-permute-start | bytes 12582920 | tf_op jit(solution)/shard_map/ppermute | solution.py:290
  359.0 134.1 %collective-permute-start.7 = (bf16[512,4096]{1,0:T(8,128)(2,1)}, bf16[512,4096]{1,0:T(8,128)(2,1)}, u32[]{:S(2)}, u32[]{:S(2)}) collective-permute-start(bf16[512,4096]{1,0:T(8,128)(2,1)} %refs_4_.2), channel_id=1, source_target_pairs={{0,2},{1,3},{2,0},{3,1},{4,6},{5,7},{6,4},{7,5},{8,10},{9,11},{10,... | collective-permute-start | bytes 12582920 | tf_op jit(solution)/shard_map/ppermute | solution.py:290
  463.2 3.5 copy-start.1
  463.4 54.8 %collective-permute-start.3 = (bf16[2,512,768]{2,1,0:T(8,128)(2,1)S(1)}, bf16[2,512,768]{2,1,0:T(8,128)(2,1)}, u32[]{:S(2)}, u32[]{:S(2)}) collective-permute-start(bf16[2,512,768]{2,1,0:T(8,128)(2,1)S(1)} %pad_maximum_fusion.3), channel_id=1, source_target_pairs={{0,1},{1,0},{2,3},{3,2},{4,5},{5,4},{6,7},{7,6},{8,9},{9,8},{10,11... | collective-permute-start | bytes 4718600 | tf_op jit(solution)/shard_map/ppermute | solution.py:290
  463.6 54.9 %collective-permute-start.4 = (bf16[2,512,768]{2,1,0:T(8,128)(2,1)S(1)}, bf16[2,512,768]{2,1,0:T(8,128)(2,1)}, u32[]{:S(2)}, u32[]{:S(2)}) collective-permute-start(bf16[2,512,768]{2,1,0:T(8,128)(2,1)S(1)} %pad_maximum_fusion.4), channel_id=1, source_target_pairs={{0,4},{1,5},{2,6},{3,7},{4,0},{5,1},{6,2},{7,3},{8,12},{9,13},{10,... | collective-permute-start | bytes 4718600 | tf_op jit(solution)/shard_map/ppermute | solution.py:290
  466.4 70.0 %collective-permute-start.5 = (bf16[2,512,768]{2,1,0:T(8,128)(2,1)}, bf16[2,512,768]{2,1,0:T(8,128)(2,1)}, u32[]{:S(2)}, u32[]{:S(2)}) collective-permute-start(bf16[2,512,768]{2,1,0:T(8,128)(2,1)} %pad_maximum_fusion.5), channel_id=1, source_target_pairs={{0,5},{1,4},{2,7},{3,6},{4,1},{5,0},{6,3},{7,2},{8,13},{9,12},{10,... | collective-permute-start | bytes 4718600 | tf_op jit(solution)/shard_map/ppermute | solution.py:290
  468.3 25.5 %slice-start = ((s8[6291456]{0:T(1024)(128)(4,1)}), s8[4194304]{0:T(1024)(128)(4,1)S(1)}, s32[]{:S(2)}) async-start(s8[6291456]{0:T(1024)(128)(4,1)} %bitcast.16), calls=%async_computation.2 | async-start | bytes 8388608
  469.6 24.1 %slice-start.1 = ((s8[6291456]{0:T(1024)(128)(4,1)}), s8[2097152]{0:T(1024)(128)(4,1)S(1)}, s32[]{:S(2)}) async-start(s8[6291456]{0:T(1024)(128)(4,1)} %bitcast.16), calls=%async_computation.3 | async-start | bytes 4194304
  493.2 43.5 %collective-permute-start.8 = (bf16[4096,512]{1,0:T(8,128)(2,1)}, bf16[4096,512]{1,0:T(8,128)(2,1)}, u32[]{:S(2)}, u32[]{:S(2)}) collective-permute-start(bf16[4096,512]{1,0:T(8,128)(2,1)} %refs_4_.3), channel_id=1, source_target_pairs={{0,1},{1,0},{2,3},{3,2},{4,5},{5,4},{6,7},{7,6},{8,9},{9,8},{10,11... | collective-permute-start | bytes 12582920 | tf_op jit(solution)/shard_map/ppermute | solution.py:290
  493.5 43.5 %collective-permute-start.9 = (bf16[4096,512]{1,0:T(8,128)(2,1)}, bf16[4096,512]{1,0:T(8,128)(2,1)}, u32[]{:S(2)}, u32[]{:S(2)}) collective-permute-start(bf16[4096,512]{1,0:T(8,128)(2,1)} %collective-permute-done.6.refs_6_), channel_id=1, source_target_pairs={{0,1},{1,0},{2,3},{3,2},{4,5},{5,4},{6,7},{7,6},{8,9},{9,8},{10,11... | collective-permute-start | bytes 12582920 | tf_op jit(solution)/shard_map/ppermute | solution.py:290
  518.2 155.3 %collective-permute-start.10 = (bf16[512,4096]{1,0:T(8,128)(2,1)}, bf16[512,4096]{1,0:T(8,128)(2,1)}, u32[]{:S(2)}, u32[]{:S(2)}) collective-permute-start(bf16[512,4096]{1,0:T(8,128)(2,1)} %refs_4_.2), channel_id=1, source_target_pairs={{0,1},{1,0},{2,3},{3,2},{4,5},{5,4},{6,7},{7,6},{8,9},{9,8},{10,11... | collective-permute-start | bytes 12582920 | tf_op jit(solution)/shard_map/ppermute | solution.py:290
  518.5 155.0 %collective-permute-start.11 = (bf16[512,4096]{1,0:T(8,128)(2,1)}, bf16[512,4096]{1,0:T(8,128)(2,1)}, u32[]{:S(2)}, u32[]{:S(2)}) collective-permute-start(bf16[512,4096]{1,0:T(8,128)(2,1)} %collective-permute-done.7.refs_6_), channel_id=1, source_target_pairs={{0,1},{1,0},{2,3},{3,2},{4,5},{5,4},{6,7},{7,6},{8,9},{9,8},{10,11... | collective-permute-start | bytes 12582920 | tf_op jit(solution)/shard_map/ppermute | solution.py:290
  536.3 24.5 %collective-permute-start = (bf16[2,512,512]{2,1,0:T(8,128)(2,1)}, bf16[2,512,512]{2,1,0:T(8,128)(2,1)}, u32[]{:S(2)}, u32[]{:S(2)}) collective-permute-start(bf16[2,512,512]{2,1,0:T(8,128)(2,1)} %pad_maximum_fusion.7), channel_id=1, source_target_pairs={{0,1},{1,0},{2,3},{3,2},{4,5},{5,4},{6,7},{7,6},{8,9},{9,8},{10,11... | collective-permute-start | bytes 3145736 | tf_op jit(solution)/shard_map/ppermute | solution.py:290
  536.6 25.6 %collective-permute-start.1 = (bf16[2,512,512]{2,1,0:T(8,128)(2,1)S(1)}, bf16[2,512,512]{2,1,0:T(8,128)(2,1)}, u32[]{:S(2)}, u32[]{:S(2)}) collective-permute-start(bf16[2,512,512]{2,1,0:T(8,128)(2,1)S(1)} %pad_maximum_fusion.8), channel_id=1, source_target_pairs={{0,2},{1,3},{2,0},{3,1},{4,6},{5,7},{6,4},{7,5},{8,10},{9,11},{10,... | collective-permute-start | bytes 3145736 | tf_op jit(solution)/shard_map/ppermute | solution.py:290
  559.0 159.5 %collective-permute-start.13 = (bf16[512,4096]{1,0:T(8,128)(2,1)}, bf16[512,4096]{1,0:T(8,128)(2,1)}, u32[]{:S(2)}, u32[]{:S(2)}) collective-permute-start(bf16[512,4096]{1,0:T(8,128)(2,1)} %grad_mm.2), channel_id=1, source_target_pairs={{0,2},{1,3},{2,0},{3,1},{4,6},{5,7},{6,4},{7,5},{8,10},{9,11},{10,... | collective-permute-start | bytes 12582920 | tf_op jit(solution)/shard_map/ppermute | solution.py:290
  560.8 112.6 %collective-permute-start.2 = (bf16[2,512,512]{2,1,0:T(8,128)(2,1)S(1)}, bf16[2,512,512]{2,1,0:T(8,128)(2,1)S(1)}, u32[]{:S(2)}, u32[]{:S(2)}) collective-permute-start(bf16[2,512,512]{2,1,0:T(8,128)(2,1)S(1)} %pad_maximum_fusion.9), channel_id=1, source_target_pairs={{0,3},{1,2},{2,1},{3,0},{4,7},{5,6},{6,5},{7,4},{8,11},{9,10},{10,... | collective-permute-start | bytes 3145736 | tf_op jit(solution)/shard_map/ppermute | solution.py:290
  673.4 1.0 copy-start.7
  689.6 93.7 %collective-permute-start.12 = (bf16[512,4096]{1,0:T(8,128)(2,1)}, bf16[512,4096]{1,0:T(8,128)(2,1)}, u32[]{:S(2)}, u32[]{:S(2)}) collective-permute-start(bf16[512,4096]{1,0:T(8,128)(2,1)} %mix_mm.3), channel_id=1, source_target_pairs={{0,4},{1,5},{2,6},{3,7},{4,0},{5,1},{6,2},{7,3},{8,12},{9,13},{10,... | collective-permute-start | bytes 12582920 | tf_op jit(solution)/shard_map/ppermute | solution.py:290
  695.4 23.0 %copy-start.2 = (f32[4096]{0:T(1024)S(1)}, f32[4096]{0:T(1024)}, u32[]{:S(2)}) copy-start(f32[4096]{0:T(1024)} %param.11) | copy-start | bytes 49156
  695.4 23.1 %copy-start.5 = (f32[512]{0:T(512)S(1)}, f32[512]{0:T(512)}, u32[]{:S(2)}) copy-start(f32[512]{0:T(512)} %copy-done.4) | copy-start | bytes 6148
  727.3 16.4 %collective-permute-start.14 = (f32[4096]{0:T(1024)S(1)}, f32[4096]{0:T(1024)S(1)}, u32[]{:S(2)}, u32[]{:S(2)}) collective-permute-start(f32[4096]{0:T(1024)S(1)} %get-tuple-element.55), channel_id=1, source_target_pairs={{0,1},{1,0},{2,3},{3,2},{4,5},{5,4},{6,7},{7,6},{8,9},{9,8},{10,11... | collective-permute-start | bytes 49160 | tf_op jit(solution)/shard_map/ppermute | solution.py:214
  743.7 3.8 collective-permute-start.15
  747.5 48.5 %collective-permute-start.16 = (f32[4096]{0:T(1024)S(1)}, f32[4096]{0:T(1024)S(1)}, u32[]{:S(2)}, u32[]{:S(2)}) collective-permute-start(f32[4096]{0:T(1024)S(1)} %add.104), channel_id=1, source_target_pairs={{0,4},{1,5},{2,6},{3,7},{4,0},{5,1},{6,2},{7,3},{8,12},{9,13},{10,... | collective-permute-start | bytes 49160 | tf_op jit(solution)/shard_map/ppermute | solution.py:214
Sparse Core Ops, SparseCore 0:
  15.6 159.6 all-gather.2
  177.1 156.9 all-gather.4

commit v3 on v2

--- a/solution.py
+++ b/solution.py
@@ -57,7 +57,6 @@
 def fwd_kernel(heads, lo_ref, full_ref, q_ref, k_ref, v_ref, cos_ref, sin_ref, cosf_ref, sinf_ref, ds_ref, o_ref, lse_ref, k_s, m_s, l_s, acc_s):
     i = pl.program_id(0)
     bq, bk = BQ, BK
-    rows = heads * bq
 
     @pl.when(i == 0)
     def _():
@@ -99,7 +98,6 @@
 def bwd_kernel(heads, n_blk, lo_ref, full_ref, q_ref, k_ref, v_ref, o_ref, do_ref, lse_ref, cos_ref, sin_ref, cosf_ref, sinf_ref, ds_ref, out_ref, k_s, dq_s, dk_s, dv_s):
     i = pl.program_id(0)
     bq, bk = BQ, BK
-    rows = heads * bq
     width = heads * HEAD_DIM
 
     @pl.when(i == 0)
@@ -196,8 +194,7 @@
 
 def norm_forward(x_f32, norm_gain):
     inv_rms = lax.rsqrt(jnp.mean(x_f32 * x_f32, axis=-1, keepdims=True) + NORM_EPS)
-    x_hat = x_f32 * inv_rms
-    return (x_hat * norm_gain).astype(BF16), x_hat, inv_rms
+    return (x_f32 * inv_rms * norm_gain).astype(BF16)
 
 
 def dot32(a, b, dims=(((1,), (0,)), ((), ()))):
@@ -286,6 +283,39 @@
     )(*pieces, *weights)
 
 
+def finish_kernel(own_ref, got_ref, x_ref, dy_ref, gain_ref, dx_ref, dg_ref):
+    x = x_ref[...].astype(F32)
+    inv_rms = lax.rsqrt(jnp.mean(x * x, axis=-1, keepdims=True) + NORM_EPS)
+    x_hat = x * inv_rms
+    d_hidden = (own_ref[...] + got_ref[...].astype(F32)).astype(BF16).astype(F32)
+
+    @pl.when(pl.program_id(0) == 0)
+    def _():
+        dg_ref[...] = jnp.zeros_like(dg_ref)
+
+    dg_ref[...] += jnp.sum(d_hidden * x_hat, axis=0, keepdims=True)
+    scaled = d_hidden * gain_ref[...]
+    d_input = inv_rms * (scaled - x_hat * jnp.mean(scaled * x_hat, axis=-1, keepdims=True))
+    dx_ref[...] = (dy_ref[...].astype(F32) + d_input).astype(BF16)
+
+
+def finish(dh_own, dh_got, x_blk, dy_blk, norm_gain):
+    rows, d_model = x_blk.shape
+    blk = pl.BlockSpec((64, d_model), lambda i: (i, 0))
+    one = pl.BlockSpec((1, d_model), lambda i: (0, 0))
+    grad_x, d_gain = pl.pallas_call(
+        finish_kernel,
+        out_shape=(jax.ShapeDtypeStruct((rows, d_model), BF16), jax.ShapeDtypeStruct((1, d_model), F32)),
+        grid=(rows // 64,),
+        in_specs=[blk, blk, blk, blk, one],
+        out_specs=[blk, one],
+        compiler_params=pltpu.CompilerParams(dimension_semantics=("arbitrary",), vmem_limit_bytes=VMEM_LIMIT),
+        cost_estimate=pl.CostEstimate(flops=20 * rows * d_model, bytes_accessed=12 * rows * d_model, transcendentals=0),
+        name="finish",
+    )(dh_own, dh_got, x_blk, dy_blk, norm_gain[None, :])
+    return grad_x, d_gain[0]
+
+
 def swap(value, bit, tp_size):
     return lax.ppermute(value, 'tp', [(d, d ^ bit) for d in range(tp_size)])
 
@@ -293,6 +323,7 @@
 def group_rows(blocks, me, pair_bit, mate_bit, tp_size):
     def rows_of(owner):
         return jnp.stack([lax.dynamic_index_in_dim(blocks, owner, 0, False), lax.dynamic_index_in_dim(blocks, owner ^ mate_bit, 0, False)])
+
     pieces = [rows_of(me)]
     for bit in (1, pair_bit, pair_bit | 1):
         pieces.append(swap(row_major(rows_of(me ^ bit)), bit, tp_size))
@@ -303,10 +334,10 @@
     tp_size = mesh.shape['tp']
     x_bit, y_bit = 2, 4
 
-    def device_step(x_blk, dy_blk, positions, norm_gain, wq_loc, wk_all, wv_all, wo_loc):
+    def layer(x_blk, dy_blk, positions, norm_gain, wq_loc, wk_all, wv_all, wo_loc):
         heads = wq_loc.shape[1] // HEAD_DIM
         width = heads * HEAD_DIM
-        rows, d_model = x_blk.shape
+        rows, _ = x_blk.shape
         me = lax.axis_index('tp')
 
         def head_of(weights, owner):
@@ -315,7 +346,7 @@
         wqkv = jnp.concatenate([wq_loc, head_of(wk_all, me), head_of(wv_all, me)], axis=1)
 
         x_f32 = x_blk.astype(F32)
-        hidden, x_hat, inv_rms = norm_forward(x_f32, norm_gain)
+        hidden = norm_forward(x_f32, norm_gain)
         h_full = lax.all_gather(hidden, 'tp', axis=0, tiled=True)
         seq = h_full.shape[0]
         dy_in, h_full = lax.optimization_barrier((dy_blk, h_full))
@@ -336,31 +367,30 @@
         d_o = dot32(dy_full, wo_loc, NT).astype(BF16)
         d_qkv = attend_backward(lo, full, qkv, o, d_o, lse, cos_t, sin_t, doc_start, heads)
         dq_pieces = group_rows(d_qkv.reshape(tp_size, rows, width + 2 * HEAD_DIM), me, y_bit, x_bit, tp_size)
-        wq_near, wo_near, wq_own, wo_own, d_qkv = lax.optimization_barrier((wq_near, wo_near, wq_own, wo_own, d_qkv))
+        wq_near, wq_own, d_qkv = lax.optimization_barrier((wq_near, wq_own, d_qkv))
         wq_group = [wq_own, swap(wq_own, 1, tp_size), wq_near, swap(wq_near, 1, tp_size)]
-        wo_group = [wo_own, swap(wo_own, 1, tp_size), wo_near, swap(wo_near, 1, tp_size)]
 
         d_wo = dot32(o, dy_full, TN).astype(BF16)
         d_wq = dot32(h_full, d_qkv[:, :width], TN).astype(BF16)
         d_wkv = dot32(h_full, d_qkv[:, width:], TN)
-        dq_pieces, d_wo, d_wq, d_wkv = lax.optimization_barrier((dq_pieces, d_wo, d_wq, d_wkv))
+        wo_near, wo_own, d_wq = lax.optimization_barrier((wo_near, wo_own, d_wq))
+        wo_group = [wo_own, swap(wo_own, 1, tp_size), wo_near, swap(wo_near, 1, tp_size)]
+        mix_mate = mix_mm(o_pieces, 1, wo_group, BF16)
+        dq_pieces, mix_mate, d_wq, d_wkv = lax.optimization_barrier((dq_pieces, mix_mate, d_wq, d_wkv))
+        mix_got = swap(mix_mate, y_bit, tp_size)
         owners = jnp.stack([me ^ bit for bit in (0, 1, y_bit, y_bit | 1)])
         dh_mate = grad_mm(owners, dq_pieces, 1, wq_group, wk_all, wv_all, BF16)
         dh_got = swap(dh_mate, x_bit, tp_size)
-        o_pieces, dh_mate = lax.optimization_barrier((o_pieces, dh_mate))
-        mix_got = swap(mix_mm(o_pieces, 1, wo_group, BF16), y_bit, tp_size)
         dh_own = grad_mm(owners, dq_pieces, 0, wq_group, wk_all, wv_all, F32)
         mix_own = mix_mm(o_pieces, 0, wo_group, F32)
+        dh_own, dh_got, mix_own, d_wo = lax.optimization_barrier((dh_own, dh_got, mix_own, d_wo))
 
         d_wk, d_wv = d_wkv[:, :HEAD_DIM], d_wkv[:, HEAD_DIM:]
-        d_f32 = (dh_own + dh_got.astype(F32)).astype(BF16).astype(F32)
-        d_gain = sum_over_tp(jnp.sum(d_f32 * x_hat, axis=0), tp_size)
-        scaled = d_f32 * norm_gain
-        d_input = inv_rms * (scaled - x_hat * jnp.mean(scaled * x_hat, axis=-1, keepdims=True))
-        grad_x = (dy_blk.astype(F32) + d_input).astype(BF16)
+        grad_x, dg_part = finish(dh_own, dh_got, x_blk, dy_blk, norm_gain)
+        d_gain = sum_over_tp(dg_part, tp_size)
         result = (x_f32 + (mix_own + mix_got.astype(F32))).astype(BF16)
         return result, grad_x, d_wq, d_wk, d_wv, d_wo, d_gain
 
     specs_in = (P(('dp', 'tp'), None), P(('dp', 'tp'), None), P('dp'), P(), P(None, 'tp'), P(), P(), P('tp', None))
     specs_out = (P(('dp', 'tp'), None), P(('dp', 'tp'), None), P('dp', 'tp'), P('dp', 'tp'), P('dp', 'tp'), P(('dp', 'tp'), None), P('dp'))
-    return jax.shard_map(device_step, mesh=mesh, in_specs=specs_in, out_specs=specs_out, check_vma=False)
+    return jax.shard_map(layer, mesh=mesh, in_specs=specs_in, out_specs=specs_out, check_vma=False)

time: 807 us -> 767 us (0.950)
  waiting for transfers between devices: 355 us -> 309 us
  Pallas kernels: 239 us -> 252 us
  other arithmetic: 47.1 us -> 38.2 us
    ppermute x14, waiting for transfers between devices: 147 us -> 99.7 us  [swap(): return lax.ppermute(value, 'tp', [(d, d ^ bit) for d in range(tp_size)])]
    pallas_call x0 -> x1, Pallas kernels: none -> 14 us  [finish(): pl.pallas_call(finish_kernel, out_shape=(jax.ShapeDtypeStruct((rows, d_mo...]
    reduce_sum x1 -> x0, other arithmetic: 8.79 us -> none  [device_step(): d_gain = sum_over_tp(jnp.sum(d_f32 * x_hat, axis=0), tp_size)]
  transfers between devices with their start and end apart: 19 -> 19, of which waited for: 6 -> 9; matrix products, arithmetic and copies ran while one was open for 19% -> 22% of each run, Pallas kernels for 30% -> 30%
where the time goes in v3:
time: 767 us; the launch traced here: 764 us
  waiting for transfers between devices  309 us (40%)
  Pallas kernels  252 us (33%)
  matrix products  123 us (16%)
  other arithmetic  38.2 us (5%)
  local copies, waits for them, and re-layouts  15.3 us (2%)
  between operations  14.4 us (2%)
  starting transfers between devices  11.4 us (1%)
    all_gather x1, waiting for transfers between devices, layer(): h_full = lax.all_gather(hidden, 'tp', axis=0, tiled=True)  159 us
    dot_general x5, matrix products, dot32(): return lax.dot_general(a, b, dims, preferred_element_type=F32)  123 us
    ppermute x14, waiting for transfers between devices, swap(): return lax.ppermute(value, 'tp', [(d, d ^ bit) for d in range(tp_size)])  99.7 us
    pallas_call x1, Pallas kernels, attend_backward(): pl.pallas_call(functools.partial(bwd_kernel, heads, n_blk), out_shape=jax...  99.4 us
    pallas_call x1, Pallas kernels, attend_forward(): pl.pallas_call(functools.partial(fwd_kernel, heads), out_shape=(jax.Shape...  63 us
    all_gather x1, waiting for transfers between devices, layer(): dy_full = lax.all_gather(dy_in, 'tp', axis=0, tiled=True)  48.5 us
    pallas_call x2, Pallas kernels, grad_mm(): pl.pallas_call(functools.partial(grad_mm_kernel, width), out_shape=jax.Sh...  44.9 us
    pallas_call x2, Pallas kernels, mix_mm(): pl.pallas_call(functools.partial(mix_mm_kernel, width), out_shape=jax.Sha...  31 us
  transfers between devices with their start and end apart: 19, of which 9 were waited for; matrix products, arithmetic and copies ran while one was open for 22% of the time, Pallas kernels for 30%

profile of v3, /device:TPU:0, one launch (start us, length us, event | category | flops | bytes accessed | tf_op | source)
XLA Modules:
  0.0 763.7 jit_solution(9756007432703887370)
XLA Ops:
  7.2 3.2 fusion
  10.7 4.4 fusion.2
  15.6 159.3 %all-gather.3.cloned.1.call-done = bf16[4096,4096]{1,0:T(8,128)(2,1)} async-done(((bf16[512,4096]{1,0:T(8,128)(2,1)}), bf16[4096,4096]{1,0:T(8,128)(2,1)}) %all-gather.3.cloned.1.call-update) | async-done | bytes 33554448 | tf_op jit(solution)/shard_map/all_gather | solution.py:350
  175.2 2.0 copy.15.ds_ref
  177.2 0.6 and_select_fusion
  177.7 1.7 constant_dynamic-slice_fusion.16
  179.4 7.5 fusion.12
  187.0 3.4 pad_maximum_fusion
  190.6 31.6 %convolution_convert_fusion.q_ref.k_ref.v_ref = bf16[4096,768]{1,0:T(8,128)(2,1)} fusion(bf16[4096,4096]{1,0:T(8,128)(2,1)} %all-gather.3.cloned.1.call-done, bf16[4096,128]{1,0:T(8,128)(2,1)S(1)} %get-tuple-element.86, bf16[4096,128]{1,0:T(8,128)(2,1)S(1)} %get-tuple-element.87, bf16[4096,512]{1,0:T(8,128)(2,1)S(1)} %copy-done.2), kind=kOutput, calls=%fused_computation.7 | convolution fusion | flops 25791823872 | bytes 46137344 | tf_op jit(solution)/shard_map/dot_general | solution.py:201
  222.2 63.0 %attend_fwd.1 = (bf16[4096,512]{1,0:T(8,128)(2,1)}, f32[16,1,1024]{2,1,0:T(1,128)}) custom-call(s32[16]{0:T(128)} %get-tuple-element.85.lo_ref, s32[16]{0:T(128)} %get-tuple-element.84.full_ref, bf16[4096,768]{1,0:T(8,128)(2,1)} %convolution_convert_fusion.q_ref.k_ref.v_ref, bf16[4096,768]{1,0:T(8,128)(2,1)} %convolution_convert_fusion.q_ref.k_ref.v_ref, ...), custom_call_target="tpu_custom_call" | custom-call | flops 17179869184 | bytes 16777216 | tf_op jit(solution)/shard_map/attend_fwd/pallas_call | solution.py:162
  285.2 48.5 %all-gather.5.cloned.1.call-done = bf16[4096,4096]{1,0:T(8,128)(2,1)} async-done(((bf16[512,4096]{1,0:T(8,128)(2,1)}), bf16[4096,4096]{1,0:T(8,128)(2,1)}) %all-gather.5.cloned.1.call-update) | async-done | bytes 33554448 | tf_op jit(solution)/shard_map/all_gather | solution.py:353
  334.1 24.6 %convolution_convert_fusion.3.do_ref = bf16[4096,512]{1,0:T(8,128)(2,1)} fusion(bf16[4096,4096]{1,0:T(8,128)(2,1)} %all-gather.5.cloned.1.call-done, bf16[512,4096]{1,0:T(8,128)(2,1)} %refs_4_.3), kind=kOutput, calls=%fused_computation.15 | convolution fusion | flops 17181966336 | bytes 41943040 | tf_op jit(solution)/shard_map/dot_general | solution.py:201
  358.6 1.7 collective-permute-start.6
  360.3 99.4 %attend_bwd.1 = bf16[4096,768]{1,0:T(8,128)(2,1)} custom-call(s32[16]{0:T(128)} %get-tuple-element.85.lo_ref, s32[16]{0:T(128)} %get-tuple-element.84.full_ref, bf16[4096,768]{1,0:T(8,128)(2,1)} %convolution_convert_fusion.q_ref.k_ref.v_ref, bf16[4096,768]{1,0:T(8,128)(2,1)} %convolution_convert_fusion.q_ref.k_ref.v_ref, ...), custom_call_target="tpu_custom_call" | custom-call | flops 42949672960 | bytes 25165824 | tf_op jit(solution)/shard_map/attend_bwd/pallas_call | solution.py:181
  459.7 25.5 %convolution_convert_fusion.2 = bf16[4096,512]{1,0:T(8,128)(2,1)} fusion(bf16[4096,4096]{1,0:T(8,128)(2,1)} %all-gather.3.cloned.1.call-done, bf16[4096,768]{1,0:T(8,128)(2,1)} %attend_bwd.1), kind=kOutput, calls=%fused_computation.14 | convolution fusion | flops 17181966336 | bytes 41943040 | tf_op jit(solution)/shard_map/dot_general | solution.py:201
  485.7 2.5 constant_dynamic-slice_fusion.1
  488.3 1.1 pad_maximum_fusion.7
  489.4 1.1 pad_maximum_fusion.8
  490.9 1.5 collective-permute-start.5
  492.4 7.8 %collective-permute-done.3.refs_1_ = bf16[2,512,512]{2,1,0:T(8,128)(2,1)} collective-permute-done((bf16[2,512,512]{2,1,0:T(8,128)(2,1)}, bf16[2,512,512]{2,1,0:T(8,128)(2,1)}, u32[]{:S(2)}, u32[]{:S(2)}) %collective-permute-start.3) | collective-permute-done | bytes 1048608 | tf_op jit(solution)/shard_map/ppermute | solution.py:320
  500.3 16.4 %collective-permute-done.4.refs_2_ = bf16[2,512,512]{2,1,0:T(8,128)(2,1)} collective-permute-done((bf16[2,512,512]{2,1,0:T(8,128)(2,1)}, bf16[2,512,512]{2,1,0:T(8,128)(2,1)}, u32[]{:S(2)}, u32[]{:S(2)}) %collective-permute-start.4) | collective-permute-done | bytes 1048608 | tf_op jit(solution)/shard_map/ppermute | solution.py:320
  516.8 0.7 pad_add_fusion.owner_ref
  517.5 1.1 pad_maximum_fusion.6.refs_0_
  518.5 3.2 constant_dynamic-slice_fusion.9
  521.7 1.3 pad_maximum_fusion.5
  523.1 1.3 pad_maximum_fusion.4
  524.3 1.3 pad_maximum_fusion.3
  525.6 1.3 pad_maximum_fusion.2.refs_0_
  526.9 11.2 %collective-permute-done.5.refs_3_ = bf16[2,512,512]{2,1,0:T(8,128)(2,1)S(1)} collective-permute-done((bf16[2,512,512]{2,1,0:T(8,128)(2,1)S(1)}, bf16[2,512,512]{2,1,0:T(8,128)(2,1)S(1)}, u32[]{:S(2)}, u32[]{:S(2)}) %collective-permute-start.5) | collective-permute-done | bytes 1048608 | tf_op jit(solution)/shard_map/ppermute | solution.py:320
  538.5 0.6 copy-done.7
  539.1 1.5 collective-permute-start.1
  540.8 17.7 %fusion.10 = f32[4096,256]{1,0:T(8,128)} fusion(bf16[4096,4096]{1,0:T(8,128)(2,1)} %all-gather.3.cloned.1.call-done, bf16[4096,768]{1,0:T(8,128)(2,1)} %attend_bwd.1), kind=kOutput, calls=%fused_computation.21 | convolution fusion | flops 8589934592 | bytes 39845888 | tf_op jit(solution)/shard_map/dot_general | solution.py:201
  558.4 15.0 %mix_mm.2 = bf16[512,4096]{1,0:T(8,128)(2,1)} custom-call(bf16[2,512,512]{2,1,0:T(8,128)(2,1)} %pad_maximum_fusion.6.refs_0_, bf16[2,512,512]{2,1,0:T(8,128)(2,1)} %collective-permute-done.3.refs_1_, bf16[2,512,512]{2,1,0:T(8,128)(2,1)} %collective-permute-done.4.refs_2_, bf16[2,512,512]{2,1,0:T(8,128)(2,1)} %copy-done.7, bf16[512,4096]{1,0:T(8,128)(2,1)} %refs_4_.3, ...), custom_call_target="tpu_custom_call" | custom-call | flops 8589934592 | bytes 25165824 | tf_op jit(solution)/shard_map/mix_mm/pallas_call | solution.py:273
  573.5 3.1 collective-permute-done.1.refs_2_
  576.6 32.5 %collective-permute-done.2.refs_3_ = bf16[2,512,768]{2,1,0:T(8,128)(2,1)} collective-permute-done((bf16[2,512,768]{2,1,0:T(8,128)(2,1)}, bf16[2,512,768]{2,1,0:T(8,128)(2,1)}, u32[]{:S(2)}, u32[]{:S(2)}) %collective-permute-start.2) | collective-permute-done | bytes 1572896 | tf_op jit(solution)/shard_map/ppermute | solution.py:320
  609.1 22.1 %grad_mm.3 = bf16[512,4096]{1,0:T(8,128)(2,1)} custom-call(s32[4]{0:T(128)} %pad_add_fusion.owner_ref, bf16[2,512,768]{2,1,0:T(8,128)(2,1)} %pad_maximum_fusion.2.refs_0_, bf16[2,512,768]{2,1,0:T(8,128)(2,1)} %copy-done.3, bf16[2,512,768]{2,1,0:T(8,128)(2,1)} %copy-done.4, bf16[2,512,768]{2,1,0:T(8,128)(2,1)} %collective-permute-done.2.refs_3_, ...), custom_call_target="tpu_custom_call" | custom-call | flops 12884901888 | bytes 33554432 | tf_op jit(solution)/shard_map/grad_mm/pallas_call | solution.py:240
  631.5 1.7 collective-permute-start.13
  633.2 23.8 %convolution_convert_fusion.1 = bf16[512,4096]{1,0:T(8,128)(2,1)} fusion(bf16[4096,512]{1,0:T(8,128)(2,1)} %get-tuple-element.37.o_ref, bf16[4096,4096]{1,0:T(8,128)(2,1)} %all-gather.5.cloned.1.call-done), kind=kOutput, calls=%fused_computation.13 | convolution fusion | flops 17181966336 | bytes 41943040 | tf_op jit(solution)/shard_map/dot_general | solution.py:201
  657.0 16.0 %mix_mm.3 = f32[512,4096]{1,0:T(8,128)} custom-call(bf16[2,512,512]{2,1,0:T(8,128)(2,1)} %pad_maximum_fusion.6.refs_0_, bf16[2,512,512]{2,1,0:T(8,128)(2,1)} %collective-permute-done.3.refs_1_, bf16[2,512,512]{2,1,0:T(8,128)(2,1)} %collective-permute-done.4.refs_2_, bf16[2,512,512]{2,1,0:T(8,128)(2,1)} %copy-done.7, bf16[512,4096]{1,0:T(8,128)(2,1)} %refs_4_.3, ...), custom_call_target="tpu_custom_call" | custom-call | flops 8589934592 | bytes 25165824 | tf_op jit(solution)/shard_map/mix_mm/pallas_call | solution.py:273
  672.9 22.9 %grad_mm.2.own_ref = f32[512,4096]{1,0:T(8,128)} custom-call(s32[4]{0:T(128)} %pad_add_fusion.owner_ref, bf16[2,512,768]{2,1,0:T(8,128)(2,1)} %pad_maximum_fusion.2.refs_0_, bf16[2,512,768]{2,1,0:T(8,128)(2,1)} %copy-done.3, bf16[2,512,768]{2,1,0:T(8,128)(2,1)} %copy-done.4, bf16[2,512,768]{2,1,0:T(8,128)(2,1)} %collective-permute-done.2.refs_3_, ...), custom_call_target="tpu_custom_call" | custom-call | flops 12884901888 | bytes 33554432 | tf_op jit(solution)/shard_map/grad_mm/pallas_call | solution.py:240
  695.8 28.6 %collective-permute-done.12.got_ref = bf16[512,4096]{1,0:T(8,128)(2,1)} collective-permute-done((bf16[512,4096]{1,0:T(8,128)(2,1)}, bf16[512,4096]{1,0:T(8,128)(2,1)}, u32[]{:S(2)}, u32[]{:S(2)}) %collective-permute-start.12) | collective-permute-done | bytes 4194336 | tf_op jit(solution)/shard_map/ppermute | solution.py:320
  724.4 14.0 %finish.1 = (bf16[512,4096]{1,0:T(8,128)(2,1)}, f32[1,4096]{1,0:T(1,128)}) custom-call(f32[512,4096]{1,0:T(8,128)} %grad_mm.2.own_ref, bf16[512,4096]{1,0:T(8,128)(2,1)} %collective-permute-done.12.got_ref, bf16[512,4096]{1,0:T(8,128)(2,1)} %x_ref.1, bf16[512,4096]{1,0:T(8,128)(2,1)} %dy_ref.1, f32[1,4096]{1,0:T(1,128)} %bitcast.21), custom_call_target="tpu_custom_call" | custom-call | flops 41943040 | bytes 25165824 | tf_op jit(solution)/shard_map/finish/pallas_call | solution.py:306
  738.4 1.4 collective-permute-done.14
  739.8 0.7 add.95
  740.9 4.7 fusion.14
  745.6 1.8 collective-permute-start.16
  747.4 8.7 %fusion.3 = bf16[512,4096]{1,0:T(8,128)(2,1)} fusion(bf16[512,4096]{1,0:T(8,128)(2,1)S(1)} %copy-done.1, f32[512,4096]{1,0:T(8,128)} %mix_mm.3, bf16[512,4096]{1,0:T(8,128)(2,1)} %collective-permute-done.13), kind=kLoop, calls=%fused_computation.6 | loop fusion | flops 10485760 | bytes 20971520 | tf_op jit(solution)/shard_map/convert_element_type | solution.py:391
  756.1 0.6 add.97
  (48 shorter events, 4.2 us)
Async XLA Ops:
  7.2 167.7 %all-gather.3.cloned.1.call-start = ((), (), s32[]{:S(2)}) async-start(), calls=%async_computation | async-start | bytes 37748736 | tf_op jit(solution)/shard_map/all_gather | solution.py:350
  7.2 3.5 copy-start
  15.0 159.9 %copy-start.6 = (s32[4096]{0:T(1024)S(1)}, s32[4096]{0:T(1024)}, u32[]{:S(2)}) copy-start(s32[4096]{0:T(1024)} %param.10) | copy-start | bytes 49156
  15.0 318.7 %all-gather.5.cloned.1.call-start = ((), (), s32[]{:S(2)}) async-start(), calls=%async_computation.1 | async-start | bytes 37748736 | tf_op jit(solution)/shard_map/all_gather | solution.py:353
  175.0 12.0 %copy-start.5 = (s32[4096]{0:T(1024)}, s32[4096]{0:T(1024)S(1)}, u32[]{:S(2)}) copy-start(s32[4096]{0:T(1024)S(1)} %get-tuple-element.83) | copy-start | bytes 49156
  186.9 3.6 copy-start.2
  333.7 126.0 %collective-permute-start.7 = (bf16[4096,512]{1,0:T(8,128)(2,1)}, bf16[4096,512]{1,0:T(8,128)(2,1)}, u32[]{:S(2)}, u32[]{:S(2)}) collective-permute-start(bf16[4096,512]{1,0:T(8,128)(2,1)} %refs_4_.2), channel_id=1, source_target_pairs={{0,4},{1,5},{2,6},{3,7},{4,0},{5,1},{6,2},{7,3},{8,12},{9,13},{10,... | collective-permute-start | bytes 12582920 | tf_op jit(solution)/shard_map/ppermute | solution.py:320
  358.6 126.5 %collective-permute-start.6 = (bf16[512,4096]{1,0:T(8,128)(2,1)}, bf16[512,4096]{1,0:T(8,128)(2,1)}, u32[]{:S(2)}, u32[]{:S(2)}) collective-permute-start(bf16[512,4096]{1,0:T(8,128)(2,1)} %refs_4_.3), channel_id=1, source_target_pairs={{0,2},{1,3},{2,0},{3,1},{4,6},{5,7},{6,4},{7,5},{8,10},{9,11},{10,... | collective-permute-start | bytes 12582920 | tf_op jit(solution)/shard_map/ppermute | solution.py:320
  485.2 53.9 %collective-permute-start.8 = (bf16[512,4096]{1,0:T(8,128)(2,1)}, bf16[512,4096]{1,0:T(8,128)(2,1)}, u32[]{:S(2)}, u32[]{:S(2)}) collective-permute-start(bf16[512,4096]{1,0:T(8,128)(2,1)} %refs_4_.3), channel_id=1, source_target_pairs={{0,1},{1,0},{2,3},{3,2},{4,5},{5,4},{6,7},{7,6},{8,9},{9,8},{10,11... | collective-permute-start | bytes 12582920 | tf_op jit(solution)/shard_map/ppermute | solution.py:320
  485.2 55.3 %collective-permute-start.9 = (bf16[512,4096]{1,0:T(8,128)(2,1)}, bf16[512,4096]{1,0:T(8,128)(2,1)}, u32[]{:S(2)}, u32[]{:S(2)}) collective-permute-start(bf16[512,4096]{1,0:T(8,128)(2,1)} %collective-permute-done.6.refs_6_), channel_id=1, source_target_pairs={{0,1},{1,0},{2,3},{3,2},{4,5},{5,4},{6,7},{7,6},{8,9},{9,8},{10,11... | collective-permute-start | bytes 12582920 | tf_op jit(solution)/shard_map/ppermute | solution.py:320
  489.3 10.9 %collective-permute-start.3 = (bf16[2,512,512]{2,1,0:T(8,128)(2,1)}, bf16[2,512,512]{2,1,0:T(8,128)(2,1)}, u32[]{:S(2)}, u32[]{:S(2)}) collective-permute-start(bf16[2,512,512]{2,1,0:T(8,128)(2,1)} %pad_maximum_fusion.7), channel_id=1, source_target_pairs={{0,1},{1,0},{2,3},{3,2},{4,5},{5,4},{6,7},{7,6},{8,9},{9,8},{10,11... | collective-permute-start | bytes 3145736 | tf_op jit(solution)/shard_map/ppermute | solution.py:320
  490.4 26.3 %collective-permute-start.4 = (bf16[2,512,512]{2,1,0:T(8,128)(2,1)}, bf16[2,512,512]{2,1,0:T(8,128)(2,1)}, u32[]{:S(2)}, u32[]{:S(2)}) collective-permute-start(bf16[2,512,512]{2,1,0:T(8,128)(2,1)} %pad_maximum_fusion.8), channel_id=1, source_target_pairs={{0,2},{1,3},{2,0},{3,1},{4,6},{5,7},{6,4},{7,5},{8,10},{9,11},{10,... | collective-permute-start | bytes 3145736 | tf_op jit(solution)/shard_map/ppermute | solution.py:320
  490.9 47.2 %collective-permute-start.5 = (bf16[2,512,512]{2,1,0:T(8,128)(2,1)S(1)}, bf16[2,512,512]{2,1,0:T(8,128)(2,1)S(1)}, u32[]{:S(2)}, u32[]{:S(2)}) collective-permute-start(bf16[2,512,512]{2,1,0:T(8,128)(2,1)S(1)} %pad_maximum_fusion.9), channel_id=1, source_target_pairs={{0,3},{1,2},{2,1},{3,0},{4,7},{5,6},{6,5},{7,4},{8,11},{9,10},{10,... | collective-permute-start | bytes 3145736 | tf_op jit(solution)/shard_map/ppermute | solution.py:320
  500.2 108.9 %collective-permute-start.10 = (bf16[4096,512]{1,0:T(8,128)(2,1)}, bf16[4096,512]{1,0:T(8,128)(2,1)}, u32[]{:S(2)}, u32[]{:S(2)}) collective-permute-start(bf16[4096,512]{1,0:T(8,128)(2,1)} %refs_4_.2), channel_id=1, source_target_pairs={{0,1},{1,0},{2,3},{3,2},{4,5},{5,4},{6,7},{7,6},{8,9},{9,8},{10,11... | collective-permute-start | bytes 12582920 | tf_op jit(solution)/shard_map/ppermute | solution.py:320
  516.8 92.3 %collective-permute-start.11 = (bf16[4096,512]{1,0:T(8,128)(2,1)}, bf16[4096,512]{1,0:T(8,128)(2,1)}, u32[]{:S(2)}, u32[]{:S(2)}) collective-permute-start(bf16[4096,512]{1,0:T(8,128)(2,1)} %collective-permute-done.7.refs_6_), channel_id=1, source_target_pairs={{0,1},{1,0},{2,3},{3,2},{4,5},{5,4},{6,7},{7,6},{8,9},{9,8},{10,11... | collective-permute-start | bytes 12582920 | tf_op jit(solution)/shard_map/ppermute | solution.py:320
  538.1 0.9 copy-start.7
  538.1 35.3 %collective-permute-start = (bf16[2,512,768]{2,1,0:T(8,128)(2,1)}, bf16[2,512,768]{2,1,0:T(8,128)(2,1)S(1)}, u32[]{:S(2)}, u32[]{:S(2)}) collective-permute-start(bf16[2,512,768]{2,1,0:T(8,128)(2,1)} %pad_maximum_fusion.3), channel_id=1, source_target_pairs={{0,1},{1,0},{2,3},{3,2},{4,5},{5,4},{6,7},{7,6},{8,9},{9,8},{10,11... | collective-permute-start | bytes 4718600 | tf_op jit(solution)/shard_map/ppermute | solution.py:320
  539.1 37.5 %collective-permute-start.1 = (bf16[2,512,768]{2,1,0:T(8,128)(2,1)}, bf16[2,512,768]{2,1,0:T(8,128)(2,1)S(1)}, u32[]{:S(2)}, u32[]{:S(2)}) collective-permute-start(bf16[2,512,768]{2,1,0:T(8,128)(2,1)} %pad_maximum_fusion.4), channel_id=1, source_target_pairs={{0,4},{1,5},{2,6},{3,7},{4,0},{5,1},{6,2},{7,3},{8,12},{9,13},{10,... | collective-permute-start | bytes 4718600 | tf_op jit(solution)/shard_map/ppermute | solution.py:320
  540.5 68.5 %collective-permute-start.2 = (bf16[2,512,768]{2,1,0:T(8,128)(2,1)}, bf16[2,512,768]{2,1,0:T(8,128)(2,1)}, u32[]{:S(2)}, u32[]{:S(2)}) collective-permute-start(bf16[2,512,768]{2,1,0:T(8,128)(2,1)} %pad_maximum_fusion.5), channel_id=1, source_target_pairs={{0,5},{1,4},{2,7},{3,6},{4,1},{5,0},{6,3},{7,2},{8,13},{9,12},{10,... | collective-permute-start | bytes 4718600 | tf_op jit(solution)/shard_map/ppermute | solution.py:320
  573.5 35.6 %copy-start.3 = (bf16[2,512,768]{2,1,0:T(8,128)(2,1)}, bf16[2,512,768]{2,1,0:T(8,128)(2,1)S(1)}, u32[]{:S(2)}) copy-start(bf16[2,512,768]{2,1,0:T(8,128)(2,1)S(1)} %collective-permute-done.refs_1_) | copy-start | bytes 4718596
  576.6 32.6 %copy-start.4 = (bf16[2,512,768]{2,1,0:T(8,128)(2,1)}, bf16[2,512,768]{2,1,0:T(8,128)(2,1)S(1)}, u32[]{:S(2)}) copy-start(bf16[2,512,768]{2,1,0:T(8,128)(2,1)S(1)} %collective-permute-done.1.refs_2_) | copy-start | bytes 4718596
  631.2 93.2 %collective-permute-start.12 = (bf16[512,4096]{1,0:T(8,128)(2,1)}, bf16[512,4096]{1,0:T(8,128)(2,1)}, u32[]{:S(2)}, u32[]{:S(2)}) collective-permute-start(bf16[512,4096]{1,0:T(8,128)(2,1)} %grad_mm.3), channel_id=1, source_target_pairs={{0,2},{1,3},{2,0},{3,1},{4,6},{5,7},{6,4},{7,5},{8,10},{9,11},{10,... | collective-permute-start | bytes 12582920 | tf_op jit(solution)/shard_map/ppermute | solution.py:320
  631.5 115.8 %collective-permute-start.13 = (bf16[512,4096]{1,0:T(8,128)(2,1)}, bf16[512,4096]{1,0:T(8,128)(2,1)}, u32[]{:S(2)}, u32[]{:S(2)}) collective-permute-start(bf16[512,4096]{1,0:T(8,128)(2,1)} %mix_mm.2), channel_id=1, source_target_pairs={{0,4},{1,5},{2,6},{3,7},{4,0},{5,1},{6,2},{7,3},{8,12},{9,13},{10,... | collective-permute-start | bytes 12582920 | tf_op jit(solution)/shard_map/ppermute | solution.py:320
  738.4 1.4 collective-permute-start.14
  740.5 6.9 copy-start.1
  740.5 5.1 collective-permute-start.15
  745.6 10.5 %collective-permute-start.16 = (f32[4096]{0:T(1024)S(1)}, f32[4096]{0:T(1024)S(1)}, u32[]{:S(2)}, u32[]{:S(2)}) collective-permute-start(f32[4096]{0:T(1024)S(1)} %add.96), channel_id=1, source_target_pairs={{0,4},{1,5},{2,6},{3,7},{4,0},{5,1},{6,2},{7,3},{8,12},{9,13},{10,... | collective-permute-start | bytes 49160 | tf_op jit(solution)/shard_map/ppermute | solution.py:211
Sparse Core Ops, SparseCore 0:
  15.2 159.6 all-gather.2
  176.7 156.9 all-gather.4

commit v4 on v3

--- a/solution.py
+++ b/solution.py
@@ -4,7 +4,6 @@
 from jax import lax
 from jax.experimental import pallas as pl
 from jax.experimental.pallas import tpu as pltpu
-from jax.experimental.layout import Layout, with_layout_constraint
 from jax.sharding import PartitionSpec as P
 
 HEAD_DIM = 128
@@ -95,16 +94,25 @@
     lse_ref[0] = lse.T[0:1, :]
 
 
-def bwd_kernel(heads, n_blk, lo_ref, full_ref, q_ref, k_ref, v_ref, o_ref, do_ref, lse_ref, cos_ref, sin_ref, cosf_ref, sinf_ref, ds_ref, out_ref, k_s, dq_s, dk_s, dv_s):
-    i = pl.program_id(0)
+def bwd_kernel(heads, half, parts, n_blk, lo_ref, full_ref, q_ref, k_ref, v_ref, o_ref, do_ref, lse_ref, cos_ref, sin_ref, cosf_ref, sinf_ref, ds_ref, *refs):
+    first, last = half == 0, half == parts - 1
+    if not first:
+        refs = refs[1:]
+        dk_in, dv_in = refs[:2]
+        refs = refs[2:]
+    if last:
+        dq_ref, dkv_ref, k_s, dq_s, dk_s, dv_s = refs
+    else:
+        dq_ref, dk_s, dv_s, k_s, dq_s = refs
+    step = pl.program_id(0)
+    i = step * parts + half
     bq, bk = BQ, BK
-    width = heads * HEAD_DIM
-
-    @pl.when(i == 0)
+
+    @pl.when(step == 0)
     def _():
         k_s[...] = rope(k_ref[...], cosf_ref[...], sinf_ref[...])
-        dk_s[...] = jnp.zeros_like(dk_s)
-        dv_s[...] = jnp.zeros_like(dv_s)
+        dk_s[...] = jnp.zeros_like(dk_s) if first else dk_in[...]
+        dv_s[...] = jnp.zeros_like(dv_s) if first else dv_in[...]
 
     cos_t, sin_t = cos_ref[...], sin_ref[...]
     q4 = jnp.concatenate([rope(q_ref[:, h * HEAD_DIM:(h + 1) * HEAD_DIM], cos_t, sin_t) for h in range(heads)], axis=0)
@@ -132,16 +140,16 @@
         dq_s[...] += lax.dot_general(d_s, kj, TN, preferred_element_type=F32)
 
     key_loops(i, lo_ref, full_ref, bq, bk, body)
-    row0 = pl.multiple_of(i * bq, bq)
     for h in range(heads):
         dq = (dq_s[h * bq:(h + 1) * bq, :] * SCORE_SCALE).astype(BF16)
-        out_ref[pl.ds(row0, bq), h * HEAD_DIM:(h + 1) * HEAD_DIM] = rope_back(dq, cos_t, sin_t)
-
-    @pl.when(i == n_blk - 1)
-    def _():
-        dk = (dk_s[...] * SCORE_SCALE).astype(BF16)
-        out_ref[:, width:width + HEAD_DIM] = rope_back(dk, cosf_ref[...], sinf_ref[...])
-        out_ref[:, width + HEAD_DIM:width + 2 * HEAD_DIM] = dv_s[...].astype(BF16)
+        dq_ref[:, h * HEAD_DIM:(h + 1) * HEAD_DIM] = rope_back(dq, cos_t, sin_t)
+
+    if last:
+        @pl.when(step == n_blk - 1)
+        def _():
+            dk = (dk_s[...] * SCORE_SCALE).astype(BF16)
+            dkv_ref[:, :HEAD_DIM] = rope_back(dk, cosf_ref[...], sinf_ref[...])
+            dkv_ref[:, HEAD_DIM:] = dv_s[...].astype(BF16)
 
 
 def attention_specs(seq, heads):
@@ -173,23 +181,41 @@
     )(lo, full, qkv, qkv, qkv, cos_t, sin_t, cos_t, sin_t, doc_start[:, None])
 
 
-def attend_backward(lo, full, qkv, o, d_o, lse, cos_t, sin_t, doc_start, heads):
+def attend_backward(half, parts, carry, lo, full, qkv, o, d_o, lse, cos_t, sin_t, doc_start, heads):
     seq = qkv.shape[0]
-    n_blk = seq // BQ
+    n_blk = seq // BQ // parts
     width = heads * HEAD_DIM
-    q_spec, k_spec, v_spec, tab_spec, tabf_spec, row_spec = attention_specs(seq, heads)
+    _, k_spec, v_spec, _, full_spec, _ = attention_specs(seq, heads)
+    q_spec = pl.BlockSpec((BQ, width), lambda i, *_: (i * parts + half, 0))
+    do_spec = pl.BlockSpec((BQ, width), lambda i, *_: (i, 0))
+    tab_spec = pl.BlockSpec((BQ, HEAD_DIM), lambda i, *_: (i * parts + half, 0))
+    row_spec = pl.BlockSpec((1, 1, heads * BQ), lambda i, *_: (i * parts + half, 0, 0))
+    ds_spec = pl.BlockSpec((1, 1, BQ), lambda i, *_: (i * parts + half, 0, 0))
+    in_specs = [q_spec, k_spec, v_spec, q_spec, do_spec, row_spec, tab_spec, tab_spec, full_spec, full_spec, ds_spec]
+    operands = [lo, full, qkv, qkv, qkv, o, d_o, lse, cos_t, sin_t, cos_t, sin_t, doc_start.reshape(seq // BQ, 1, BQ)]
+    aliases = {}
+    if half:
+        aliases = {len(operands): 0}
+        in_specs += [pl.BlockSpec(memory_space=pl.ANY), full_spec, full_spec]
+        operands += list(carry)
+    dq_shape = jax.ShapeDtypeStruct((seq, width), BF16)
+    sum_shape = jax.ShapeDtypeStruct((seq, HEAD_DIM), F32)
+    scratch = [pltpu.VMEM((seq, HEAD_DIM), BF16), pltpu.VMEM((heads * BQ, HEAD_DIM), F32)]
+    if half == parts - 1:
+        out_shape = (dq_shape, jax.ShapeDtypeStruct((seq, 2 * HEAD_DIM), BF16))
+        out_specs = [q_spec, pl.BlockSpec((seq, 2 * HEAD_DIM), lambda i, *_: (0, 0))]
+        scratch += [pltpu.VMEM((seq, HEAD_DIM), F32)] * 2
+    else:
+        out_shape = (dq_shape, sum_shape, sum_shape)
+        out_specs = [q_spec, full_spec, full_spec]
     return pl.pallas_call(
-        functools.partial(bwd_kernel, heads, n_blk),
-        out_shape=jax.ShapeDtypeStruct((seq, width + 2 * HEAD_DIM), BF16),
-        grid_spec=pltpu.PrefetchScalarGridSpec(
-            num_scalar_prefetch=2, grid=(n_blk,),
-            in_specs=[q_spec, k_spec, v_spec, q_spec, q_spec, row_spec, tab_spec, tab_spec, tabf_spec, tabf_spec, pl.BlockSpec((1, 1, BQ), lambda i, *_: (i, 0, 0))],
-            out_specs=pl.BlockSpec((seq, width + 2 * HEAD_DIM), lambda i, *_: (0, 0)),
-            scratch_shapes=[pltpu.VMEM((seq, HEAD_DIM), BF16), pltpu.VMEM((heads * BQ, HEAD_DIM), F32), pltpu.VMEM((seq, HEAD_DIM), F32), pltpu.VMEM((seq, HEAD_DIM), F32)]),
-        compiler_params=pltpu.CompilerParams(dimension_semantics=("arbitrary",), vmem_limit_bytes=VMEM_LIMIT),
-        cost_estimate=pl.CostEstimate(flops=10 * heads * seq * seq // 2 * HEAD_DIM, bytes_accessed=24 * 2 ** 20, transcendentals=heads * seq * seq // 2),
-        name="attend_bwd",
-    )(lo, full, qkv, qkv, qkv, o, d_o, lse, cos_t, sin_t, cos_t, sin_t, doc_start.reshape(n_blk, 1, BQ))
+        functools.partial(bwd_kernel, heads, half, parts, n_blk),
+        out_shape=out_shape,
+        grid_spec=pltpu.PrefetchScalarGridSpec(num_scalar_prefetch=2, grid=(n_blk,), in_specs=in_specs, out_specs=out_specs, scratch_shapes=scratch),
+        input_output_aliases=aliases,
+        compiler_params=pltpu.CompilerParams(dimension_semantics=("arbitrary",), vmem_limit_bytes=VMEM_LIMIT),
+        cost_estimate=pl.CostEstimate(flops=10 * heads * seq * seq // 2 * HEAD_DIM // parts, bytes_accessed=24 * 2 ** 20 // parts, transcendentals=heads * seq * seq // 2 // parts),
+    )(*operands)
 
 
 def norm_forward(x_f32, norm_gain):
@@ -199,10 +225,6 @@
 
 def dot32(a, b, dims=(((1,), (0,)), ((), ()))):
     return lax.dot_general(a, b, dims, preferred_element_type=F32)
-
-
-def row_major(x):
-    return with_layout_constraint(x, Layout(major_to_minor=tuple(range(x.ndim))))
 
 
 def sum_over_tp(value, tp_size):
@@ -230,11 +252,12 @@
     out_ref[...] = lax.dot_general(x_s[...], w_s[...], NT, preferred_element_type=F32).astype(out_ref.dtype)
 
 
-def grad_mm(owners, pieces, half, weights, wk_all, wv_all, dtype):
+def grad_mm(owners, pieces, half, weights, wk_all, wv_all, dtype, part=0, parts=1):
     _, rows, span = pieces[0].shape
+    rows = rows // parts
     d_model, width = weights[0].shape
     bn = 512
-    g_spec = pl.BlockSpec((1, rows, span), lambda j, *_: (half, 0, 0))
+    g_spec = pl.BlockSpec((1, rows, span), lambda j, *_: (half, part, 0))
     w_spec = pl.BlockSpec((bn, width), lambda j, *_: (j, 0))
     kv_spec = pl.BlockSpec((bn, wk_all.shape[1]), lambda j, *_: (j, 0))
     return pl.pallas_call(
@@ -283,7 +306,8 @@
     )(*pieces, *weights)
 
 
-def finish_kernel(own_ref, got_ref, x_ref, dy_ref, gain_ref, dx_ref, dg_ref):
+def finish_kernel(part, own_ref, got_ref, x_ref, dy_ref, gain_ref, *refs):
+    dx_ref, dg_ref = refs[-2:]
     x = x_ref[...].astype(F32)
     inv_rms = lax.rsqrt(jnp.mean(x * x, axis=-1, keepdims=True) + NORM_EPS)
     x_hat = x * inv_rms
@@ -291,7 +315,7 @@
 
     @pl.when(pl.program_id(0) == 0)
     def _():
-        dg_ref[...] = jnp.zeros_like(dg_ref)
+        dg_ref[...] = refs[1][...] if part else jnp.zeros_like(dg_ref)
 
     dg_ref[...] += jnp.sum(d_hidden * x_hat, axis=0, keepdims=True)
     scaled = d_hidden * gain_ref[...]
@@ -299,34 +323,63 @@
     dx_ref[...] = (dy_ref[...].astype(F32) + d_input).astype(BF16)
 
 
-def finish(dh_own, dh_got, x_blk, dy_blk, norm_gain):
+def finish(part, parts, carry, dh_own, dh_got, x_blk, dy_blk, norm_gain):
     rows, d_model = x_blk.shape
-    blk = pl.BlockSpec((64, d_model), lambda i: (i, 0))
+    blk_rows = 64
+    steps = rows // parts // blk_rows
+    blk = pl.BlockSpec((blk_rows, d_model), lambda i: (i + part * steps, 0))
+    got = pl.BlockSpec((blk_rows, d_model), lambda i: (i, 0))
     one = pl.BlockSpec((1, d_model), lambda i: (0, 0))
-    grad_x, d_gain = pl.pallas_call(
-        finish_kernel,
+    operands = [dh_own, dh_got, x_blk, dy_blk, norm_gain[None, :]]
+    in_specs = [blk, got, blk, blk, one]
+    aliases = {}
+    if part:
+        aliases = {5: 0}
+        operands += list(carry)
+        in_specs += [pl.BlockSpec(memory_space=pl.ANY), one]
+    return pl.pallas_call(
+        functools.partial(finish_kernel, part),
         out_shape=(jax.ShapeDtypeStruct((rows, d_model), BF16), jax.ShapeDtypeStruct((1, d_model), F32)),
-        grid=(rows // 64,),
-        in_specs=[blk, blk, blk, blk, one],
+        grid=(steps,),
+        in_specs=in_specs,
         out_specs=[blk, one],
-        compiler_params=pltpu.CompilerParams(dimension_semantics=("arbitrary",), vmem_limit_bytes=VMEM_LIMIT),
-        cost_estimate=pl.CostEstimate(flops=20 * rows * d_model, bytes_accessed=12 * rows * d_model, transcendentals=0),
-        name="finish",
-    )(dh_own, dh_got, x_blk, dy_blk, norm_gain[None, :])
-    return grad_x, d_gain[0]
+        input_output_aliases=aliases,
+        compiler_params=pltpu.CompilerParams(dimension_semantics=("arbitrary",), vmem_limit_bytes=VMEM_LIMIT),
+        cost_estimate=pl.CostEstimate(flops=20 * rows * d_model // parts, bytes_accessed=12 * rows * d_model // parts, transcendentals=0),
+    )(*operands)
 
 
 def swap(value, bit, tp_size):
     return lax.ppermute(value, 'tp', [(d, d ^ bit) for d in range(tp_size)])
 
 
+def pack_kernel(n_in, owner_ref, *refs):
+    ins, outs = refs[:4 * n_in], refs[4 * n_in:]
+    for p, out_ref in enumerate(outs):
+        at = 0
+        for ref in ins[p * n_in:(p + 1) * n_in]:
+            out_ref[0, :, at:at + ref.shape[2]] = ref[0]
+            at += ref.shape[2]
+
+
 def group_rows(blocks, me, pair_bit, mate_bit, tp_size):
-    def rows_of(owner):
-        return jnp.stack([lax.dynamic_index_in_dim(blocks, owner, 0, False), lax.dynamic_index_in_dim(blocks, owner ^ mate_bit, 0, False)])
-
-    pieces = [rows_of(me)]
-    for bit in (1, pair_bit, pair_bit | 1):
-        pieces.append(swap(row_major(rows_of(me ^ bit)), bit, tp_size))
+    bits = (0, 1, pair_bit, pair_bit | 1)
+    owners = jnp.stack([me ^ bit ^ mate for bit in bits for mate in (0, mate_bit)])
+    rows = blocks[0].shape[1]
+    span = sum(b.shape[2] for b in blocks)
+    in_specs = [pl.BlockSpec((1, rows, b.shape[2]), functools.partial(lambda p, h, owner: (owner[2 * p + h], 0, 0), p)) for p in range(4) for b in blocks]
+    sent = pl.pallas_call(
+        functools.partial(pack_kernel, len(blocks)),
+        out_shape=[jax.ShapeDtypeStruct((2, rows, span), BF16)] * 4,
+        grid_spec=pltpu.PrefetchScalarGridSpec(num_scalar_prefetch=1, grid=(2,), in_specs=in_specs,
+                                               out_specs=[pl.BlockSpec((1, rows, span), lambda h, owner: (h, 0, 0))] * 4),
+        compiler_params=pltpu.CompilerParams(dimension_semantics=("arbitrary",), vmem_limit_bytes=VMEM_LIMIT),
+        cost_estimate=pl.CostEstimate(flops=0, bytes_accessed=32 * rows * span, transcendentals=0),
+        name="pack_rows",
+    )(owners, *(list(blocks) * 4))
+    pieces = [sent[0]]
+    for bit, rows_sent in zip(bits[1:], sent[1:]):
+        pieces.append(swap(rows_sent, bit, tp_size))
     return pieces
 
 
@@ -349,8 +402,10 @@
         hidden = norm_forward(x_f32, norm_gain)
         h_full = lax.all_gather(hidden, 'tp', axis=0, tiled=True)
         seq = h_full.shape[0]
-        dy_in, h_full = lax.optimization_barrier((dy_blk, h_full))
-        dy_full = lax.all_gather(dy_in, 'tp', axis=0, tiled=True)
+        parts = rows // BQ
+        dy_late, _ = lax.optimization_barrier((dy_blk, hidden))
+        dy_in = [dy_late[p * BQ:(p + 1) * BQ] for p in range(parts)]
+        dy_full = [lax.all_gather(dy_in[0], 'tp', axis=0, tiled=True)]
 
         cos_t, sin_t = rope_tables(positions)
         doc_start = lax.iota(jnp.int32, seq) - positions
@@ -358,37 +413,51 @@
         full = (doc_start[BQ - 1::BQ] + BK - 1) // BK
 
         qkv = dot32(h_full, wqkv).astype(BF16)
+        *dy_rest, qkv = lax.optimization_barrier((*dy_in[1:], qkv))
+        dy_full += [lax.all_gather(dy_part, 'tp', axis=0, tiled=True) for dy_part in dy_rest]
         o, lse = attend_forward(lo, full, qkv, cos_t, sin_t, doc_start, heads)
-        dy_full, o, wo_own, wq_own = lax.optimization_barrier((dy_full, o, wo_loc, wq_loc))
+        dy_full[0], o = lax.optimization_barrier((dy_full[0], o))
+        o_blocks = o.reshape(tp_size, parts, BQ, width)
+        carry = None
+        for p in range(parts - 1):
+            d_o = dot32(dy_full[p], wo_loc, NT).astype(BF16)
+            carry = attend_backward(p, parts, carry, lo, full, qkv, o, d_o, lse, cos_t, sin_t, doc_start, heads)
+        dy_full[-1], o_sent, wo_own, wq_own = lax.optimization_barrier((dy_full[-1], o, wo_loc, wq_loc))
         wq_near = swap(wq_own, y_bit, tp_size)
         wo_near = swap(wo_own, x_bit, tp_size)
-        o_pieces = group_rows(o.reshape(tp_size, rows, width), me, x_bit, y_bit, tp_size)
-
-        d_o = dot32(dy_full, wo_loc, NT).astype(BF16)
-        d_qkv = attend_backward(lo, full, qkv, o, d_o, lse, cos_t, sin_t, doc_start, heads)
-        dq_pieces = group_rows(d_qkv.reshape(tp_size, rows, width + 2 * HEAD_DIM), me, y_bit, x_bit, tp_size)
-        wq_near, wq_own, d_qkv = lax.optimization_barrier((wq_near, wq_own, d_qkv))
-        wq_group = [wq_own, swap(wq_own, 1, tp_size), wq_near, swap(wq_near, 1, tp_size)]
-
-        d_wo = dot32(o, dy_full, TN).astype(BF16)
-        d_wq = dot32(h_full, d_qkv[:, :width], TN).astype(BF16)
-        d_wkv = dot32(h_full, d_qkv[:, width:], TN)
-        wo_near, wo_own, d_wq = lax.optimization_barrier((wo_near, wo_own, d_wq))
+        o_pieces = group_rows([o_sent.reshape(tp_size, rows, width)], me, x_bit, y_bit, tp_size)
+
+        d_o = dot32(dy_full[-1], wo_loc, NT).astype(BF16)
+        d_q, d_kv = attend_backward(parts - 1, parts, carry, lo, full, qkv, o, d_o, lse, cos_t, sin_t, doc_start, heads)
+        dq_pieces = group_rows([d_q.reshape(tp_size, rows, width), d_kv.reshape(tp_size, rows, 2 * HEAD_DIM)], me, y_bit, x_bit, tp_size)
+        d_wq = dot32(h_full, d_q, TN).astype(BF16)
+        d_wkv = dot32(h_full, d_kv, TN)
+        wq_near, wq_own, d_wq, d_wkv = lax.optimization_barrier((wq_near, wq_own, d_wq, d_wkv))
+        wq_side = swap(wq_own, 1, tp_size)
+        wq_group = [wq_own, wq_side, wq_near, swap(wq_near, 1, tp_size)]
+        o_blocks, d_wkv = lax.optimization_barrier((o_blocks, d_wkv))
+        d_wo = dot32(o_blocks[:, 0].reshape(-1, width), dy_full[0], TN)
+        d_wo = (d_wo + sum(dot32(o_blocks[:, p].reshape(-1, width), dy_full[p], TN) for p in range(1, parts))).astype(BF16)
+        wo_near, wo_own, d_wo = lax.optimization_barrier((wo_near, wo_own, d_wo))
         wo_group = [wo_own, swap(wo_own, 1, tp_size), wo_near, swap(wo_near, 1, tp_size)]
         mix_mate = mix_mm(o_pieces, 1, wo_group, BF16)
         dq_pieces, mix_mate, d_wq, d_wkv = lax.optimization_barrier((dq_pieces, mix_mate, d_wq, d_wkv))
         mix_got = swap(mix_mate, y_bit, tp_size)
         owners = jnp.stack([me ^ bit for bit in (0, 1, y_bit, y_bit | 1)])
-        dh_mate = grad_mm(owners, dq_pieces, 1, wq_group, wk_all, wv_all, BF16)
-        dh_got = swap(dh_mate, x_bit, tp_size)
+        halves = 2
+        dh_got = []
+        for p in range(halves):
+            dh_mate = grad_mm(owners, dq_pieces, 1, wq_group, wk_all, wv_all, BF16, p, halves)
+            dh_got.append(swap(dh_mate, x_bit, tp_size))
         dh_own = grad_mm(owners, dq_pieces, 0, wq_group, wk_all, wv_all, F32)
         mix_own = mix_mm(o_pieces, 0, wo_group, F32)
-        dh_own, dh_got, mix_own, d_wo = lax.optimization_barrier((dh_own, dh_got, mix_own, d_wo))
-
+        result = (x_f32 + (mix_own + mix_got.astype(F32))).astype(BF16)
         d_wk, d_wv = d_wkv[:, :HEAD_DIM], d_wkv[:, HEAD_DIM:]
-        grad_x, dg_part = finish(dh_own, dh_got, x_blk, dy_blk, norm_gain)
-        d_gain = sum_over_tp(dg_part, tp_size)
-        result = (x_f32 + (mix_own + mix_got.astype(F32))).astype(BF16)
+        dh_own, dh_got[0], result, d_wo, d_wk, d_wv = lax.optimization_barrier((dh_own, dh_got[0], result, d_wo, d_wk, d_wv))
+        done = None
+        for p in range(halves):
+            done = finish(p, halves, done, dh_own, dh_got[p], x_blk, dy_blk, norm_gain)
+        grad_x, d_gain = done[0], sum_over_tp(done[1][0], tp_size)
         return result, grad_x, d_wq, d_wk, d_wv, d_wo, d_gain
 
     specs_in = (P(('dp', 'tp'), None), P(('dp', 'tp'), None), P('dp'), P(), P(None, 'tp'), P(), P(), P('tp', None))

time: 767 us -> 772 us (level)
  Pallas kernels: 252 us -> 286 us
  waiting for transfers between devices: 309 us -> 278 us
  matrix products: 123 us -> 131 us
    all_gather x1 -> x2, waiting for transfers between devices: 48.5 us -> 0.03 us  [the longest x1 0.01 us: layer(): dy_full = [lax.all_gather(dy_in[0], 'tp', axis=0, tiled=True)]]
    pallas_call x2 -> x6, Pallas kernels: 113 us -> 134 us  [the longest x2 108 us: attend_backward(): pl.pallas_call(functools.partial(bwd_kernel, heads, half, parts, n_blk),...]
    ppermute x14 -> x15, waiting for transfers between devices: 99.7 us -> 117 us  [swap(): return lax.ppermute(value, 'tp', [(d, d ^ bit) for d in range(tp_size)])]
    pallas_call x2 -> x3, Pallas kernels: 44.9 us -> 57.8 us  [grad_mm(): pl.pallas_call(functools.partial(grad_mm_kernel, width), out_shape=jax.Sh...]
    another operation x8 -> x0, other arithmetic: 8.44 us -> none  [rows_of(): jnp.stack([lax.dynamic_index_in_dim(blocks, owner, 0, False), lax.dynamic...]
    dot_general x5 -> x7, matrix products: 123 us -> 131 us  [dot32(): return lax.dot_general(a, b, dims, preferred_element_type=F32)]
  transfers between devices with their start and end apart: 19 -> 21, of which waited for: 9 -> 11; matrix products, arithmetic and copies ran while one was open for 22% -> 20% of each run, Pallas kernels for 30% -> 36%
where the time goes in v4:
time: 772 us; the launch traced here: 768 us
  Pallas kernels  286 us (37%)
  waiting for transfers between devices  278 us (36%)
  matrix products  131 us (17%)
  other arithmetic  30.8 us (4%)
  local copies, waits for them, and re-layouts  17.3 us (2%)
  between operations  14.3 us (2%)
  starting transfers between devices  10.9 us (1%)
    all_gather x1, waiting for transfers between devices, layer(): h_full = lax.all_gather(hidden, 'tp', axis=0, tiled=True)  153 us
    dot_general x7, matrix products, dot32(): return lax.dot_general(a, b, dims, preferred_element_type=F32)  131 us
    ppermute x15, waiting for transfers between devices, swap(): return lax.ppermute(value, 'tp', [(d, d ^ bit) for d in range(tp_size)])  117 us
    pallas_call x2, Pallas kernels, attend_backward(): pl.pallas_call(functools.partial(bwd_kernel, heads, half, parts, n_blk),...  108 us
    pallas_call x1, Pallas kernels, attend_forward(): pl.pallas_call(functools.partial(fwd_kernel, heads), out_shape=(jax.Shape...  63.2 us
    pallas_call x3, Pallas kernels, grad_mm(): pl.pallas_call(functools.partial(grad_mm_kernel, width), out_shape=jax.Sh...  57.8 us
    pallas_call x2, Pallas kernels, mix_mm(): pl.pallas_call(functools.partial(mix_mm_kernel, width), out_shape=jax.Sha...  31 us
    pallas_call x2, Pallas kernels, finish(): pl.pallas_call(functools.partial(finish_kernel, part), out_shape=(jax.Sha...  15.6 us
  transfers between devices with their start and end apart: 21, of which 11 were waited for; matrix products, arithmetic and copies ran while one was open for 20% of the time, Pallas kernels for 36%

profile of v4, /device:TPU:0, one launch (start us, length us, event | category | flops | bytes accessed | tf_op | source)
XLA Modules:
  0.0 768.0 jit_solution(17591672414823014421)
XLA Ops:
  7.2 3.2 fusion
  10.7 4.4 fusion.2
  15.1 4.8 fusion.13
  20.1 1.7 constant_dynamic-slice_fusion
  21.8 153.1 %all-gather.4.cloned.1.call-done = bf16[4096,4096]{1,0:T(8,128)(2,1)} async-done(((bf16[512,4096]{1,0:T(8,128)(2,1)}), bf16[4096,4096]{1,0:T(8,128)(2,1)}) %all-gather.4.cloned.1.call-update) | async-done | bytes 33554448 | tf_op jit(solution)/shard_map/all_gather | solution.py:403
  174.9 32.3 %convolution_convert_fusion.q_ref.k_ref.v_ref = bf16[4096,768]{1,0:T(8,128)(2,1)} fusion(bf16[4096,4096]{1,0:T(8,128)(2,1)} %all-gather.4.cloned.1.call-done, bf16[4096,128]{1,0:T(8,128)(2,1)S(1)} %get-tuple-element.120, bf16[4096,128]{1,0:T(8,128)(2,1)S(1)} %get-tuple-element.121, bf16[4096,512]{1,0:T(8,128)(2,1)} %refs_4_.4), kind=kOutput, calls=%fused_computation.8 | convolution fusion | flops 25791823872 | bytes 46137344 | tf_op jit(solution)/shard_map/dot_general | solution.py:227
  207.5 2.0 copy.17.ds_ref
  210.1 7.5 fusion.9
  217.6 3.2 pad_maximum_fusion
  220.7 63.2 %attend_fwd.1 = (bf16[4096,512]{1,0:T(8,128)(2,1)}, f32[16,1,1024]{2,1,0:T(1,128)}) custom-call(s32[16]{0:T(128)} %get-tuple-element.119.lo_ref, s32[16]{0:T(128)} %get-tuple-element.118.full_ref, bf16[4096,768]{1,0:T(8,128)(2,1)} %convolution_convert_fusion.q_ref.k_ref.v_ref, bf16[4096,768]{1,0:T(8,128)(2,1)} %convolution_convert_fusion.q_ref.k_ref.v_ref, ...), custom_call_target="tpu_custom_call" | custom-call | flops 17179869184 | bytes 16777216 | tf_op jit(solution)/shard_map/attend_fwd/pallas_call | solution.py:170
  284.0 14.6 %convolution_convert_fusion.2.do_ref = bf16[2048,512]{1,0:T(8,128)(2,1)} fusion(bf16[2048,4096]{1,0:T(8,128)(2,1)} %all-gather.6.cloned.1.call-done, bf16[512,4096]{1,0:T(8,128)(2,1)} %refs_4_.3), kind=kOutput, calls=%fused_computation.17 | convolution fusion | flops 8590983168 | bytes 23068672 | tf_op jit(solution)/shard_map/dot_general | solution.py:227
  298.6 55.9 %shard_map.135 = (bf16[4096,512]{1,0:T(8,128)(2,1)}, f32[4096,128]{1,0:T(8,128)}, f32[4096,128]{1,0:T(8,128)}) custom-call(s32[16]{0:T(128)} %get-tuple-element.119.lo_ref, s32[16]{0:T(128)} %get-tuple-element.118.full_ref, bf16[4096,768]{1,0:T(8,128)(2,1)} %convolution_convert_fusion.q_ref.k_ref.v_ref, ...), custom_call_target="tpu_custom_call" | custom-call | flops 21474836480 | bytes 12582912 | tf_op jit(solution)/shard_map/pallas_call | solution.py:211
  354.5 14.6 %convolution_convert_fusion.3.do_ref = bf16[2048,512]{1,0:T(8,128)(2,1)} fusion(bf16[2048,4096]{1,0:T(8,128)(2,1)} %all-gather.8.cloned.1.call-done, bf16[512,4096]{1,0:T(8,128)(2,1)} %refs_4_.3), kind=kOutput, calls=%fused_computation.18 | convolution fusion | flops 8590983168 | bytes 23068672 | tf_op jit(solution)/shard_map/dot_general | solution.py:227
  369.1 1.0 collective-permute-start.6
  370.1 52.2 %shard_map.136 = (bf16[4096,512]{1,0:T(8,128)(2,1)}, bf16[4096,256]{1,0:T(8,128)(2,1)}) custom-call(s32[16]{0:T(128)} %get-tuple-element.119.lo_ref, s32[16]{0:T(128)} %get-tuple-element.118.full_ref, bf16[4096,768]{1,0:T(8,128)(2,1)} %convolution_convert_fusion.q_ref.k_ref.v_ref, ...), custom_call_target="tpu_custom_call", output_to_operand_aliasing={{0}: (13, {})} | custom-call | flops 21474836480 | bytes 12582912 | tf_op jit(solution)/shard_map/pallas_call | solution.py:211
  422.3 25.2 %convolution_convert_fusion.1 = bf16[4096,512]{1,0:T(8,128)(2,1)} fusion(bf16[4096,4096]{1,0:T(8,128)(2,1)} %all-gather.4.cloned.1.call-done, bf16[4096,512]{1,0:T(8,128)(2,1)} %get-tuple-element.68), kind=kOutput, calls=%fused_computation.14 | convolution fusion | flops 17181966336 | bytes 41943040 | tf_op jit(solution)/shard_map/dot_general | solution.py:227
  447.5 18.0 %fusion.15 = f32[4096,256]{1,0:T(8,128)} fusion(bf16[4096,4096]{1,0:T(8,128)(2,1)} %all-gather.4.cloned.1.call-done, bf16[4096,256]{1,0:T(8,128)(2,1)S(1)} %copy-done.2), kind=kOutput, calls=%fused_computation.41 | convolution fusion | flops 8589934592 | bytes 39845888 | tf_op jit(solution)/shard_map/dot_general | solution.py:227
  465.9 12.0 %fusion.16 = f32[512,4096]{1,0:T(8,128)S(1)} fusion(bf16[2048,512]{1,0:T(8,128)(2,1)S(1)} %bitcast.49, bf16[2048,4096]{1,0:T(8,128)(2,1)} %all-gather.6.cloned.1.call-done), kind=kOutput, calls=%fused_computation.42 | convolution fusion | flops 8589934592 | bytes 27262976 | tf_op jit(solution)/shard_map/dot_general | solution.py:227
  477.9 14.4 %add_convert_fusion = bf16[512,4096]{1,0:T(8,128)(2,1)} fusion(f32[512,4096]{1,0:T(8,128)S(1)} %fusion.16, bf16[2048,512]{1,0:T(8,128)(2,1)S(1)} %bitcast.48, bf16[2048,4096]{1,0:T(8,128)(2,1)} %all-gather.8.cloned.1.call-done), kind=kOutput, calls=%fused_computation.7 | convolution fusion | flops 8594128896 | bytes 31457280 | tf_op jit(solution)/shard_map/dot_general | solution.py:227
  493.5 4.4 pack_rows.3
  498.4 8.9 %collective-permute-done.3.refs_1_ = bf16[2,512,512]{2,1,0:T(8,128)(2,1)} collective-permute-done((bf16[2,512,512]{2,1,0:T(8,128)(2,1)}, bf16[2,512,512]{2,1,0:T(8,128)(2,1)}, u32[]{:S(2)}, u32[]{:S(2)}) %collective-permute-start.3) | collective-permute-done | bytes 1048608 | tf_op jit(solution)/shard_map/ppermute | solution.py:353
  507.3 1.0 collective-permute-start.4
  508.4 24.5 %collective-permute-done.4.refs_2_ = bf16[2,512,512]{2,1,0:T(8,128)(2,1)} collective-permute-done((bf16[2,512,512]{2,1,0:T(8,128)(2,1)}, bf16[2,512,512]{2,1,0:T(8,128)(2,1)}, u32[]{:S(2)}, u32[]{:S(2)}) %collective-permute-start.4) | collective-permute-done | bytes 1048608 | tf_op jit(solution)/shard_map/ppermute | solution.py:353
  533.5 5.7 pack_rows.2
  539.2 18.9 %collective-permute-done.5.refs_3_ = bf16[2,512,512]{2,1,0:T(8,128)(2,1)S(1)} collective-permute-done((bf16[2,512,512]{2,1,0:T(8,128)(2,1)}, bf16[2,512,512]{2,1,0:T(8,128)(2,1)S(1)}, u32[]{:S(2)}, u32[]{:S(2)}) %collective-permute-start.5) | collective-permute-done | bytes 1048608 | tf_op jit(solution)/shard_map/ppermute | solution.py:353
  558.1 1.0 copy-done.8
  559.1 2.0 collective-permute-start.1
  561.8 15.1 %mix_mm.2 = bf16[512,4096]{1,0:T(8,128)(2,1)} custom-call(bf16[2,512,512]{2,1,0:T(8,128)(2,1)} %get-tuple-element.75.refs_0_, bf16[2,512,512]{2,1,0:T(8,128)(2,1)} %collective-permute-done.3.refs_1_, bf16[2,512,512]{2,1,0:T(8,128)(2,1)} %collective-permute-done.4.refs_2_, bf16[2,512,512]{2,1,0:T(8,128)(2,1)} %copy-done.8, bf16[512,4096]{1,0:T(8,128)(2,1)} %refs_4_.3, ...), custom_call_target="tpu_custom_call" | custom-call | flops 8589934592 | bytes 25165824 | tf_op jit(solution)/shard_map/mix_mm/pallas_call | solution.py:296
  576.9 19.6 %collective-permute-done.1.refs_2_ = bf16[2,512,768]{2,1,0:T(8,128)(2,1)S(1)} collective-permute-done((bf16[2,512,768]{2,1,0:T(8,128)(2,1)}, bf16[2,512,768]{2,1,0:T(8,128)(2,1)S(1)}, u32[]{:S(2)}, u32[]{:S(2)}) %collective-permute-start.1) | collective-permute-done | bytes 1572896 | tf_op jit(solution)/shard_map/ppermute | solution.py:353
  596.6 33.4 %collective-permute-done.2.refs_3_ = bf16[2,512,768]{2,1,0:T(8,128)(2,1)} collective-permute-done((bf16[2,512,768]{2,1,0:T(8,128)(2,1)}, bf16[2,512,768]{2,1,0:T(8,128)(2,1)}, u32[]{:S(2)}, u32[]{:S(2)}) %collective-permute-start.2) | collective-permute-done | bytes 1572896 | tf_op jit(solution)/shard_map/ppermute | solution.py:353
  630.0 1.5 collective-permute-start.13
  631.5 17.4 %grad_mm.4 = bf16[256,4096]{1,0:T(8,128)(2,1)} custom-call(s32[4]{0:T(128)} %pad_add_fusion.owner_ref, bf16[2,512,768]{2,1,0:T(8,128)(2,1)} %get-tuple-element.87.refs_0_, bf16[2,512,768]{2,1,0:T(8,128)(2,1)} %copy-done.3, bf16[2,512,768]{2,1,0:T(8,128)(2,1)} %copy-done.4, bf16[2,512,768]{2,1,0:T(8,128)(2,1)} %collective-permute-done.2.refs_3_, ...), custom_call_target="tpu_custom_call" | custom-call | flops 6442450944 | bytes 29360128 | tf_op jit(solution)/shard_map/grad_mm/pallas_call | solution.py:263
  648.9 1.1 collective-permute-start.12
  650.0 17.4 %grad_mm.5 = bf16[256,4096]{1,0:T(8,128)(2,1)} custom-call(s32[4]{0:T(128)} %pad_add_fusion.owner_ref, bf16[2,512,768]{2,1,0:T(8,128)(2,1)} %get-tuple-element.87.refs_0_, bf16[2,512,768]{2,1,0:T(8,128)(2,1)} %copy-done.3, bf16[2,512,768]{2,1,0:T(8,128)(2,1)} %copy-done.4, bf16[2,512,768]{2,1,0:T(8,128)(2,1)} %collective-permute-done.2.refs_3_, ...), custom_call_target="tpu_custom_call" | custom-call | flops 6442450944 | bytes 29360128 | tf_op jit(solution)/shard_map/grad_mm/pallas_call | solution.py:263
  667.4 1.0 collective-permute-start.14
  668.5 4.5 fusion.11
  673.0 22.9 %grad_mm.3.own_ref = f32[512,4096]{1,0:T(8,128)} custom-call(s32[4]{0:T(128)} %pad_add_fusion.owner_ref, bf16[2,512,768]{2,1,0:T(8,128)(2,1)} %get-tuple-element.87.refs_0_, bf16[2,512,768]{2,1,0:T(8,128)(2,1)} %copy-done.3, bf16[2,512,768]{2,1,0:T(8,128)(2,1)} %copy-done.4, bf16[2,512,768]{2,1,0:T(8,128)(2,1)} %collective-permute-done.2.refs_3_, ...), custom_call_target="tpu_custom_call" | custom-call | flops 12884901888 | bytes 33554432 | tf_op jit(solution)/shard_map/grad_mm/pallas_call | solution.py:263
  695.9 16.0 %mix_mm.3 = f32[512,4096]{1,0:T(8,128)} custom-call(bf16[2,512,512]{2,1,0:T(8,128)(2,1)} %get-tuple-element.75.refs_0_, bf16[2,512,512]{2,1,0:T(8,128)(2,1)} %collective-permute-done.3.refs_1_, bf16[2,512,512]{2,1,0:T(8,128)(2,1)} %collective-permute-done.4.refs_2_, bf16[2,512,512]{2,1,0:T(8,128)(2,1)} %copy-done.8, bf16[512,4096]{1,0:T(8,128)(2,1)} %refs_4_.3, ...), custom_call_target="tpu_custom_call" | custom-call | flops 8589934592 | bytes 25165824 | tf_op jit(solution)/shard_map/mix_mm/pallas_call | solution.py:296
  711.9 11.0 %collective-permute-done.13 = bf16[512,4096]{1,0:T(8,128)(2,1)} collective-permute-done((bf16[512,4096]{1,0:T(8,128)(2,1)}, bf16[512,4096]{1,0:T(8,128)(2,1)}, u32[]{:S(2)}, u32[]{:S(2)}) %collective-permute-start.13) | collective-permute-done | bytes 4194336 | tf_op jit(solution)/shard_map/ppermute | solution.py:353
  722.9 10.0 %fusion.3 = bf16[512,4096]{1,0:T(8,128)(2,1)} fusion(bf16[512,4096]{1,0:T(8,128)(2,1)} %x_ref.3, f32[512,4096]{1,0:T(8,128)} %mix_mm.3, bf16[512,4096]{1,0:T(8,128)(2,1)} %collective-permute-done.13), kind=kLoop, calls=%fused_computation.6 | loop fusion | flops 10485760 | bytes 20971520 | tf_op jit(solution)/shard_map/convert_element_type | solution.py:454
  732.9 7.8 %shard_map.137 = (bf16[512,4096]{1,0:T(8,128)(2,1)}, f32[1,4096]{1,0:T(1,128)}) custom-call(f32[512,4096]{1,0:T(8,128)} %grad_mm.3.own_ref, bf16[256,4096]{1,0:T(8,128)(2,1)} %collective-permute-done.12.got_ref, bf16[512,4096]{1,0:T(8,128)(2,1)} %x_ref.3, bf16[512,4096]{1,0:T(8,128)(2,1)} %dy_ref.3, f32[1,4096]{1,0:T(1,128)} %bitcast.50), custom_call_target="tpu_custom_call" | custom-call | flops 20971520 | bytes 12582912 | tf_op jit(solution)/shard_map/pallas_call | solution.py:340
  740.7 0.9 collective-permute-done.14.got_ref
  741.6 1.3 copy-done.5
  742.9 7.8 %shard_map.138 = (bf16[512,4096]{1,0:T(8,128)(2,1)}, f32[1,4096]{1,0:T(1,128)}) custom-call(f32[512,4096]{1,0:T(8,128)} %grad_mm.3.own_ref, bf16[256,4096]{1,0:T(8,128)(2,1)} %copy-done.5, bf16[512,4096]{1,0:T(8,128)(2,1)} %x_ref.3, bf16[512,4096]{1,0:T(8,128)(2,1)} %dy_ref.3, f32[1,4096]{1,0:T(1,128)} %bitcast.51, ...), custom_call_target="tpu_custom_call", output_to_operand_aliasing={{0}: (5, {})} | custom-call | flops 20971520 | bytes 12582912 | tf_op jit(solution)/shard_map/pallas_call | solution.py:340
  750.8 1.4 collective-permute-done.15
  752.9 1.1 collective-permute-start.16
  754.0 2.7 collective-permute-done.16
  757.3 3.0 collective-permute-done.17
  (56 shorter events, 7.0 us)
Async XLA Ops:
  7.2 167.7 %all-gather.4.cloned.1.call-start = ((), (), s32[]{:S(2)}) async-start(), calls=%async_computation | async-start | bytes 37748736 | tf_op jit(solution)/shard_map/all_gather | solution.py:403
  7.2 3.5 copy-start.1
  15.0 268.9 %all-gather.6.cloned.1.call-start = ((), (), s32[]{:S(2)}) async-start(), calls=%async_computation.1 | async-start | bytes 18874368 | tf_op jit(solution)/shard_map/all_gather | solution.py:408
  19.9 334.6 %all-gather.8.cloned.1.call-start = ((), (), s32[]{:S(2)}) async-start(), calls=%async_computation.2 | async-start | bytes 18874368 | tf_op jit(solution)/shard_map/all_gather | solution.py:417
  174.9 32.3 %copy-start.7 = (s32[4096]{0:T(1024)S(1)}, s32[4096]{0:T(1024)}, u32[]{:S(2)}) copy-start(s32[4096]{0:T(1024)} %param.10) | copy-start | bytes 49156
  207.3 10.3 %copy-start.6 = (s32[4096]{0:T(1024)}, s32[4096]{0:T(1024)S(1)}, u32[]{:S(2)}) copy-start(s32[4096]{0:T(1024)S(1)} %get-tuple-element.117) | copy-start | bytes 49156
  369.1 96.4 %collective-permute-start.7 = (bf16[4096,512]{1,0:T(8,128)(2,1)}, bf16[4096,512]{1,0:T(8,128)(2,1)}, u32[]{:S(2)}, u32[]{:S(2)}) collective-permute-start(bf16[4096,512]{1,0:T(8,128)(2,1)} %refs_4_.4), channel_id=1, source_target_pairs={{0,4},{1,5},{2,6},{3,7},{4,0},{5,1},{6,2},{7,3},{8,12},{9,13},{10,... | collective-permute-start | bytes 12582920 | tf_op jit(solution)/shard_map/ppermute | solution.py:353
  369.1 123.2 %collective-permute-start.6 = (bf16[512,4096]{1,0:T(8,128)(2,1)}, bf16[512,4096]{1,0:T(8,128)(2,1)}, u32[]{:S(2)}, u32[]{:S(2)}) collective-permute-start(bf16[512,4096]{1,0:T(8,128)(2,1)} %refs_4_.3), channel_id=1, source_target_pairs={{0,2},{1,3},{2,0},{3,1},{4,6},{5,7},{6,4},{7,5},{8,10},{9,11},{10,... | collective-permute-start | bytes 12582920 | tf_op jit(solution)/shard_map/ppermute | solution.py:353
  422.2 25.2 %copy-start.2 = (bf16[4096,256]{1,0:T(8,128)(2,1)S(1)}, bf16[4096,256]{1,0:T(8,128)(2,1)}, u32[]{:S(2)}) copy-start(bf16[4096,256]{1,0:T(8,128)(2,1)} %get-tuple-element.69) | copy-start | bytes 6291460
  447.5 18.0 %copy-start = (bf16[4096,512]{1,0:T(8,128)(2,1)S(1)}, bf16[4096,512]{1,0:T(8,128)(2,1)}, u32[]{:S(2)}) copy-start(bf16[4096,512]{1,0:T(8,128)(2,1)} %get-tuple-element.74.o_ref) | copy-start | bytes 12582916
  492.3 66.8 %collective-permute-start.8 = (bf16[512,4096]{1,0:T(8,128)(2,1)}, bf16[512,4096]{1,0:T(8,128)(2,1)}, u32[]{:S(2)}, u32[]{:S(2)}) collective-permute-start(bf16[512,4096]{1,0:T(8,128)(2,1)} %refs_4_.3), channel_id=1, source_target_pairs={{0,1},{1,0},{2,3},{3,2},{4,5},{5,4},{6,7},{7,6},{8,9},{9,8},{10,11... | collective-permute-start | bytes 12582920 | tf_op jit(solution)/shard_map/ppermute | solution.py:353
  492.3 68.8 %collective-permute-start.9 = (bf16[512,4096]{1,0:T(8,128)(2,1)}, bf16[512,4096]{1,0:T(8,128)(2,1)}, u32[]{:S(2)}, u32[]{:S(2)}) collective-permute-start(bf16[512,4096]{1,0:T(8,128)(2,1)} %collective-permute-done.6.refs_6_), channel_id=1, source_target_pairs={{0,1},{1,0},{2,3},{3,2},{4,5},{5,4},{6,7},{7,6},{8,9},{9,8},{10,11... | collective-permute-start | bytes 12582920 | tf_op jit(solution)/shard_map/ppermute | solution.py:353
  497.8 9.5 %collective-permute-start.3 = (bf16[2,512,512]{2,1,0:T(8,128)(2,1)}, bf16[2,512,512]{2,1,0:T(8,128)(2,1)}, u32[]{:S(2)}, u32[]{:S(2)}) collective-permute-start(bf16[2,512,512]{2,1,0:T(8,128)(2,1)} %get-tuple-element.76), channel_id=1, source_target_pairs={{0,1},{1,0},{2,3},{3,2},{4,5},{5,4},{6,7},{7,6},{8,9},{9,8},{10,11... | collective-permute-start | bytes 3145736 | tf_op jit(solution)/shard_map/ppermute | solution.py:353
  497.9 133.6 %collective-permute-start.10 = (bf16[4096,512]{1,0:T(8,128)(2,1)}, bf16[4096,512]{1,0:T(8,128)(2,1)}, u32[]{:S(2)}, u32[]{:S(2)}) collective-permute-start(bf16[4096,512]{1,0:T(8,128)(2,1)} %refs_4_.4), channel_id=1, source_target_pairs={{0,1},{1,0},{2,3},{3,2},{4,5},{5,4},{6,7},{7,6},{8,9},{9,8},{10,11... | collective-permute-start | bytes 12582920 | tf_op jit(solution)/shard_map/ppermute | solution.py:353
  498.3 133.1 %collective-permute-start.11 = (bf16[4096,512]{1,0:T(8,128)(2,1)}, bf16[4096,512]{1,0:T(8,128)(2,1)}, u32[]{:S(2)}, u32[]{:S(2)}) collective-permute-start(bf16[4096,512]{1,0:T(8,128)(2,1)} %collective-permute-done.7.refs_6_), channel_id=1, source_target_pairs={{0,1},{1,0},{2,3},{3,2},{4,5},{5,4},{6,7},{7,6},{8,9},{9,8},{10,11... | collective-permute-start | bytes 12582920 | tf_op jit(solution)/shard_map/ppermute | solution.py:353
  507.3 25.5 %collective-permute-start.4 = (bf16[2,512,512]{2,1,0:T(8,128)(2,1)}, bf16[2,512,512]{2,1,0:T(8,128)(2,1)}, u32[]{:S(2)}, u32[]{:S(2)}) collective-permute-start(bf16[2,512,512]{2,1,0:T(8,128)(2,1)} %get-tuple-element.77), channel_id=1, source_target_pairs={{0,2},{1,3},{2,0},{3,1},{4,6},{5,7},{6,4},{7,5},{8,10},{9,11},{10,... | collective-permute-start | bytes 3145736 | tf_op jit(solution)/shard_map/ppermute | solution.py:353
  532.8 25.3 %collective-permute-start.5 = (bf16[2,512,512]{2,1,0:T(8,128)(2,1)}, bf16[2,512,512]{2,1,0:T(8,128)(2,1)S(1)}, u32[]{:S(2)}, u32[]{:S(2)}) collective-permute-start(bf16[2,512,512]{2,1,0:T(8,128)(2,1)} %get-tuple-element.78), channel_id=1, source_target_pairs={{0,3},{1,2},{2,1},{3,0},{4,7},{5,6},{6,5},{7,4},{8,11},{9,10},{10,... | collective-permute-start | bytes 3145736 | tf_op jit(solution)/shard_map/ppermute | solution.py:353
  558.1 1.0 copy-start.8
  559.1 17.8 %collective-permute-start = (bf16[2,512,768]{2,1,0:T(8,128)(2,1)}, bf16[2,512,768]{2,1,0:T(8,128)(2,1)S(1)}, u32[]{:S(2)}, u32[]{:S(2)}) collective-permute-start(bf16[2,512,768]{2,1,0:T(8,128)(2,1)} %get-tuple-element.71), channel_id=1, source_target_pairs={{0,1},{1,0},{2,3},{3,2},{4,5},{5,4},{6,7},{7,6},{8,9},{9,8},{10,11... | collective-permute-start | bytes 4718600 | tf_op jit(solution)/shard_map/ppermute | solution.py:353
  559.1 37.5 %collective-permute-start.1 = (bf16[2,512,768]{2,1,0:T(8,128)(2,1)}, bf16[2,512,768]{2,1,0:T(8,128)(2,1)S(1)}, u32[]{:S(2)}, u32[]{:S(2)}) collective-permute-start(bf16[2,512,768]{2,1,0:T(8,128)(2,1)} %get-tuple-element.72), channel_id=1, source_target_pairs={{0,4},{1,5},{2,6},{3,7},{4,0},{5,1},{6,2},{7,3},{8,12},{9,13},{10,... | collective-permute-start | bytes 4718600 | tf_op jit(solution)/shard_map/ppermute | solution.py:353
  561.1 68.9 %collective-permute-start.2 = (bf16[2,512,768]{2,1,0:T(8,128)(2,1)}, bf16[2,512,768]{2,1,0:T(8,128)(2,1)}, u32[]{:S(2)}, u32[]{:S(2)}) collective-permute-start(bf16[2,512,768]{2,1,0:T(8,128)(2,1)} %get-tuple-element.73), channel_id=1, source_target_pairs={{0,5},{1,4},{2,7},{3,6},{4,1},{5,0},{6,3},{7,2},{8,13},{9,12},{10,... | collective-permute-start | bytes 4718600 | tf_op jit(solution)/shard_map/ppermute | solution.py:353
  576.9 54.6 %copy-start.3 = (bf16[2,512,768]{2,1,0:T(8,128)(2,1)}, bf16[2,512,768]{2,1,0:T(8,128)(2,1)S(1)}, u32[]{:S(2)}) copy-start(bf16[2,512,768]{2,1,0:T(8,128)(2,1)S(1)} %collective-permute-done.refs_1_) | copy-start | bytes 4718596
  596.6 34.9 %copy-start.4 = (bf16[2,512,768]{2,1,0:T(8,128)(2,1)}, bf16[2,512,768]{2,1,0:T(8,128)(2,1)S(1)}, u32[]{:S(2)}) copy-start(bf16[2,512,768]{2,1,0:T(8,128)(2,1)S(1)} %collective-permute-done.1.refs_2_) | copy-start | bytes 4718596
  630.0 92.9 %collective-permute-start.13 = (bf16[512,4096]{1,0:T(8,128)(2,1)}, bf16[512,4096]{1,0:T(8,128)(2,1)}, u32[]{:S(2)}, u32[]{:S(2)}) collective-permute-start(bf16[512,4096]{1,0:T(8,128)(2,1)} %mix_mm.2), channel_id=1, source_target_pairs={{0,4},{1,5},{2,6},{3,7},{4,0},{5,1},{6,2},{7,3},{8,12},{9,13},{10,... | collective-permute-start | bytes 12582920 | tf_op jit(solution)/shard_map/ppermute | solution.py:353
  648.9 84.0 %collective-permute-start.12 = (bf16[256,4096]{1,0:T(8,128)(2,1)}, bf16[256,4096]{1,0:T(8,128)(2,1)}, u32[]{:S(2)}, u32[]{:S(2)}) collective-permute-start(bf16[256,4096]{1,0:T(8,128)(2,1)} %grad_mm.4), channel_id=1, source_target_pairs={{0,2},{1,3},{2,0},{3,1},{4,6},{5,7},{6,4},{7,5},{8,10},{9,11},{10,... | collective-permute-start | bytes 6291464 | tf_op jit(solution)/shard_map/ppermute | solution.py:353
  667.4 74.2 %collective-permute-start.14 = (bf16[256,4096]{1,0:T(8,128)(2,1)}, bf16[256,4096]{1,0:T(8,128)(2,1)S(1)}, u32[]{:S(2)}, u32[]{:S(2)}) collective-permute-start(bf16[256,4096]{1,0:T(8,128)(2,1)} %grad_mm.5), channel_id=1, source_target_pairs={{0,2},{1,3},{2,0},{3,1},{4,6},{5,7},{6,4},{7,5},{8,10},{9,11},{10,... | collective-permute-start | bytes 6291464 | tf_op jit(solution)/shard_map/ppermute | solution.py:353
  741.6 1.3 copy-start.5
  750.8 1.4 collective-permute-start.15
  752.9 3.7 collective-permute-start.16
  756.6 3.7 collective-permute-start.17
Sparse Core Ops, SparseCore 0:
  15.2 159.6 all-gather.3
  177.3 85.9 all-gather.5
  265.2 85.9 all-gather.7

commit v5 on v4

--- a/solution.py
+++ b/solution.py
@@ -236,7 +236,7 @@
 
 
 def grad_mm_kernel(width, owner_ref, *refs):
-    g_refs, w_refs, (wk_ref, wv_ref, out_ref, x_s, w_s) = refs[:4], refs[4:8], refs[8:]
+    g_refs, w_refs, (wk_ref, wv_ref, *out_refs, x_s, w_s) = refs[:4], refs[4:8], refs[8:]
     span = width + 2 * HEAD_DIM
 
     @pl.when(pl.program_id(0) == 0)
@@ -249,24 +249,26 @@
         w_s[:, p * span:p * span + width] = w_ref[...]
         w_s[:, p * span + width:p * span + width + HEAD_DIM] = wk_ref[:, head]
         w_s[:, p * span + width + HEAD_DIM:(p + 1) * span] = wv_ref[:, head]
-    out_ref[...] = lax.dot_general(x_s[...], w_s[...], NT, preferred_element_type=F32).astype(out_ref.dtype)
-
-
-def grad_mm(owners, pieces, half, weights, wk_all, wv_all, dtype, part=0, parts=1):
+    out = lax.dot_general(x_s[...], w_s[...], NT, preferred_element_type=F32)
+    rows = out_refs[0].shape[0]
+    for r, out_ref in enumerate(out_refs):
+        out_ref[...] = out[r * rows:(r + 1) * rows].astype(out_ref.dtype)
+
+
+def grad_mm(owners, pieces, half, weights, wk_all, wv_all, dtype, parts=1):
     _, rows, span = pieces[0].shape
-    rows = rows // parts
     d_model, width = weights[0].shape
     bn = 512
-    g_spec = pl.BlockSpec((1, rows, span), lambda j, *_: (half, part, 0))
+    g_spec = pl.BlockSpec((1, rows, span), lambda j, *_: (half, 0, 0))
     w_spec = pl.BlockSpec((bn, width), lambda j, *_: (j, 0))
     kv_spec = pl.BlockSpec((bn, wk_all.shape[1]), lambda j, *_: (j, 0))
     return pl.pallas_call(
         functools.partial(grad_mm_kernel, width),
-        out_shape=jax.ShapeDtypeStruct((rows, d_model), dtype),
+        out_shape=[jax.ShapeDtypeStruct((rows // parts, d_model), dtype)] * parts,
         grid_spec=pltpu.PrefetchScalarGridSpec(
             num_scalar_prefetch=1, grid=(d_model // bn,),
             in_specs=[g_spec] * 4 + [w_spec] * 4 + [kv_spec] * 2,
-            out_specs=pl.BlockSpec((rows, bn), lambda j, *_: (0, j)),
+            out_specs=[pl.BlockSpec((rows // parts, bn), lambda j, *_: (0, j))] * parts,
             scratch_shapes=[pltpu.VMEM((rows, 4 * span), BF16), pltpu.VMEM((bn, 4 * span), BF16)]),
         compiler_params=pltpu.CompilerParams(dimension_semantics=("arbitrary",), vmem_limit_bytes=VMEM_LIMIT),
         cost_estimate=pl.CostEstimate(flops=2 * rows * 4 * span * d_model, bytes_accessed=2 * (4 * span + 2 * rows) * d_model, transcendentals=0),
@@ -275,7 +277,7 @@
 
 
 def mix_mm_kernel(width, *refs):
-    o_refs, w_refs, (out_ref, x_s, w_s) = refs[:4], refs[4:8], refs[8:]
+    o_refs, w_refs, (*add_refs, out_ref, x_s, w_s) = refs[:4], refs[4:8], refs[8:]
 
     @pl.when(pl.program_id(0) == 0)
     def _():
@@ -284,10 +286,13 @@
 
     for p, w_ref in enumerate(w_refs):
         w_s[p * width:(p + 1) * width, :] = w_ref[...]
-    out_ref[...] = jnp.dot(x_s[...], w_s[...], preferred_element_type=F32).astype(out_ref.dtype)
-
-
-def mix_mm(pieces, half, weights, dtype):
+    out = jnp.dot(x_s[...], w_s[...], preferred_element_type=F32)
+    for add_ref in reversed(add_refs):
+        out = out + add_ref[...].astype(F32)
+    out_ref[...] = out.astype(out_ref.dtype)
+
+
+def mix_mm(pieces, half, weights, dtype, added=()):
     _, rows, width = pieces[0].shape
     d_model = weights[0].shape[1]
     bn = 512
@@ -297,13 +302,13 @@
         functools.partial(mix_mm_kernel, width),
         out_shape=jax.ShapeDtypeStruct((rows, d_model), dtype),
         grid=(d_model // bn,),
-        in_specs=[o_spec] * 4 + [w_spec] * 4,
+        in_specs=[o_spec] * 4 + [w_spec] * 4 + [pl.BlockSpec((rows, bn), lambda j: (0, j))] * len(added),
         out_specs=pl.BlockSpec((rows, bn), lambda j: (0, j)),
         scratch_shapes=[pltpu.VMEM((rows, 4 * width), BF16), pltpu.VMEM((4 * width, bn), BF16)],
         compiler_params=pltpu.CompilerParams(dimension_semantics=("arbitrary",), vmem_limit_bytes=VMEM_LIMIT),
         cost_estimate=pl.CostEstimate(flops=2 * rows * 4 * width * d_model, bytes_accessed=2 * (4 * width + 2 * rows) * d_model, transcendentals=0),
         name="mix_mm",
-    )(*pieces, *weights)
+    )(*pieces, *weights, *added)
 
 
 def finish_kernel(part, own_ref, got_ref, x_ref, dy_ref, gain_ref, *refs):
@@ -412,6 +417,7 @@
         lo = doc_start[::BQ] // BK
         full = (doc_start[BQ - 1::BQ] + BK - 1) // BK
 
+        h_full, cos_t, sin_t, lo, full, doc_start, wqkv = lax.optimization_barrier((h_full, cos_t, sin_t, lo, full, doc_start, wqkv))
         qkv = dot32(h_full, wqkv).astype(BF16)
         *dy_rest, qkv = lax.optimization_barrier((*dy_in[1:], qkv))
         dy_full += [lax.all_gather(dy_part, 'tp', axis=0, tiled=True) for dy_part in dy_rest]
@@ -435,23 +441,24 @@
         wq_near, wq_own, d_wq, d_wkv = lax.optimization_barrier((wq_near, wq_own, d_wq, d_wkv))
         wq_side = swap(wq_own, 1, tp_size)
         wq_group = [wq_own, wq_side, wq_near, swap(wq_near, 1, tp_size)]
+        wo_near, wo_own, d_wkv = lax.optimization_barrier((wo_near, wo_own, d_wkv))
+        wo_side = swap(wo_own, 1, tp_size)
+        wo_group = [wo_own, wo_side, wo_near, swap(wo_near, 1, tp_size)]
         o_blocks, d_wkv = lax.optimization_barrier((o_blocks, d_wkv))
         d_wo = dot32(o_blocks[:, 0].reshape(-1, width), dy_full[0], TN)
         d_wo = (d_wo + sum(dot32(o_blocks[:, p].reshape(-1, width), dy_full[p], TN) for p in range(1, parts))).astype(BF16)
-        wo_near, wo_own, d_wo = lax.optimization_barrier((wo_near, wo_own, d_wo))
-        wo_group = [wo_own, swap(wo_own, 1, tp_size), wo_near, swap(wo_near, 1, tp_size)]
         mix_mate = mix_mm(o_pieces, 1, wo_group, BF16)
         dq_pieces, mix_mate, d_wq, d_wkv = lax.optimization_barrier((dq_pieces, mix_mate, d_wq, d_wkv))
         mix_got = swap(mix_mate, y_bit, tp_size)
         owners = jnp.stack([me ^ bit for bit in (0, 1, y_bit, y_bit | 1)])
         halves = 2
+        dh_mate = grad_mm(owners, dq_pieces, 1, wq_group, wk_all, wv_all, BF16, halves)
         dh_got = []
         for p in range(halves):
-            dh_mate = grad_mm(owners, dq_pieces, 1, wq_group, wk_all, wv_all, BF16, p, halves)
-            dh_got.append(swap(dh_mate, x_bit, tp_size))
-        dh_own = grad_mm(owners, dq_pieces, 0, wq_group, wk_all, wv_all, F32)
-        mix_own = mix_mm(o_pieces, 0, wo_group, F32)
-        result = (x_f32 + (mix_own + mix_got.astype(F32))).astype(BF16)
+            dh_got.append(swap(dh_mate[p], x_bit, tp_size))
+        dh_own, = grad_mm(owners, dq_pieces, 0, wq_group, wk_all, wv_all, F32)
+        mix_got, dh_own = lax.optimization_barrier((mix_got, dh_own))
+        result = mix_mm(o_pieces, 0, wo_group, BF16, (x_blk, mix_got))
         d_wk, d_wv = d_wkv[:, :HEAD_DIM], d_wkv[:, HEAD_DIM:]
         dh_own, dh_got[0], result, d_wo, d_wk, d_wv = lax.optimization_barrier((dh_own, dh_got[0], result, d_wo, d_wk, d_wv))
         done = None

time: 772 us -> 726 us (0.940)
  waiting for transfers between devices: 278 us -> 239 us
  Pallas kernels: 286 us -> 272 us
    ppermute x15, waiting for transfers between devices: 117 us -> 88.2 us  [swap(): return lax.ppermute(value, 'tp', [(d, d ^ bit) for d in range(tp_size)])]
    all_gather x1, waiting for transfers between devices: 153 us -> 136 us  [layer(): h_full = lax.all_gather(hidden, 'tp', axis=0, tiled=True)]
    pallas_call x3 -> x2, Pallas kernels: 57.8 us -> 44.6 us  [grad_mm(): pl.pallas_call(functools.partial(grad_mm_kernel, width), out_shape=[jax.S...]
    convert_element_type x2 -> x0, other arithmetic: 9.98 us -> none  [the longest x1 9.98 us: layer(): result = (x_f32 + (mix_own + mix_got.astype(F32))).astype(BF16)]
    all_gather x1, waiting for transfers between devices: 0.01 us -> 8.92 us  [layer(): lax.all_gather(dy_part, 'tp', axis=0, tiled=True)]
  transfers between devices with their start and end apart: 21 -> 21, of which waited for: 11 -> 10; matrix products, arithmetic and copies ran while one was open for 20% -> 22% of each run, Pallas kernels for 36% -> 37%
where the time goes in v5:
time: 726 us; the launch traced here: 722 us
  Pallas kernels  272 us (37%)
  waiting for transfers between devices  239 us (33%)
  matrix products  137 us (19%)
  other arithmetic  26.3 us (4%)
  local copies, waits for them, and re-layouts  19.6 us (3%)
  between operations  14.2 us (2%)
  starting transfers between devices  14 us (2%)
    dot_general x7, matrix products, dot32(): return lax.dot_general(a, b, dims, preferred_element_type=F32)  137 us
    all_gather x1, waiting for transfers between devices, layer(): h_full = lax.all_gather(hidden, 'tp', axis=0, tiled=True)  136 us
    pallas_call x2, Pallas kernels, attend_backward(): pl.pallas_call(functools.partial(bwd_kernel, heads, half, parts, n_blk),...  107 us
    ppermute x15, waiting for transfers between devices, swap(): return lax.ppermute(value, 'tp', [(d, d ^ bit) for d in range(tp_size)])  88.2 us
    pallas_call x1, Pallas kernels, attend_forward(): pl.pallas_call(functools.partial(fwd_kernel, heads), out_shape=(jax.Shape...  63.1 us
    pallas_call x2, Pallas kernels, grad_mm(): pl.pallas_call(functools.partial(grad_mm_kernel, width), out_shape=[jax.S...  44.6 us
    pallas_call x2, Pallas kernels, mix_mm(): pl.pallas_call(functools.partial(mix_mm_kernel, width), out_shape=jax.Sha...  31.9 us
    pallas_call x2, Pallas kernels, finish(): pl.pallas_call(functools.partial(finish_kernel, part), out_shape=(jax.Sha...  15.7 us
  transfers between devices with their start and end apart: 21, of which 10 were waited for; matrix products, arithmetic and copies ran while one was open for 22% of the time, Pallas kernels for 37%

profile of v5, /device:TPU:0, one launch (start us, length us, event | category | flops | bytes accessed | tf_op | source)
XLA Modules:
  0.0 721.9 jit_solution(3214094077671856478)
XLA Ops:
  7.2 3.2 fusion
  10.7 4.4 fusion.2
  15.1 4.7 fusion.6
  20.9 1.8 constant_dynamic-slice_fusion
  22.7 7.5 %fusion.3 = (f32[4096,64]{1,0:T(8,128)S(1)}, f32[4096,64]{1,0:T(8,128)S(1)}, f32[4096,64]{1,0:T(8,128)S(1)}) fusion(f32[64]{0:T(128)S(1)} %negate_power_fusion, f32[4096]{0:T(1024)S(1)} %get-tuple-element.139), kind=kLoop, calls=%fused_computation.15 | loop fusion | flops 524288 | bytes 3162368 | tf_op jit(solution)/shard_map/neg | solution.py:28
  30.2 3.2 pad_maximum_fusion.1
  33.4 5.5 pad_maximum_fusion
  38.9 136.0 %all-gather.4.cloned.1.call-done = bf16[4096,4096]{1,0:T(8,128)(2,1)} async-done(((bf16[512,4096]{1,0:T(8,128)(2,1)}), bf16[4096,4096]{1,0:T(8,128)(2,1)}) %all-gather.4.cloned.1.call-update) | async-done | bytes 33554448 | tf_op jit(solution)/shard_map/all_gather | solution.py:408
  174.9 32.9 %convolution_convert_fusion.q_ref.k_ref.v_ref = bf16[4096,768]{1,0:T(8,128)(2,1)} fusion(bf16[4096,4096]{1,0:T(8,128)(2,1)} %all-gather.4.cloned.1.call-done, bf16[4096,768]{1,0:T(8,128)(2,1)} %pad_maximum_fusion), kind=kOutput, calls=%fused_computation.6 | convolution fusion | flops 25772949504 | bytes 46137344 | tf_op jit(solution)/shard_map/dot_general | solution.py:227
  207.8 2.0 copy.17.ds_ref
  209.8 63.1 %attend_fwd.1 = (bf16[4096,512]{1,0:T(8,128)(2,1)}, f32[16,1,1024]{2,1,0:T(1,128)}) custom-call(s32[16]{0:T(128)} %get-tuple-element.68.lo_ref, s32[16]{0:T(128)} %get-tuple-element.69.full_ref, bf16[4096,768]{1,0:T(8,128)(2,1)} %convolution_convert_fusion.q_ref.k_ref.v_ref, bf16[4096,768]{1,0:T(8,128)(2,1)} %convolution_convert_fusion.q_ref.k_ref.v_ref, ...), custom_call_target="tpu_custom_call" | custom-call | flops 17179869184 | bytes 16777216 | tf_op jit(solution)/shard_map/attend_fwd/pallas_call | solution.py:170
  272.9 15.4 %convolution_convert_fusion.2.do_ref = bf16[2048,512]{1,0:T(8,128)(2,1)} fusion(bf16[2048,4096]{1,0:T(8,128)(2,1)} %all-gather.6.cloned.1.call-done, bf16[512,4096]{1,0:T(8,128)(2,1)} %refs_4_.3), kind=kOutput, calls=%fused_computation.11 | convolution fusion | flops 8590983168 | bytes 23068672 | tf_op jit(solution)/shard_map/dot_general | solution.py:227
  288.3 54.5 %shard_map.135 = (bf16[4096,512]{1,0:T(8,128)(2,1)}, f32[4096,128]{1,0:T(8,128)}, f32[4096,128]{1,0:T(8,128)}) custom-call(s32[16]{0:T(128)} %get-tuple-element.68.lo_ref, s32[16]{0:T(128)} %get-tuple-element.69.full_ref, bf16[4096,768]{1,0:T(8,128)(2,1)} %convolution_convert_fusion.q_ref.k_ref.v_ref, ...), custom_call_target="tpu_custom_call" | custom-call | flops 21474836480 | bytes 12582912 | tf_op jit(solution)/shard_map/pallas_call | solution.py:211
  342.9 8.9 %all-gather.8.cloned.1.call-done = bf16[2048,4096]{1,0:T(8,128)(2,1)} async-done(((bf16[256,4096]{1,0:T(8,128)(2,1)}), bf16[2048,4096]{1,0:T(8,128)(2,1)}) %all-gather.8.cloned.1.call-update) | async-done | bytes 16777232 | tf_op jit(solution)/shard_map/all_gather | solution.py:423
  351.8 14.6 %convolution_convert_fusion.3.do_ref = bf16[2048,512]{1,0:T(8,128)(2,1)} fusion(bf16[2048,4096]{1,0:T(8,128)(2,1)} %all-gather.8.cloned.1.call-done, bf16[512,4096]{1,0:T(8,128)(2,1)} %refs_4_.3), kind=kOutput, calls=%fused_computation.12 | convolution fusion | flops 8590983168 | bytes 23068672 | tf_op jit(solution)/shard_map/dot_general | solution.py:227
  367.1 1.3 collective-permute-start.6
  368.4 52.2 %shard_map.136 = (bf16[4096,512]{1,0:T(8,128)(2,1)}, bf16[4096,256]{1,0:T(8,128)(2,1)}) custom-call(s32[16]{0:T(128)} %get-tuple-element.68.lo_ref, s32[16]{0:T(128)} %get-tuple-element.69.full_ref, bf16[4096,768]{1,0:T(8,128)(2,1)} %convolution_convert_fusion.q_ref.k_ref.v_ref, ...), custom_call_target="tpu_custom_call", output_to_operand_aliasing={{0}: (13, {})} | custom-call | flops 21474836480 | bytes 12582912 | tf_op jit(solution)/shard_map/pallas_call | solution.py:211
  420.6 17.8 %fusion.7 = f32[4096,256]{1,0:T(8,128)} fusion(bf16[4096,4096]{1,0:T(8,128)(2,1)} %all-gather.4.cloned.1.call-done, bf16[4096,256]{1,0:T(8,128)(2,1)} %get-tuple-element.87), kind=kOutput, calls=%fused_computation.33 | convolution fusion | flops 8589934592 | bytes 39845888 | tf_op jit(solution)/shard_map/dot_general | solution.py:227
  438.4 24.3 %convolution_convert_fusion.1 = bf16[4096,512]{1,0:T(8,128)(2,1)} fusion(bf16[4096,4096]{1,0:T(8,128)(2,1)} %all-gather.4.cloned.1.call-done, bf16[4096,512]{1,0:T(8,128)(2,1)S(1)} %copy-done.1), kind=kOutput, calls=%fused_computation.8 | convolution fusion | flops 17181966336 | bytes 41943040 | tf_op jit(solution)/shard_map/dot_general | solution.py:227
  463.9 4.4 pack_rows.3
  469.0 1.1 collective-permute-start.5
  471.4 5.4 pack_rows.2
  476.8 2.6 fusion.5
  479.4 1.0 copy-done.4
  480.7 13.9 %collective-permute-done.4.refs_2_ = bf16[2,512,512]{2,1,0:T(8,128)(2,1)} collective-permute-done((bf16[2,512,512]{2,1,0:T(8,128)(2,1)}, bf16[2,512,512]{2,1,0:T(8,128)(2,1)}, u32[]{:S(2)}, u32[]{:S(2)}) %collective-permute-start.4) | collective-permute-done | bytes 1048608 | tf_op jit(solution)/shard_map/ppermute | solution.py:358
  494.6 1.5 collective-permute-start.1
  496.1 20.0 %collective-permute-done.5.refs_3_ = bf16[2,512,512]{2,1,0:T(8,128)(2,1)} collective-permute-done((bf16[2,512,512]{2,1,0:T(8,128)(2,1)}, bf16[2,512,512]{2,1,0:T(8,128)(2,1)}, u32[]{:S(2)}, u32[]{:S(2)}) %collective-permute-start.5) | collective-permute-done | bytes 1048608 | tf_op jit(solution)/shard_map/ppermute | solution.py:358
  516.1 1.7 collective-permute-start.2
  518.3 14.5 %fusion.8 = f32[512,4096]{1,0:T(8,128)} fusion(bf16[2048,512]{1,0:T(8,128)(2,1)S(1)} %bitcast.50, bf16[2048,4096]{1,0:T(8,128)(2,1)} %all-gather.6.cloned.1.call-done), kind=kOutput, calls=%fused_computation.34 | convolution fusion | flops 8589934592 | bytes 27262976 | tf_op jit(solution)/shard_map/dot_general | solution.py:227
  532.8 15.0 %mix_mm.2 = bf16[512,4096]{1,0:T(8,128)(2,1)} custom-call(bf16[2,512,512]{2,1,0:T(8,128)(2,1)} %get-tuple-element.93.refs_0_, bf16[2,512,512]{2,1,0:T(8,128)(2,1)} %copy-done.4, bf16[2,512,512]{2,1,0:T(8,128)(2,1)} %collective-permute-done.4.refs_2_, bf16[2,512,512]{2,1,0:T(8,128)(2,1)} %collective-permute-done.5.refs_3_, bf16[512,4096]{1,0:T(8,128)(2,1)} %refs_4_.3, ...), custom_call_target="tpu_custom_call" | custom-call | flops 8589934592 | bytes 25165824 | tf_op jit(solution)/shard_map/mix_mm/pallas_call | solution.py:301
  547.9 15.1 %collective-permute-done.2.refs_3_ = bf16[2,512,768]{2,1,0:T(8,128)(2,1)} collective-permute-done((bf16[2,512,768]{2,1,0:T(8,128)(2,1)}, bf16[2,512,768]{2,1,0:T(8,128)(2,1)}, u32[]{:S(2)}, u32[]{:S(2)}) %collective-permute-start.2) | collective-permute-done | bytes 1572896 | tf_op jit(solution)/shard_map/ppermute | solution.py:358
  563.6 17.2 %add_convert_fusion = bf16[512,4096]{1,0:T(8,128)(2,1)} fusion(f32[512,4096]{1,0:T(8,128)} %fusion.8, bf16[2048,512]{1,0:T(8,128)(2,1)S(1)} %bitcast.49, bf16[2048,4096]{1,0:T(8,128)(2,1)} %all-gather.8.cloned.1.call-done), kind=kOutput, calls=%fused_computation.5 | convolution fusion | flops 8594128896 | bytes 31457280 | tf_op jit(solution)/shard_map/dot_general | solution.py:227
  580.9 21.7 %grad_mm.3 = (bf16[256,4096]{1,0:T(8,128)(2,1)}, bf16[256,4096]{1,0:T(8,128)(2,1)}) custom-call(s32[4]{0:T(128)} %pad_add_fusion.owner_ref, bf16[2,512,768]{2,1,0:T(8,128)(2,1)} %get-tuple-element.106.refs_0_, bf16[2,512,768]{2,1,0:T(8,128)(2,1)} %copy-done.3, bf16[2,512,768]{2,1,0:T(8,128)(2,1)} %collective-permute-done.1.refs_2_, ...), custom_call_target="tpu_custom_call" | custom-call | flops 12884901888 | bytes 33554432 | tf_op jit(solution)/shard_map/grad_mm/pallas_call | solution.py:265
  602.6 0.7 collective-permute-start.13
  603.3 1.3 collective-permute-start.14
  604.6 4.5 fusion.4
  609.1 22.9 %grad_mm.2.own_ref = f32[512,4096]{1,0:T(8,128)} custom-call(s32[4]{0:T(128)} %pad_add_fusion.owner_ref, bf16[2,512,768]{2,1,0:T(8,128)(2,1)} %get-tuple-element.106.refs_0_, bf16[2,512,768]{2,1,0:T(8,128)(2,1)} %copy-done.3, bf16[2,512,768]{2,1,0:T(8,128)(2,1)} %collective-permute-done.1.refs_2_, bf16[2,512,768]{2,1,0:T(8,128)(2,1)} %collective-permute-done.2.refs_3_, ...), custom_call_target="tpu_custom_call" | custom-call | flops 12884901888 | bytes 33554432 | tf_op jit(solution)/shard_map/grad_mm/pallas_call | solution.py:265
  632.0 24.6 %collective-permute-done.10.refs_9_ = bf16[512,4096]{1,0:T(8,128)(2,1)} collective-permute-done((bf16[512,4096]{1,0:T(8,128)(2,1)}, bf16[512,4096]{1,0:T(8,128)(2,1)}, u32[]{:S(2)}, u32[]{:S(2)}) %collective-permute-start.10) | collective-permute-done | bytes 4194336 | tf_op jit(solution)/shard_map/ppermute | solution.py:358
  656.7 16.8 %mix_mm.3 = bf16[512,4096]{1,0:T(8,128)(2,1)} custom-call(bf16[2,512,512]{2,1,0:T(8,128)(2,1)} %get-tuple-element.93.refs_0_, bf16[2,512,512]{2,1,0:T(8,128)(2,1)} %copy-done.4, bf16[2,512,512]{2,1,0:T(8,128)(2,1)} %collective-permute-done.4.refs_2_, bf16[2,512,512]{2,1,0:T(8,128)(2,1)} %collective-permute-done.5.refs_3_, bf16[512,4096]{1,0:T(8,128)(2,1)} %refs_4_.3, ...), custom_call_target="tpu_custom_call" | custom-call | flops 8589934592 | bytes 25165824 | tf_op jit(solution)/shard_map/mix_mm/pallas_call | solution.py:301
  673.5 7.8 %shard_map.137 = (bf16[512,4096]{1,0:T(8,128)(2,1)}, f32[1,4096]{1,0:T(1,128)}) custom-call(f32[512,4096]{1,0:T(8,128)} %grad_mm.2.own_ref, bf16[256,4096]{1,0:T(8,128)(2,1)} %collective-permute-done.13.got_ref, bf16[512,4096]{1,0:T(8,128)(2,1)} %x_ref.3, bf16[512,4096]{1,0:T(8,128)(2,1)} %dy_ref.3, f32[1,4096]{1,0:T(1,128)} %bitcast.51), custom_call_target="tpu_custom_call" | custom-call | flops 20971520 | bytes 12582912 | tf_op jit(solution)/shard_map/pallas_call | solution.py:345
  681.3 14.5 %collective-permute-done.14.got_ref = bf16[256,4096]{1,0:T(8,128)(2,1)S(1)} collective-permute-done((bf16[256,4096]{1,0:T(8,128)(2,1)}, bf16[256,4096]{1,0:T(8,128)(2,1)S(1)}, u32[]{:S(2)}, u32[]{:S(2)}) %collective-permute-start.14) | collective-permute-done | bytes 2097184 | tf_op jit(solution)/shard_map/ppermute | solution.py:358
  695.8 1.3 copy-done.2
  697.1 7.9 %shard_map.138 = (bf16[512,4096]{1,0:T(8,128)(2,1)}, f32[1,4096]{1,0:T(1,128)}) custom-call(f32[512,4096]{1,0:T(8,128)} %grad_mm.2.own_ref, bf16[256,4096]{1,0:T(8,128)(2,1)} %copy-done.2, bf16[512,4096]{1,0:T(8,128)(2,1)} %x_ref.3, bf16[512,4096]{1,0:T(8,128)(2,1)} %dy_ref.3, f32[1,4096]{1,0:T(1,128)} %bitcast.52, ...), custom_call_target="tpu_custom_call", output_to_operand_aliasing={{0}: (5, {})} | custom-call | flops 20971520 | bytes 12582912 | tf_op jit(solution)/shard_map/pallas_call | solution.py:345
  705.2 1.1 collective-permute-done.15
  707.1 0.9 collective-permute-start.16
  707.9 2.9 collective-permute-done.16
  710.8 1.5 collective-permute-start.17
  712.3 2.3 collective-permute-done.17
  (51 shorter events, 8.4 us)
Async XLA Ops:
  7.2 167.7 %all-gather.4.cloned.1.call-start = ((), (), s32[]{:S(2)}) async-start(), calls=%async_computation | async-start | bytes 37748736 | tf_op jit(solution)/shard_map/all_gather | solution.py:408
  7.2 3.5 copy-start
  15.0 5.0 copy-start.6
  15.1 257.9 %all-gather.6.cloned.1.call-start = ((), (), s32[]{:S(2)}) async-start(), calls=%async_computation.1 | async-start | bytes 18874368 | tf_op jit(solution)/shard_map/all_gather | solution.py:413
  19.9 331.9 %all-gather.8.cloned.1.call-start = ((), (), s32[]{:S(2)}) async-start(), calls=%async_computation.2 | async-start | bytes 18874368 | tf_op jit(solution)/shard_map/all_gather | solution.py:423
  20.1 187.7 %copy-start.5 = (s32[4096]{0:T(1024)}, s32[4096]{0:T(1024)S(1)}, u32[]{:S(2)}) copy-start(s32[4096]{0:T(1024)S(1)} %get-tuple-element.76) | copy-start | bytes 49156
  366.4 96.3 %collective-permute-start.7 = (bf16[4096,512]{1,0:T(8,128)(2,1)}, bf16[4096,512]{1,0:T(8,128)(2,1)}, u32[]{:S(2)}, u32[]{:S(2)}) collective-permute-start(bf16[4096,512]{1,0:T(8,128)(2,1)} %refs_4_.2), channel_id=1, source_target_pairs={{0,4},{1,5},{2,6},{3,7},{4,0},{5,1},{6,2},{7,3},{8,12},{9,13},{10,... | collective-permute-start | bytes 12582920 | tf_op jit(solution)/shard_map/ppermute | solution.py:358
  367.1 95.6 %collective-permute-start.6 = (bf16[512,4096]{1,0:T(8,128)(2,1)}, bf16[512,4096]{1,0:T(8,128)(2,1)}, u32[]{:S(2)}, u32[]{:S(2)}) collective-permute-start(bf16[512,4096]{1,0:T(8,128)(2,1)} %refs_4_.3), channel_id=1, source_target_pairs={{0,2},{1,3},{2,0},{3,1},{4,6},{5,7},{6,4},{7,5},{8,10},{9,11},{10,... | collective-permute-start | bytes 12582920 | tf_op jit(solution)/shard_map/ppermute | solution.py:358
  420.6 17.8 %copy-start.1 = (bf16[4096,512]{1,0:T(8,128)(2,1)S(1)}, bf16[4096,512]{1,0:T(8,128)(2,1)}, u32[]{:S(2)}) copy-start(bf16[4096,512]{1,0:T(8,128)(2,1)} %get-tuple-element.86) | copy-start | bytes 12582916
  462.7 55.1 %collective-permute-start.8 = (bf16[512,4096]{1,0:T(8,128)(2,1)}, bf16[512,4096]{1,0:T(8,128)(2,1)}, u32[]{:S(2)}, u32[]{:S(2)}) collective-permute-start(bf16[512,4096]{1,0:T(8,128)(2,1)} %refs_4_.3), channel_id=1, source_target_pairs={{0,1},{1,0},{2,3},{3,2},{4,5},{5,4},{6,7},{7,6},{8,9},{9,8},{10,11... | collective-permute-start | bytes 12582920 | tf_op jit(solution)/shard_map/ppermute | solution.py:358
  462.8 55.0 %collective-permute-start.9 = (bf16[512,4096]{1,0:T(8,128)(2,1)}, bf16[512,4096]{1,0:T(8,128)(2,1)}, u32[]{:S(2)}, u32[]{:S(2)}) collective-permute-start(bf16[512,4096]{1,0:T(8,128)(2,1)} %collective-permute-done.6.refs_6_), channel_id=1, source_target_pairs={{0,1},{1,0},{2,3},{3,2},{4,5},{5,4},{6,7},{7,6},{8,9},{9,8},{10,11... | collective-permute-start | bytes 12582920 | tf_op jit(solution)/shard_map/ppermute | solution.py:358
  468.2 11.2 %collective-permute-start.3 = (bf16[2,512,512]{2,1,0:T(8,128)(2,1)}, bf16[2,512,512]{2,1,0:T(8,128)(2,1)S(1)}, u32[]{:S(2)}, u32[]{:S(2)}) collective-permute-start(bf16[2,512,512]{2,1,0:T(8,128)(2,1)} %get-tuple-element.94), channel_id=1, source_target_pairs={{0,1},{1,0},{2,3},{3,2},{4,5},{5,4},{6,7},{7,6},{8,9},{9,8},{10,11... | collective-permute-start | bytes 3145736 | tf_op jit(solution)/shard_map/ppermute | solution.py:358
  468.3 26.3 %collective-permute-start.4 = (bf16[2,512,512]{2,1,0:T(8,128)(2,1)}, bf16[2,512,512]{2,1,0:T(8,128)(2,1)}, u32[]{:S(2)}, u32[]{:S(2)}) collective-permute-start(bf16[2,512,512]{2,1,0:T(8,128)(2,1)} %get-tuple-element.95), channel_id=1, source_target_pairs={{0,2},{1,3},{2,0},{3,1},{4,6},{5,7},{6,4},{7,5},{8,10},{9,11},{10,... | collective-permute-start | bytes 3145736 | tf_op jit(solution)/shard_map/ppermute | solution.py:358
  469.0 47.1 %collective-permute-start.5 = (bf16[2,512,512]{2,1,0:T(8,128)(2,1)}, bf16[2,512,512]{2,1,0:T(8,128)(2,1)}, u32[]{:S(2)}, u32[]{:S(2)}) collective-permute-start(bf16[2,512,512]{2,1,0:T(8,128)(2,1)} %get-tuple-element.96), channel_id=1, source_target_pairs={{0,3},{1,2},{2,1},{3,0},{4,7},{5,6},{6,5},{7,4},{8,11},{9,10},{10,... | collective-permute-start | bytes 3145736 | tf_op jit(solution)/shard_map/ppermute | solution.py:358
  479.4 1.0 copy-start.4
  480.4 67.5 %collective-permute-start = (bf16[2,512,768]{2,1,0:T(8,128)(2,1)}, bf16[2,512,768]{2,1,0:T(8,128)(2,1)S(1)}, u32[]{:S(2)}, u32[]{:S(2)}) collective-permute-start(bf16[2,512,768]{2,1,0:T(8,128)(2,1)} %get-tuple-element.89), channel_id=1, source_target_pairs={{0,1},{1,0},{2,3},{3,2},{4,5},{5,4},{6,7},{7,6},{8,9},{9,8},{10,11... | collective-permute-start | bytes 4718600 | tf_op jit(solution)/shard_map/ppermute | solution.py:358
  494.6 53.3 %collective-permute-start.1 = (bf16[2,512,768]{2,1,0:T(8,128)(2,1)}, bf16[2,512,768]{2,1,0:T(8,128)(2,1)}, u32[]{:S(2)}, u32[]{:S(2)}) collective-permute-start(bf16[2,512,768]{2,1,0:T(8,128)(2,1)} %get-tuple-element.90), channel_id=1, source_target_pairs={{0,4},{1,5},{2,6},{3,7},{4,0},{5,1},{6,2},{7,3},{8,12},{9,13},{10,... | collective-permute-start | bytes 4718600 | tf_op jit(solution)/shard_map/ppermute | solution.py:358
  516.1 47.0 %collective-permute-start.2 = (bf16[2,512,768]{2,1,0:T(8,128)(2,1)}, bf16[2,512,768]{2,1,0:T(8,128)(2,1)}, u32[]{:S(2)}, u32[]{:S(2)}) collective-permute-start(bf16[2,512,768]{2,1,0:T(8,128)(2,1)} %get-tuple-element.91), channel_id=1, source_target_pairs={{0,5},{1,4},{2,7},{3,6},{4,1},{5,0},{6,3},{7,2},{8,13},{9,12},{10,... | collective-permute-start | bytes 4718600 | tf_op jit(solution)/shard_map/ppermute | solution.py:358
  517.8 63.1 %collective-permute-start.11 = (bf16[4096,512]{1,0:T(8,128)(2,1)}, bf16[4096,512]{1,0:T(8,128)(2,1)}, u32[]{:S(2)}, u32[]{:S(2)}) collective-permute-start(bf16[4096,512]{1,0:T(8,128)(2,1)} %refs_4_.2), channel_id=1, source_target_pairs={{0,1},{1,0},{2,3},{3,2},{4,5},{5,4},{6,7},{7,6},{8,9},{9,8},{10,11... | collective-permute-start | bytes 12582920 | tf_op jit(solution)/shard_map/ppermute | solution.py:358
  517.8 63.1 %collective-permute-start.12 = (bf16[4096,512]{1,0:T(8,128)(2,1)}, bf16[4096,512]{1,0:T(8,128)(2,1)}, u32[]{:S(2)}, u32[]{:S(2)}) collective-permute-start(bf16[4096,512]{1,0:T(8,128)(2,1)} %collective-permute-done.7.refs_6_), channel_id=1, source_target_pairs={{0,1},{1,0},{2,3},{3,2},{4,5},{5,4},{6,7},{7,6},{8,9},{9,8},{10,11... | collective-permute-start | bytes 12582920 | tf_op jit(solution)/shard_map/ppermute | solution.py:358
  547.9 33.0 %copy-start.3 = (bf16[2,512,768]{2,1,0:T(8,128)(2,1)}, bf16[2,512,768]{2,1,0:T(8,128)(2,1)S(1)}, u32[]{:S(2)}) copy-start(bf16[2,512,768]{2,1,0:T(8,128)(2,1)S(1)} %collective-permute-done.refs_1_) | copy-start | bytes 4718596
  563.0 93.6 %collective-permute-start.10 = (bf16[512,4096]{1,0:T(8,128)(2,1)}, bf16[512,4096]{1,0:T(8,128)(2,1)}, u32[]{:S(2)}, u32[]{:S(2)}) collective-permute-start(bf16[512,4096]{1,0:T(8,128)(2,1)} %mix_mm.2), channel_id=1, source_target_pairs={{0,4},{1,5},{2,6},{3,7},{4,0},{5,1},{6,2},{7,3},{8,12},{9,13},{10,... | collective-permute-start | bytes 12582920 | tf_op jit(solution)/shard_map/ppermute | solution.py:358
  602.6 70.9 %collective-permute-start.13 = (bf16[256,4096]{1,0:T(8,128)(2,1)}, bf16[256,4096]{1,0:T(8,128)(2,1)}, u32[]{:S(2)}, u32[]{:S(2)}) collective-permute-start(bf16[256,4096]{1,0:T(8,128)(2,1)} %get-tuple-element.113), channel_id=1, source_target_pairs={{0,2},{1,3},{2,0},{3,1},{4,6},{5,7},{6,4},{7,5},{8,10},{9,11},{10,... | collective-permute-start | bytes 6291464 | tf_op jit(solution)/shard_map/ppermute | solution.py:358
  603.3 92.5 %collective-permute-start.14 = (bf16[256,4096]{1,0:T(8,128)(2,1)}, bf16[256,4096]{1,0:T(8,128)(2,1)S(1)}, u32[]{:S(2)}, u32[]{:S(2)}) collective-permute-start(bf16[256,4096]{1,0:T(8,128)(2,1)} %get-tuple-element.119), channel_id=1, source_target_pairs={{0,2},{1,3},{2,0},{3,1},{4,6},{5,7},{6,4},{7,5},{8,10},{9,11},{10,... | collective-permute-start | bytes 6291464 | tf_op jit(solution)/shard_map/ppermute | solution.py:358
  695.8 1.3 copy-start.2
  704.9 1.4 collective-permute-start.15
  707.1 3.7 collective-permute-start.16
  710.8 3.7 collective-permute-start.17
Sparse Core Ops, SparseCore 0:
  15.2 159.6 all-gather.3
  177.3 85.9 all-gather.5
  265.8 85.9 all-gather.7

commit v6 on v5

--- a/solution.py
+++ b/solution.py
@@ -14,6 +14,7 @@
 MASKED = -1e30
 BQ = 256
 BK = 512
+BK_BWD = 256
 VMEM_LIMIT = 60 * 1024 * 1024
 NT = (((1,), (1,)), ((), ()))
 TN = (((0,), (0,)), ((), ()))
@@ -106,7 +107,7 @@
         dq_ref, dk_s, dv_s, k_s, dq_s = refs
     step = pl.program_id(0)
     i = step * parts + half
-    bq, bk = BQ, BK
+    bq, bk = BQ, BK_BWD
 
     @pl.when(step == 0)
     def _():
@@ -414,8 +415,8 @@
 
         cos_t, sin_t = rope_tables(positions)
         doc_start = lax.iota(jnp.int32, seq) - positions
-        lo = doc_start[::BQ] // BK
-        full = (doc_start[BQ - 1::BQ] + BK - 1) // BK
+        lo, lo_bwd = doc_start[::BQ] // BK, doc_start[::BQ] // BK_BWD
+        full, full_bwd = (doc_start[BQ - 1::BQ] + BK - 1) // BK, (doc_start[BQ - 1::BQ] + BK_BWD - 1) // BK_BWD
 
         h_full, cos_t, sin_t, lo, full, doc_start, wqkv = lax.optimization_barrier((h_full, cos_t, sin_t, lo, full, doc_start, wqkv))
         qkv = dot32(h_full, wqkv).astype(BF16)
@@ -427,14 +428,14 @@
         carry = None
         for p in range(parts - 1):
             d_o = dot32(dy_full[p], wo_loc, NT).astype(BF16)
-            carry = attend_backward(p, parts, carry, lo, full, qkv, o, d_o, lse, cos_t, sin_t, doc_start, heads)
+            carry = attend_backward(p, parts, carry, lo_bwd, full_bwd, qkv, o, d_o, lse, cos_t, sin_t, doc_start, heads)
         dy_full[-1], o_sent, wo_own, wq_own = lax.optimization_barrier((dy_full[-1], o, wo_loc, wq_loc))
         wq_near = swap(wq_own, y_bit, tp_size)
         wo_near = swap(wo_own, x_bit, tp_size)
         o_pieces = group_rows([o_sent.reshape(tp_size, rows, width)], me, x_bit, y_bit, tp_size)
 
         d_o = dot32(dy_full[-1], wo_loc, NT).astype(BF16)
-        d_q, d_kv = attend_backward(parts - 1, parts, carry, lo, full, qkv, o, d_o, lse, cos_t, sin_t, doc_start, heads)
+        d_q, d_kv = attend_backward(parts - 1, parts, carry, lo_bwd, full_bwd, qkv, o, d_o, lse, cos_t, sin_t, doc_start, heads)
         dq_pieces = group_rows([d_q.reshape(tp_size, rows, width), d_kv.reshape(tp_size, rows, 2 * HEAD_DIM)], me, y_bit, x_bit, tp_size)
         d_wq = dot32(h_full, d_q, TN).astype(BF16)
         d_wkv = dot32(h_full, d_kv, TN)
@@ -446,13 +447,16 @@
         wo_group = [wo_own, wo_side, wo_near, swap(wo_near, 1, tp_size)]
         o_blocks, d_wkv = lax.optimization_barrier((o_blocks, d_wkv))
         d_wo = dot32(o_blocks[:, 0].reshape(-1, width), dy_full[0], TN)
-        d_wo = (d_wo + sum(dot32(o_blocks[:, p].reshape(-1, width), dy_full[p], TN) for p in range(1, parts))).astype(BF16)
         mix_mate = mix_mm(o_pieces, 1, wo_group, BF16)
         dq_pieces, mix_mate, d_wq, d_wkv = lax.optimization_barrier((dq_pieces, mix_mate, d_wq, d_wkv))
         mix_got = swap(mix_mate, y_bit, tp_size)
         owners = jnp.stack([me ^ bit for bit in (0, 1, y_bit, y_bit | 1)])
         halves = 2
-        dh_mate = grad_mm(owners, dq_pieces, 1, wq_group, wk_all, wv_all, BF16, halves)
+        dh_mate = list(grad_mm(owners, dq_pieces, 1, wq_group, wk_all, wv_all, BF16, halves))
+        o_blocks, dh_mate[0] = lax.optimization_barrier((o_blocks, dh_mate[0]))
+        for p in range(1, parts):
+            d_wo = d_wo + dot32(o_blocks[:, p].reshape(-1, width), dy_full[p], TN)
+        d_wo = d_wo.astype(BF16)
         dh_got = []
         for p in range(halves):
             dh_got.append(swap(dh_mate[p], x_bit, tp_size))

time: 726 us -> 740 us (1.019)
  waiting for transfers between devices: 239 us -> 262 us
    ppermute x15, waiting for transfers between devices: 88.2 us -> 104 us  [swap(): return lax.ppermute(value, 'tp', [(d, d ^ bit) for d in range(tp_size)])]
  transfers between devices with their start and end apart: 21 -> 21, of which waited for: 10 -> 11; matrix products, arithmetic and copies ran while one was open for 22% -> 21% of each run, Pallas kernels for 37% -> 35%
where the time goes in v6:
time: 740 us; the launch traced here: 736 us
  Pallas kernels  267 us (36%)
  waiting for transfers between devices  262 us (35%)
  matrix products  137 us (19%)
  other arithmetic  26.3 us (4%)
  local copies, waits for them, and re-layouts  18.2 us (2%)
  between operations  14.2 us (2%)
  starting transfers between devices  11.2 us (2%)
    dot_general x7, matrix products, dot32(): return lax.dot_general(a, b, dims, preferred_element_type=F32)  137 us
    all_gather x1, waiting for transfers between devices, layer(): h_full = lax.all_gather(hidden, 'tp', axis=0, tiled=True)  136 us
    ppermute x15, waiting for transfers between devices, swap(): return lax.ppermute(value, 'tp', [(d, d ^ bit) for d in range(tp_size)])  104 us
    pallas_call x2, Pallas kernels, attend_backward(): pl.pallas_call(functools.partial(bwd_kernel, heads, half, parts, n_blk),...  102 us
    pallas_call x1, Pallas kernels, attend_forward(): pl.pallas_call(functools.partial(fwd_kernel, heads), out_shape=(jax.Shape...  63.1 us
    pallas_call x2, Pallas kernels, grad_mm(): pl.pallas_call(functools.partial(grad_mm_kernel, width), out_shape=[jax.S...  44.6 us
    pallas_call x2, Pallas kernels, mix_mm(): pl.pallas_call(functools.partial(mix_mm_kernel, width), out_shape=jax.Sha...  32.1 us
    pallas_call x2, Pallas kernels, finish(): pl.pallas_call(functools.partial(finish_kernel, part), out_shape=(jax.Sha...  15.7 us
  transfers between devices with their start and end apart: 21, of which 11 were waited for; matrix products, arithmetic and copies ran while one was open for 21% of the time, Pallas kernels for 35%

profile of v6, /device:TPU:0, one launch (start us, length us, event | category | flops | bytes accessed | tf_op | source)
XLA Modules:
  0.0 736.3 jit_solution(3681489816772627596)
XLA Ops:
  7.2 3.2 fusion
  10.7 4.4 fusion.2
  15.1 4.7 fusion.5
  21.0 1.8 constant_dynamic-slice_fusion
  22.8 7.5 %fusion.3 = (f32[4096,64]{1,0:T(8,128)S(1)}, f32[4096,64]{1,0:T(8,128)S(1)}, f32[4096,64]{1,0:T(8,128)S(1)}) fusion(f32[64]{0:T(128)S(1)} %negate_power_fusion, f32[4096]{0:T(1024)S(1)} %get-tuple-element.140), kind=kLoop, calls=%fused_computation.15 | loop fusion | flops 524288 | bytes 3162368 | tf_op jit(solution)/shard_map/neg | solution.py:29
  30.3 3.2 pad_maximum_fusion.1
  33.4 5.5 pad_maximum_fusion
  38.9 136.0 %all-gather.4.cloned.1.call-done = bf16[4096,4096]{1,0:T(8,128)(2,1)} async-done(((bf16[512,4096]{1,0:T(8,128)(2,1)}), bf16[4096,4096]{1,0:T(8,128)(2,1)}) %all-gather.4.cloned.1.call-update) | async-done | bytes 33554448 | tf_op jit(solution)/shard_map/all_gather | solution.py:409
  174.9 32.9 %convolution_convert_fusion.q_ref.k_ref.v_ref = bf16[4096,768]{1,0:T(8,128)(2,1)} fusion(bf16[4096,4096]{1,0:T(8,128)(2,1)} %all-gather.4.cloned.1.call-done, bf16[4096,768]{1,0:T(8,128)(2,1)} %pad_maximum_fusion), kind=kOutput, calls=%fused_computation.6 | convolution fusion | flops 25772949504 | bytes 46137344 | tf_op jit(solution)/shard_map/dot_general | solution.py:228
  207.9 2.0 copy.17.ds_ref
  209.8 63.1 %attend_fwd.1 = (bf16[4096,512]{1,0:T(8,128)(2,1)}, f32[16,1,1024]{2,1,0:T(1,128)}) custom-call(s32[16]{0:T(128)} %get-tuple-element.74.lo_ref, s32[16]{0:T(128)} %get-tuple-element.75.full_ref, bf16[4096,768]{1,0:T(8,128)(2,1)} %convolution_convert_fusion.q_ref.k_ref.v_ref, bf16[4096,768]{1,0:T(8,128)(2,1)} %convolution_convert_fusion.q_ref.k_ref.v_ref, ...), custom_call_target="tpu_custom_call" | custom-call | flops 17179869184 | bytes 16777216 | tf_op jit(solution)/shard_map/attend_fwd/pallas_call | solution.py:171
  272.9 15.4 %convolution_convert_fusion.2.do_ref = bf16[2048,512]{1,0:T(8,128)(2,1)} fusion(bf16[2048,4096]{1,0:T(8,128)(2,1)} %all-gather.6.cloned.1.call-done, bf16[512,4096]{1,0:T(8,128)(2,1)} %refs_4_.3), kind=kOutput, calls=%fused_computation.11 | convolution fusion | flops 8590983168 | bytes 23068672 | tf_op jit(solution)/shard_map/dot_general | solution.py:228
  288.3 48.1 %shard_map.135 = (bf16[4096,512]{1,0:T(8,128)(2,1)}, f32[4096,128]{1,0:T(8,128)}, f32[4096,128]{1,0:T(8,128)}) custom-call(s32[16]{0:T(128)} %get-tuple-element.146.lo_ref, s32[16]{0:T(128)} %get-tuple-element.143.full_ref, bf16[4096,768]{1,0:T(8,128)(2,1)} %convolution_convert_fusion.q_ref.k_ref.v_ref, ...), custom_call_target="tpu_custom_call" | custom-call | flops 21474836480 | bytes 12582912 | tf_op jit(solution)/shard_map/pallas_call | solution.py:212
  336.5 15.3 %all-gather.8.cloned.1.call-done = bf16[2048,4096]{1,0:T(8,128)(2,1)} async-done(((bf16[256,4096]{1,0:T(8,128)(2,1)}), bf16[2048,4096]{1,0:T(8,128)(2,1)}) %all-gather.8.cloned.1.call-update) | async-done | bytes 16777232 | tf_op jit(solution)/shard_map/all_gather | solution.py:424
  351.8 15.0 %convolution_convert_fusion.3.do_ref = bf16[2048,512]{1,0:T(8,128)(2,1)} fusion(bf16[2048,4096]{1,0:T(8,128)(2,1)} %all-gather.8.cloned.1.call-done, bf16[512,4096]{1,0:T(8,128)(2,1)} %refs_4_.3), kind=kOutput, calls=%fused_computation.12 | convolution fusion | flops 8590983168 | bytes 23068672 | tf_op jit(solution)/shard_map/dot_general | solution.py:228
  367.5 1.3 collective-permute-start.6
  368.8 53.7 %shard_map.136 = (bf16[4096,512]{1,0:T(8,128)(2,1)}, bf16[4096,256]{1,0:T(8,128)(2,1)}) custom-call(s32[16]{0:T(128)} %get-tuple-element.146.lo_ref, s32[16]{0:T(128)} %get-tuple-element.143.full_ref, bf16[4096,768]{1,0:T(8,128)(2,1)} %convolution_convert_fusion.q_ref.k_ref.v_ref, ...), custom_call_target="tpu_custom_call", output_to_operand_aliasing={{0}: (13, {})} | custom-call | flops 21474836480 | bytes 12582912 | tf_op jit(solution)/shard_map/pallas_call | solution.py:212
  422.5 18.0 %fusion.7 = f32[4096,256]{1,0:T(8,128)} fusion(bf16[4096,4096]{1,0:T(8,128)(2,1)} %all-gather.4.cloned.1.call-done, bf16[4096,256]{1,0:T(8,128)(2,1)} %get-tuple-element.89), kind=kOutput, calls=%fused_computation.40 | convolution fusion | flops 8589934592 | bytes 39845888 | tf_op jit(solution)/shard_map/dot_general | solution.py:228
  440.5 24.1 %convolution_convert_fusion.1 = bf16[4096,512]{1,0:T(8,128)(2,1)} fusion(bf16[4096,4096]{1,0:T(8,128)(2,1)} %all-gather.4.cloned.1.call-done, bf16[4096,512]{1,0:T(8,128)(2,1)S(1)} %copy-done.1), kind=kOutput, calls=%fused_computation.8 | convolution fusion | flops 17181966336 | bytes 41943040 | tf_op jit(solution)/shard_map/dot_general | solution.py:228
  465.7 4.4 pack_rows.3
  471.1 8.5 %collective-permute-done.3.refs_1_ = bf16[2,512,512]{2,1,0:T(8,128)(2,1)} collective-permute-done((bf16[2,512,512]{2,1,0:T(8,128)(2,1)}, bf16[2,512,512]{2,1,0:T(8,128)(2,1)}, u32[]{:S(2)}, u32[]{:S(2)}) %collective-permute-start.3) | collective-permute-done | bytes 1048608 | tf_op jit(solution)/shard_map/ppermute | solution.py:359
  479.7 16.3 %collective-permute-done.4.refs_2_ = bf16[2,512,512]{2,1,0:T(8,128)(2,1)} collective-permute-done((bf16[2,512,512]{2,1,0:T(8,128)(2,1)}, bf16[2,512,512]{2,1,0:T(8,128)(2,1)}, u32[]{:S(2)}, u32[]{:S(2)}) %collective-permute-start.4) | collective-permute-done | bytes 1048608 | tf_op jit(solution)/shard_map/ppermute | solution.py:359
  497.2 5.4 pack_rows.2
  502.7 1.7 slice.30
  504.4 17.0 %collective-permute-done.5.refs_3_ = bf16[2,512,512]{2,1,0:T(8,128)(2,1)S(1)} collective-permute-done((bf16[2,512,512]{2,1,0:T(8,128)(2,1)}, bf16[2,512,512]{2,1,0:T(8,128)(2,1)S(1)}, u32[]{:S(2)}, u32[]{:S(2)}) %collective-permute-start.5) | collective-permute-done | bytes 1048608 | tf_op jit(solution)/shard_map/ppermute | solution.py:359
  521.5 1.0 copy-done.6
  522.4 1.5 collective-permute-start.1
  523.9 14.8 %fusion.8 = f32[512,4096]{1,0:T(8,128)} fusion(bf16[2048,512]{1,0:T(8,128)(2,1)S(1)} %bitcast.50, bf16[2048,4096]{1,0:T(8,128)(2,1)} %all-gather.6.cloned.1.call-done), kind=kOutput, calls=%fused_computation.41 | convolution fusion | flops 8589934592 | bytes 27262976 | tf_op jit(solution)/shard_map/dot_general | solution.py:228
  538.7 15.0 %mix_mm.2 = bf16[512,4096]{1,0:T(8,128)(2,1)} custom-call(bf16[2,512,512]{2,1,0:T(8,128)(2,1)} %get-tuple-element.95.refs_0_, bf16[2,512,512]{2,1,0:T(8,128)(2,1)} %collective-permute-done.3.refs_1_, bf16[2,512,512]{2,1,0:T(8,128)(2,1)} %collective-permute-done.4.refs_2_, bf16[2,512,512]{2,1,0:T(8,128)(2,1)} %copy-done.6, bf16[512,4096]{1,0:T(8,128)(2,1)} %refs_4_.3, ...), custom_call_target="tpu_custom_call" | custom-call | flops 8589934592 | bytes 25165824 | tf_op jit(solution)/shard_map/mix_mm/pallas_call | solution.py:302
  553.7 6.2 collective-permute-done.1.refs_2_
  559.9 31.7 %collective-permute-done.2.refs_3_ = bf16[2,512,768]{2,1,0:T(8,128)(2,1)} collective-permute-done((bf16[2,512,768]{2,1,0:T(8,128)(2,1)}, bf16[2,512,768]{2,1,0:T(8,128)(2,1)}, u32[]{:S(2)}, u32[]{:S(2)}) %collective-permute-start.2) | collective-permute-done | bytes 1572896 | tf_op jit(solution)/shard_map/ppermute | solution.py:359
  591.6 1.4 collective-permute-start.10
  593.1 21.7 %grad_mm.3 = (bf16[256,4096]{1,0:T(8,128)(2,1)}, bf16[256,4096]{1,0:T(8,128)(2,1)}) custom-call(s32[4]{0:T(128)} %pad_add_fusion.owner_ref, bf16[2,512,768]{2,1,0:T(8,128)(2,1)} %get-tuple-element.108.refs_0_, bf16[2,512,768]{2,1,0:T(8,128)(2,1)} %copy-done.4, bf16[2,512,768]{2,1,0:T(8,128)(2,1)} %copy-done.5, ...), custom_call_target="tpu_custom_call" | custom-call | flops 12884901888 | bytes 33554432 | tf_op jit(solution)/shard_map/grad_mm/pallas_call | solution.py:266
  614.7 1.7 slice.31
  616.5 1.3 collective-permute-start.13
  618.5 17.1 %add_convert_fusion = bf16[512,4096]{1,0:T(8,128)(2,1)} fusion(f32[512,4096]{1,0:T(8,128)} %fusion.8, bf16[2048,512]{1,0:T(8,128)(2,1)S(1)} %bitcast.51, bf16[2048,4096]{1,0:T(8,128)(2,1)} %all-gather.8.cloned.1.call-done), kind=kOutput, calls=%fused_computation.5 | convolution fusion | flops 8594128896 | bytes 31457280 | tf_op jit(solution)/shard_map/dot_general | solution.py:228
  635.7 2.3 fusion.4
  637.9 22.9 %grad_mm.2.own_ref = f32[512,4096]{1,0:T(8,128)} custom-call(s32[4]{0:T(128)} %pad_add_fusion.owner_ref, bf16[2,512,768]{2,1,0:T(8,128)(2,1)} %get-tuple-element.108.refs_0_, bf16[2,512,768]{2,1,0:T(8,128)(2,1)} %copy-done.4, bf16[2,512,768]{2,1,0:T(8,128)(2,1)} %copy-done.5, bf16[2,512,768]{2,1,0:T(8,128)(2,1)} %collective-permute-done.2.refs_3_, ...), custom_call_target="tpu_custom_call" | custom-call | flops 12884901888 | bytes 33554432 | tf_op jit(solution)/shard_map/grad_mm/pallas_call | solution.py:266
  660.9 24.4 %collective-permute-done.10.refs_9_ = bf16[512,4096]{1,0:T(8,128)(2,1)} collective-permute-done((bf16[512,4096]{1,0:T(8,128)(2,1)}, bf16[512,4096]{1,0:T(8,128)(2,1)}, u32[]{:S(2)}, u32[]{:S(2)}) %collective-permute-start.10) | collective-permute-done | bytes 4194336 | tf_op jit(solution)/shard_map/ppermute | solution.py:359
  685.3 17.1 %mix_mm.3 = bf16[512,4096]{1,0:T(8,128)(2,1)} custom-call(bf16[2,512,512]{2,1,0:T(8,128)(2,1)} %get-tuple-element.95.refs_0_, bf16[2,512,512]{2,1,0:T(8,128)(2,1)} %collective-permute-done.3.refs_1_, bf16[2,512,512]{2,1,0:T(8,128)(2,1)} %collective-permute-done.4.refs_2_, bf16[2,512,512]{2,1,0:T(8,128)(2,1)} %copy-done.6, bf16[512,4096]{1,0:T(8,128)(2,1)} %refs_4_.3, ...), custom_call_target="tpu_custom_call" | custom-call | flops 8589934592 | bytes 25165824 | tf_op jit(solution)/shard_map/mix_mm/pallas_call | solution.py:302
  702.3 7.8 %shard_map.137 = (bf16[512,4096]{1,0:T(8,128)(2,1)}, f32[1,4096]{1,0:T(1,128)}) custom-call(f32[512,4096]{1,0:T(8,128)} %grad_mm.2.own_ref, bf16[256,4096]{1,0:T(8,128)(2,1)} %collective-permute-done.13.got_ref, bf16[512,4096]{1,0:T(8,128)(2,1)} %x_ref.3, bf16[512,4096]{1,0:T(8,128)(2,1)} %dy_ref.3, f32[1,4096]{1,0:T(1,128)} %bitcast.52), custom_call_target="tpu_custom_call" | custom-call | flops 20971520 | bytes 12582912 | tf_op jit(solution)/shard_map/pallas_call | solution.py:346
  710.1 1.3 copy-done.3
  711.5 7.8 %shard_map.138 = (bf16[512,4096]{1,0:T(8,128)(2,1)}, f32[1,4096]{1,0:T(1,128)}) custom-call(f32[512,4096]{1,0:T(8,128)} %grad_mm.2.own_ref, bf16[256,4096]{1,0:T(8,128)(2,1)} %copy-done.3, bf16[512,4096]{1,0:T(8,128)(2,1)} %x_ref.3, bf16[512,4096]{1,0:T(8,128)(2,1)} %dy_ref.3, f32[1,4096]{1,0:T(1,128)} %bitcast.53, ...), custom_call_target="tpu_custom_call", output_to_operand_aliasing={{0}: (5, {})} | custom-call | flops 20971520 | bytes 12582912 | tf_op jit(solution)/shard_map/pallas_call | solution.py:346
  719.3 1.4 collective-permute-done.15
  721.4 0.9 collective-permute-start.16
  722.3 2.9 collective-permute-done.16
  725.2 1.5 collective-permute-start.17
  726.6 2.3 collective-permute-done.17
  (56 shorter events, 7.8 us)
Async XLA Ops:
  7.2 167.7 %all-gather.4.cloned.1.call-start = ((), (), s32[]{:S(2)}) async-start(), calls=%async_computation | async-start | bytes 37748736 | tf_op jit(solution)/shard_map/all_gather | solution.py:409
  7.2 3.5 copy-start
  15.0 5.0 copy-start.8
  15.1 257.9 %all-gather.6.cloned.1.call-start = ((), (), s32[]{:S(2)}) async-start(), calls=%async_computation.1 | async-start | bytes 18874368 | tf_op jit(solution)/shard_map/all_gather | solution.py:414
  19.9 331.9 %all-gather.8.cloned.1.call-start = ((), (), s32[]{:S(2)}) async-start(), calls=%async_computation.2 | async-start | bytes 18874368 | tf_op jit(solution)/shard_map/all_gather | solution.py:424
  20.1 187.7 %copy-start.7 = (s32[4096]{0:T(1024)}, s32[4096]{0:T(1024)S(1)}, u32[]{:S(2)}) copy-start(s32[4096]{0:T(1024)S(1)} %get-tuple-element.78) | copy-start | bytes 49156
  366.8 97.8 %collective-permute-start.7 = (bf16[4096,512]{1,0:T(8,128)(2,1)}, bf16[4096,512]{1,0:T(8,128)(2,1)}, u32[]{:S(2)}, u32[]{:S(2)}) collective-permute-start(bf16[4096,512]{1,0:T(8,128)(2,1)} %refs_4_.2), channel_id=1, source_target_pairs={{0,4},{1,5},{2,6},{3,7},{4,0},{5,1},{6,2},{7,3},{8,12},{9,13},{10,... | collective-permute-start | bytes 12582920 | tf_op jit(solution)/shard_map/ppermute | solution.py:359
  367.5 97.1 %collective-permute-start.6 = (bf16[512,4096]{1,0:T(8,128)(2,1)}, bf16[512,4096]{1,0:T(8,128)(2,1)}, u32[]{:S(2)}, u32[]{:S(2)}) collective-permute-start(bf16[512,4096]{1,0:T(8,128)(2,1)} %refs_4_.3), channel_id=1, source_target_pairs={{0,2},{1,3},{2,0},{3,1},{4,6},{5,7},{6,4},{7,5},{8,10},{9,11},{10,... | collective-permute-start | bytes 12582920 | tf_op jit(solution)/shard_map/ppermute | solution.py:359
  422.5 18.0 %copy-start.1 = (bf16[4096,512]{1,0:T(8,128)(2,1)S(1)}, bf16[4096,512]{1,0:T(8,128)(2,1)}, u32[]{:S(2)}) copy-start(bf16[4096,512]{1,0:T(8,128)(2,1)} %get-tuple-element.88) | copy-start | bytes 12582916
  464.6 56.9 %collective-permute-start.8 = (bf16[512,4096]{1,0:T(8,128)(2,1)}, bf16[512,4096]{1,0:T(8,128)(2,1)}, u32[]{:S(2)}, u32[]{:S(2)}) collective-permute-start(bf16[512,4096]{1,0:T(8,128)(2,1)} %refs_4_.3), channel_id=1, source_target_pairs={{0,1},{1,0},{2,3},{3,2},{4,5},{5,4},{6,7},{7,6},{8,9},{9,8},{10,11... | collective-permute-start | bytes 12582920 | tf_op jit(solution)/shard_map/ppermute | solution.py:359
  464.6 59.3 %collective-permute-start.9 = (bf16[512,4096]{1,0:T(8,128)(2,1)}, bf16[512,4096]{1,0:T(8,128)(2,1)}, u32[]{:S(2)}, u32[]{:S(2)}) collective-permute-start(bf16[512,4096]{1,0:T(8,128)(2,1)} %collective-permute-done.6.refs_6_), channel_id=1, source_target_pairs={{0,1},{1,0},{2,3},{3,2},{4,5},{5,4},{6,7},{7,6},{8,9},{9,8},{10,11... | collective-permute-start | bytes 12582920 | tf_op jit(solution)/shard_map/ppermute | solution.py:359
  470.1 9.5 %collective-permute-start.3 = (bf16[2,512,512]{2,1,0:T(8,128)(2,1)}, bf16[2,512,512]{2,1,0:T(8,128)(2,1)}, u32[]{:S(2)}, u32[]{:S(2)}) collective-permute-start(bf16[2,512,512]{2,1,0:T(8,128)(2,1)} %get-tuple-element.96), channel_id=1, source_target_pairs={{0,1},{1,0},{2,3},{3,2},{4,5},{5,4},{6,7},{7,6},{8,9},{9,8},{10,11... | collective-permute-start | bytes 3145736 | tf_op jit(solution)/shard_map/ppermute | solution.py:359
  470.2 25.8 %collective-permute-start.4 = (bf16[2,512,512]{2,1,0:T(8,128)(2,1)}, bf16[2,512,512]{2,1,0:T(8,128)(2,1)}, u32[]{:S(2)}, u32[]{:S(2)}) collective-permute-start(bf16[2,512,512]{2,1,0:T(8,128)(2,1)} %get-tuple-element.97), channel_id=1, source_target_pairs={{0,2},{1,3},{2,0},{3,1},{4,6},{5,7},{6,4},{7,5},{8,10},{9,11},{10,... | collective-permute-start | bytes 3145736 | tf_op jit(solution)/shard_map/ppermute | solution.py:359
  470.9 122.1 %collective-permute-start.11 = (bf16[4096,512]{1,0:T(8,128)(2,1)}, bf16[4096,512]{1,0:T(8,128)(2,1)}, u32[]{:S(2)}, u32[]{:S(2)}) collective-permute-start(bf16[4096,512]{1,0:T(8,128)(2,1)} %refs_4_.2), channel_id=1, source_target_pairs={{0,1},{1,0},{2,3},{3,2},{4,5},{5,4},{6,7},{7,6},{8,9},{9,8},{10,11... | collective-permute-start | bytes 12582920 | tf_op jit(solution)/shard_map/ppermute | solution.py:359
  479.6 113.4 %collective-permute-start.12 = (bf16[4096,512]{1,0:T(8,128)(2,1)}, bf16[4096,512]{1,0:T(8,128)(2,1)}, u32[]{:S(2)}, u32[]{:S(2)}) collective-permute-start(bf16[4096,512]{1,0:T(8,128)(2,1)} %collective-permute-done.7.refs_6_), channel_id=1, source_target_pairs={{0,1},{1,0},{2,3},{3,2},{4,5},{5,4},{6,7},{7,6},{8,9},{9,8},{10,11... | collective-permute-start | bytes 12582920 | tf_op jit(solution)/shard_map/ppermute | solution.py:359
  496.0 25.4 %collective-permute-start.5 = (bf16[2,512,512]{2,1,0:T(8,128)(2,1)}, bf16[2,512,512]{2,1,0:T(8,128)(2,1)S(1)}, u32[]{:S(2)}, u32[]{:S(2)}) collective-permute-start(bf16[2,512,512]{2,1,0:T(8,128)(2,1)} %get-tuple-element.98), channel_id=1, source_target_pairs={{0,3},{1,2},{2,1},{3,0},{4,7},{5,6},{6,5},{7,4},{8,11},{9,10},{10,... | collective-permute-start | bytes 3145736 | tf_op jit(solution)/shard_map/ppermute | solution.py:359
  521.4 1.0 copy-start.6
  521.5 32.2 %collective-permute-start = (bf16[2,512,768]{2,1,0:T(8,128)(2,1)}, bf16[2,512,768]{2,1,0:T(8,128)(2,1)S(1)}, u32[]{:S(2)}, u32[]{:S(2)}) collective-permute-start(bf16[2,512,768]{2,1,0:T(8,128)(2,1)} %get-tuple-element.91), channel_id=1, source_target_pairs={{0,1},{1,0},{2,3},{3,2},{4,5},{5,4},{6,7},{7,6},{8,9},{9,8},{10,11... | collective-permute-start | bytes 4718600 | tf_op jit(solution)/shard_map/ppermute | solution.py:359
  522.4 37.5 %collective-permute-start.1 = (bf16[2,512,768]{2,1,0:T(8,128)(2,1)}, bf16[2,512,768]{2,1,0:T(8,128)(2,1)S(1)}, u32[]{:S(2)}, u32[]{:S(2)}) collective-permute-start(bf16[2,512,768]{2,1,0:T(8,128)(2,1)} %get-tuple-element.92), channel_id=1, source_target_pairs={{0,4},{1,5},{2,6},{3,7},{4,0},{5,1},{6,2},{7,3},{8,12},{9,13},{10,... | collective-permute-start | bytes 4718600 | tf_op jit(solution)/shard_map/ppermute | solution.py:359
  523.9 67.7 %collective-permute-start.2 = (bf16[2,512,768]{2,1,0:T(8,128)(2,1)}, bf16[2,512,768]{2,1,0:T(8,128)(2,1)}, u32[]{:S(2)}, u32[]{:S(2)}) collective-permute-start(bf16[2,512,768]{2,1,0:T(8,128)(2,1)} %get-tuple-element.93), channel_id=1, source_target_pairs={{0,5},{1,4},{2,7},{3,6},{4,1},{5,0},{6,3},{7,2},{8,13},{9,12},{10,... | collective-permute-start | bytes 4718600 | tf_op jit(solution)/shard_map/ppermute | solution.py:359
  553.7 39.3 %copy-start.4 = (bf16[2,512,768]{2,1,0:T(8,128)(2,1)}, bf16[2,512,768]{2,1,0:T(8,128)(2,1)S(1)}, u32[]{:S(2)}) copy-start(bf16[2,512,768]{2,1,0:T(8,128)(2,1)S(1)} %collective-permute-done.refs_1_) | copy-start | bytes 4718596
  559.9 33.1 %copy-start.5 = (bf16[2,512,768]{2,1,0:T(8,128)(2,1)}, bf16[2,512,768]{2,1,0:T(8,128)(2,1)S(1)}, u32[]{:S(2)}) copy-start(bf16[2,512,768]{2,1,0:T(8,128)(2,1)S(1)} %collective-permute-done.1.refs_2_) | copy-start | bytes 4718596
  591.6 93.6 %collective-permute-start.10 = (bf16[512,4096]{1,0:T(8,128)(2,1)}, bf16[512,4096]{1,0:T(8,128)(2,1)}, u32[]{:S(2)}, u32[]{:S(2)}) collective-permute-start(bf16[512,4096]{1,0:T(8,128)(2,1)} %mix_mm.2), channel_id=1, source_target_pairs={{0,4},{1,5},{2,6},{3,7},{4,0},{5,1},{6,2},{7,3},{8,12},{9,13},{10,... | collective-permute-start | bytes 12582920 | tf_op jit(solution)/shard_map/ppermute | solution.py:359
  616.5 85.9 %collective-permute-start.13 = (bf16[256,4096]{1,0:T(8,128)(2,1)}, bf16[256,4096]{1,0:T(8,128)(2,1)}, u32[]{:S(2)}, u32[]{:S(2)}) collective-permute-start(bf16[256,4096]{1,0:T(8,128)(2,1)} %get-tuple-element.117), channel_id=1, source_target_pairs={{0,2},{1,3},{2,0},{3,1},{4,6},{5,7},{6,4},{7,5},{8,10},{9,11},{10,... | collective-permute-start | bytes 6291464 | tf_op jit(solution)/shard_map/ppermute | solution.py:359
  617.7 92.4 %collective-permute-start.14 = (bf16[256,4096]{1,0:T(8,128)(2,1)}, bf16[256,4096]{1,0:T(8,128)(2,1)S(1)}, u32[]{:S(2)}, u32[]{:S(2)}) collective-permute-start(bf16[256,4096]{1,0:T(8,128)(2,1)} %get-tuple-element.123), channel_id=1, source_target_pairs={{0,2},{1,3},{2,0},{3,1},{4,6},{5,7},{6,4},{7,5},{8,10},{9,11},{10,... | collective-permute-start | bytes 6291464 | tf_op jit(solution)/shard_map/ppermute | solution.py:359
  618.5 17.1 %copy-start.2 = (f32[4096,256]{1,0:T(8,128)S(1)}, f32[4096,256]{1,0:T(8,128)}, u32[]{:S(2)}) copy-start(f32[4096,256]{1,0:T(8,128)} %fusion.7) | copy-start | bytes 12582916
  710.1 1.3 copy-start.3
  719.3 1.4 collective-permute-start.15
  721.4 3.7 collective-permute-start.16
  725.2 3.7 collective-permute-start.17
Sparse Core Ops, SparseCore 0:
  15.2 159.6 all-gather.3
  177.3 85.9 all-gather.5
  265.8 85.9 all-gather.7

commit v7 on v6

--- a/solution.py
+++ b/solution.py
@@ -368,7 +368,7 @@
             at += ref.shape[2]
 
 
-def group_rows(blocks, me, pair_bit, mate_bit, tp_size):
+def group_rows(blocks, me, pair_bit, mate_bit, tp_size, gate=None):
     bits = (0, 1, pair_bit, pair_bit | 1)
     owners = jnp.stack([me ^ bit ^ mate for bit in bits for mate in (0, mate_bit)])
     rows = blocks[0].shape[1]
@@ -383,6 +383,8 @@
         cost_estimate=pl.CostEstimate(flops=0, bytes_accessed=32 * rows * span, transcendentals=0),
         name="pack_rows",
     )(owners, *(list(blocks) * 4))
+    if gate is not None:
+        sent = lax.optimization_barrier((*sent, gate))[:4]
     pieces = [sent[0]]
     for bit, rows_sent in zip(bits[1:], sent[1:]):
         pieces.append(swap(rows_sent, bit, tp_size))
@@ -429,31 +431,31 @@
         for p in range(parts - 1):
             d_o = dot32(dy_full[p], wo_loc, NT).astype(BF16)
             carry = attend_backward(p, parts, carry, lo_bwd, full_bwd, qkv, o, d_o, lse, cos_t, sin_t, doc_start, heads)
-        dy_full[-1], o_sent, wo_own, wq_own = lax.optimization_barrier((dy_full[-1], o, wo_loc, wq_loc))
+        o_first, _ = lax.optimization_barrier((o_blocks[:, 0], carry[0]))
+        d_wo = dot32(o_first.reshape(-1, width), dy_full[0], TN)
+        dy_full[-1], d_wo = lax.optimization_barrier((dy_full[-1], d_wo))
+        dy_full[-1], wo_own, wq_own = lax.optimization_barrier((dy_full[-1], wo_loc, wq_loc))
         wq_near = swap(wq_own, y_bit, tp_size)
         wo_near = swap(wo_own, x_bit, tp_size)
-        o_pieces = group_rows([o_sent.reshape(tp_size, rows, width)], me, x_bit, y_bit, tp_size)
+        o_pieces = group_rows([o.reshape(tp_size, rows, width)], me, x_bit, y_bit, tp_size, dy_full[-1])
 
         d_o = dot32(dy_full[-1], wo_loc, NT).astype(BF16)
         d_q, d_kv = attend_backward(parts - 1, parts, carry, lo_bwd, full_bwd, qkv, o, d_o, lse, cos_t, sin_t, doc_start, heads)
         dq_pieces = group_rows([d_q.reshape(tp_size, rows, width), d_kv.reshape(tp_size, rows, 2 * HEAD_DIM)], me, y_bit, x_bit, tp_size)
         d_wq = dot32(h_full, d_q, TN).astype(BF16)
         d_wkv = dot32(h_full, d_kv, TN)
-        wq_near, wq_own, d_wq, d_wkv = lax.optimization_barrier((wq_near, wq_own, d_wq, d_wkv))
+        wq_near, wq_own, wo_near, wo_own, d_wq = lax.optimization_barrier((wq_near, wq_own, wo_near, wo_own, d_wq))
+        wo_side = swap(wo_own, 1, tp_size)
+        wo_group = [wo_own, wo_side, wo_near, swap(wo_near, 1, tp_size)]
         wq_side = swap(wq_own, 1, tp_size)
         wq_group = [wq_own, wq_side, wq_near, swap(wq_near, 1, tp_size)]
-        wo_near, wo_own, d_wkv = lax.optimization_barrier((wo_near, wo_own, d_wkv))
-        wo_side = swap(wo_own, 1, tp_size)
-        wo_group = [wo_own, wo_side, wo_near, swap(wo_near, 1, tp_size)]
-        o_blocks, d_wkv = lax.optimization_barrier((o_blocks, d_wkv))
-        d_wo = dot32(o_blocks[:, 0].reshape(-1, width), dy_full[0], TN)
         mix_mate = mix_mm(o_pieces, 1, wo_group, BF16)
         dq_pieces, mix_mate, d_wq, d_wkv = lax.optimization_barrier((dq_pieces, mix_mate, d_wq, d_wkv))
         mix_got = swap(mix_mate, y_bit, tp_size)
         owners = jnp.stack([me ^ bit for bit in (0, 1, y_bit, y_bit | 1)])
         halves = 2
         dh_mate = list(grad_mm(owners, dq_pieces, 1, wq_group, wk_all, wv_all, BF16, halves))
-        o_blocks, dh_mate[0] = lax.optimization_barrier((o_blocks, dh_mate[0]))
+        o_blocks, d_wkv, dh_mate[0] = lax.optimization_barrier((o_blocks, d_wkv, dh_mate[0]))
         for p in range(1, parts):
             d_wo = d_wo + dot32(o_blocks[:, p].reshape(-1, width), dy_full[p], TN)
         d_wo = d_wo.astype(BF16)
@@ -461,13 +463,13 @@
         for p in range(halves):
             dh_got.append(swap(dh_mate[p], x_bit, tp_size))
         dh_own, = grad_mm(owners, dq_pieces, 0, wq_group, wk_all, wv_all, F32)
-        mix_got, dh_own = lax.optimization_barrier((mix_got, dh_own))
-        result = mix_mm(o_pieces, 0, wo_group, BF16, (x_blk, mix_got))
+        mix_own = mix_mm(o_pieces, 0, wo_group, F32, (x_blk,))
         d_wk, d_wv = d_wkv[:, :HEAD_DIM], d_wkv[:, HEAD_DIM:]
-        dh_own, dh_got[0], result, d_wo, d_wk, d_wv = lax.optimization_barrier((dh_own, dh_got[0], result, d_wo, d_wk, d_wv))
-        done = None
-        for p in range(halves):
-            done = finish(p, halves, done, dh_own, dh_got[p], x_blk, dy_blk, norm_gain)
+        dh_own, dh_got[0], mix_own, d_wo, d_wk, d_wv = lax.optimization_barrier((dh_own, dh_got[0], mix_own, d_wo, d_wk, d_wv))
+        done = finish(0, halves, None, dh_own, dh_got[0], x_blk, dy_blk, norm_gain)
+        result = (mix_own + mix_got.astype(F32)).astype(BF16)
+        result, dh_got[1] = lax.optimization_barrier((result, dh_got[1]))
+        done = finish(1, halves, done, dh_own, dh_got[1], x_blk, dy_blk, norm_gain)
         grad_x, d_gain = done[0], sum_over_tp(done[1][0], tp_size)
         return result, grad_x, d_wq, d_wk, d_wv, d_wo, d_gain
 

time: 740 us -> 745 us (level)
  other arithmetic: 26.3 us -> 34.4 us
    all_gather x1, waiting for transfers between devices: 15.3 us -> 0.01 us  [layer(): lax.all_gather(dy_part, 'tp', axis=0, tiled=True)]
    ppermute x15, waiting for transfers between devices: 104 us -> 114 us  [swap(): return lax.ppermute(value, 'tp', [(d, d ^ bit) for d in range(tp_size)])]
    convert_element_type x0 -> x1, other arithmetic: none -> 8 us  [layer(): result = (mix_own + mix_got.astype(F32)).astype(BF16)]
  transfers between devices with their start and end apart: 21 -> 21, of which waited for: 11 -> 12; matrix products, arithmetic and copies ran while one was open for 21% -> 22% of each run, Pallas kernels for 35% -> 32%
where the time goes in v7:
time: 745 us; the launch traced here: 741 us
  Pallas kernels  267 us (36%)
  waiting for transfers between devices  257 us (34%)
  matrix products  138 us (19%)
  other arithmetic  34.4 us (5%)
  local copies, waits for them, and re-layouts  18.3 us (2%)
  between operations  14.2 us (2%)
  starting transfers between devices  12.6 us (2%)
    dot_general x7, matrix products, dot32(): return lax.dot_general(a, b, dims, preferred_element_type=F32)  138 us
    all_gather x1, waiting for transfers between devices, layer(): h_full = lax.all_gather(hidden, 'tp', axis=0, tiled=True)  136 us
    ppermute x15, waiting for transfers between devices, swap(): return lax.ppermute(value, 'tp', [(d, d ^ bit) for d in range(tp_size)])  114 us
    pallas_call x2, Pallas kernels, attend_backward(): pl.pallas_call(functools.partial(bwd_kernel, heads, half, parts, n_blk),...  102 us
    pallas_call x1, Pallas kernels, attend_forward(): pl.pallas_call(functools.partial(fwd_kernel, heads), out_shape=(jax.Shape...  63.1 us
    pallas_call x2, Pallas kernels, grad_mm(): pl.pallas_call(functools.partial(grad_mm_kernel, width), out_shape=[jax.S...  44.9 us
    pallas_call x2, Pallas kernels, mix_mm(): pl.pallas_call(functools.partial(mix_mm_kernel, width), out_shape=jax.Sha...  31.9 us
    pallas_call x2, Pallas kernels, finish(): pl.pallas_call(functools.partial(finish_kernel, part), out_shape=(jax.Sha...  15.7 us
  transfers between devices with their start and end apart: 21, of which 12 were waited for; matrix products, arithmetic and copies ran while one was open for 22% of the time, Pallas kernels for 32%

profile of v7, /device:TPU:0, one launch (start us, length us, event | category | flops | bytes accessed | tf_op | source)
XLA Modules:
  0.0 741.3 jit_solution(5471467253012309257)
XLA Ops:
  7.2 3.2 fusion
  10.7 4.4 fusion.2
  15.1 4.7 fusion.5
  21.0 1.8 constant_dynamic-slice_fusion
  22.8 7.5 %fusion.3 = (f32[4096,64]{1,0:T(8,128)S(1)}, f32[4096,64]{1,0:T(8,128)S(1)}, f32[4096,64]{1,0:T(8,128)S(1)}) fusion(f32[64]{0:T(128)S(1)} %negate_power_fusion, f32[4096]{0:T(1024)S(1)} %get-tuple-element.146), kind=kLoop, calls=%fused_computation.17 | loop fusion | flops 524288 | bytes 3162368 | tf_op jit(solution)/shard_map/neg | solution.py:29
  30.3 3.2 pad_maximum_fusion.1
  33.4 5.5 pad_maximum_fusion
  38.9 136.0 %all-gather.4.cloned.1.call-done = bf16[4096,4096]{1,0:T(8,128)(2,1)} async-done(((bf16[512,4096]{1,0:T(8,128)(2,1)}), bf16[4096,4096]{1,0:T(8,128)(2,1)}) %all-gather.4.cloned.1.call-update) | async-done | bytes 33554448 | tf_op jit(solution)/shard_map/all_gather | solution.py:411
  174.9 32.9 %convolution_convert_fusion.q_ref.k_ref.v_ref = bf16[4096,768]{1,0:T(8,128)(2,1)} fusion(bf16[4096,4096]{1,0:T(8,128)(2,1)} %all-gather.4.cloned.1.call-done, bf16[4096,768]{1,0:T(8,128)(2,1)} %pad_maximum_fusion), kind=kOutput, calls=%fused_computation.7 | convolution fusion | flops 25772949504 | bytes 46137344 | tf_op jit(solution)/shard_map/dot_general | solution.py:228
  207.8 2.0 copy.17.ds_ref
  209.8 63.1 %attend_fwd.1 = (bf16[4096,512]{1,0:T(8,128)(2,1)}, f32[16,1,1024]{2,1,0:T(1,128)}) custom-call(s32[16]{0:T(128)} %get-tuple-element.77.lo_ref, s32[16]{0:T(128)} %get-tuple-element.78.full_ref, bf16[4096,768]{1,0:T(8,128)(2,1)} %convolution_convert_fusion.q_ref.k_ref.v_ref, bf16[4096,768]{1,0:T(8,128)(2,1)} %convolution_convert_fusion.q_ref.k_ref.v_ref, ...), custom_call_target="tpu_custom_call" | custom-call | flops 17179869184 | bytes 16777216 | tf_op jit(solution)/shard_map/attend_fwd/pallas_call | solution.py:171
  272.9 1.9 slice_bitcast_fusion
  274.8 14.8 %convolution_convert_fusion.3.do_ref = bf16[2048,512]{1,0:T(8,128)(2,1)} fusion(bf16[2048,4096]{1,0:T(8,128)(2,1)} %all-gather.6.cloned.1.call-done, bf16[512,4096]{1,0:T(8,128)(2,1)} %refs_4_.3), kind=kOutput, calls=%fused_computation.13 | convolution fusion | flops 8590983168 | bytes 23068672 | tf_op jit(solution)/shard_map/dot_general | solution.py:228
  289.6 48.1 %shard_map.135 = (bf16[4096,512]{1,0:T(8,128)(2,1)}, f32[4096,128]{1,0:T(8,128)}, f32[4096,128]{1,0:T(8,128)}) custom-call(s32[16]{0:T(128)} %get-tuple-element.152.lo_ref, s32[16]{0:T(128)} %get-tuple-element.149.full_ref, bf16[4096,768]{1,0:T(8,128)(2,1)} %convolution_convert_fusion.q_ref.k_ref.v_ref, ...), custom_call_target="tpu_custom_call" | custom-call | flops 21474836480 | bytes 12582912 | tf_op jit(solution)/shard_map/pallas_call | solution.py:212
  337.7 15.2 %fusion.7 = f32[512,4096]{1,0:T(8,128)} fusion(bf16[2048,512]{1,0:T(8,128)(2,1)S(1)} %bitcast.53, bf16[2048,4096]{1,0:T(8,128)(2,1)} %all-gather.6.cloned.1.call-done), kind=kOutput, calls=%fused_computation.42 | convolution fusion | flops 8589934592 | bytes 27262976 | tf_op jit(solution)/shard_map/dot_general | solution.py:228
  352.9 14.6 %convolution_convert_fusion.2.do_ref = bf16[2048,512]{1,0:T(8,128)(2,1)} fusion(bf16[2048,4096]{1,0:T(8,128)(2,1)} %all-gather.8.cloned.1.call-done, bf16[512,4096]{1,0:T(8,128)(2,1)} %refs_4_.3), kind=kOutput, calls=%fused_computation.12 | convolution fusion | flops 8590983168 | bytes 23068672 | tf_op jit(solution)/shard_map/dot_general | solution.py:228
  368.4 1.7 collective-permute-start.7
  370.1 53.8 %shard_map.136 = (bf16[4096,512]{1,0:T(8,128)(2,1)}, bf16[4096,256]{1,0:T(8,128)(2,1)}) custom-call(s32[16]{0:T(128)} %get-tuple-element.152.lo_ref, s32[16]{0:T(128)} %get-tuple-element.149.full_ref, bf16[4096,768]{1,0:T(8,128)(2,1)} %convolution_convert_fusion.q_ref.k_ref.v_ref, ...), custom_call_target="tpu_custom_call", output_to_operand_aliasing={{0}: (13, {})} | custom-call | flops 21474836480 | bytes 12582912 | tf_op jit(solution)/shard_map/pallas_call | solution.py:212
  423.9 25.1 %convolution_convert_fusion.1 = bf16[4096,512]{1,0:T(8,128)(2,1)} fusion(bf16[4096,4096]{1,0:T(8,128)(2,1)} %all-gather.4.cloned.1.call-done, bf16[4096,512]{1,0:T(8,128)(2,1)} %get-tuple-element.93), kind=kOutput, calls=%fused_computation.9 | convolution fusion | flops 17181966336 | bytes 41943040 | tf_op jit(solution)/shard_map/dot_general | solution.py:228
  449.0 11.3 %collective-permute-done.6.refs_6_ = bf16[4096,512]{1,0:T(8,128)(2,1)} collective-permute-done((bf16[4096,512]{1,0:T(8,128)(2,1)}, bf16[4096,512]{1,0:T(8,128)(2,1)}, u32[]{:S(2)}, u32[]{:S(2)}) %collective-permute-start.6) | collective-permute-done | bytes 4194336 | tf_op jit(solution)/shard_map/ppermute | solution.py:359
  462.2 4.4 pack_rows.3
  466.5 1.6 collective-permute-start.4
  468.3 7.8 %collective-permute-done.3.refs_1_ = bf16[2,512,512]{2,1,0:T(8,128)(2,1)} collective-permute-done((bf16[2,512,512]{2,1,0:T(8,128)(2,1)}, bf16[2,512,512]{2,1,0:T(8,128)(2,1)}, u32[]{:S(2)}, u32[]{:S(2)}) %collective-permute-start.3) | collective-permute-done | bytes 1048608 | tf_op jit(solution)/shard_map/ppermute | solution.py:359
  476.2 16.2 %collective-permute-done.4.refs_2_ = bf16[2,512,512]{2,1,0:T(8,128)(2,1)} collective-permute-done((bf16[2,512,512]{2,1,0:T(8,128)(2,1)}, bf16[2,512,512]{2,1,0:T(8,128)(2,1)}, u32[]{:S(2)}, u32[]{:S(2)}) %collective-permute-start.4) | collective-permute-done | bytes 1048608 | tf_op jit(solution)/shard_map/ppermute | solution.py:359
  494.4 5.6 pack_rows.2
  500.0 18.0 %collective-permute-done.5.refs_3_ = bf16[2,512,512]{2,1,0:T(8,128)(2,1)S(1)} collective-permute-done((bf16[2,512,512]{2,1,0:T(8,128)(2,1)}, bf16[2,512,512]{2,1,0:T(8,128)(2,1)S(1)}, u32[]{:S(2)}, u32[]{:S(2)}) %collective-permute-start.5) | collective-permute-done | bytes 1048608 | tf_op jit(solution)/shard_map/ppermute | solution.py:359
  519.1 1.0 collective-permute-start.1
  520.9 17.9 %fusion.8 = f32[4096,256]{1,0:T(8,128)} fusion(bf16[4096,4096]{1,0:T(8,128)(2,1)} %all-gather.4.cloned.1.call-done, bf16[4096,256]{1,0:T(8,128)(2,1)S(1)} %copy-done.1), kind=kOutput, calls=%fused_computation.43 | convolution fusion | flops 8589934592 | bytes 39845888 | tf_op jit(solution)/shard_map/dot_general | solution.py:228
  538.7 15.0 %mix_mm.2 = bf16[512,4096]{1,0:T(8,128)(2,1)} custom-call(bf16[2,512,512]{2,1,0:T(8,128)(2,1)} %get-tuple-element.103.refs_0_, bf16[2,512,512]{2,1,0:T(8,128)(2,1)} %collective-permute-done.3.refs_1_, bf16[2,512,512]{2,1,0:T(8,128)(2,1)} %collective-permute-done.4.refs_2_, bf16[2,512,512]{2,1,0:T(8,128)(2,1)} %copy-done.5, bf16[512,4096]{1,0:T(8,128)(2,1)} %refs_4_.3, ...), custom_call_target="tpu_custom_call" | custom-call | flops 8589934592 | bytes 25165824 | tf_op jit(solution)/shard_map/mix_mm/pallas_call | solution.py:302
  553.8 2.9 collective-permute-done.1.refs_2_
  556.7 32.6 %collective-permute-done.2.refs_3_ = bf16[2,512,768]{2,1,0:T(8,128)(2,1)} collective-permute-done((bf16[2,512,768]{2,1,0:T(8,128)(2,1)}, bf16[2,512,768]{2,1,0:T(8,128)(2,1)}, u32[]{:S(2)}, u32[]{:S(2)}) %collective-permute-start.2) | collective-permute-done | bytes 1572896 | tf_op jit(solution)/shard_map/ppermute | solution.py:359
  589.3 21.7 %grad_mm.3 = (bf16[256,4096]{1,0:T(8,128)(2,1)}, bf16[256,4096]{1,0:T(8,128)(2,1)}) custom-call(s32[4]{0:T(128)} %pad_add_fusion.owner_ref, bf16[2,512,768]{2,1,0:T(8,128)(2,1)} %get-tuple-element.112.refs_0_, bf16[2,512,768]{2,1,0:T(8,128)(2,1)} %copy-done.4, bf16[2,512,768]{2,1,0:T(8,128)(2,1)} %collective-permute-done.1.refs_2_, ...), custom_call_target="tpu_custom_call" | custom-call | flops 12884901888 | bytes 33554432 | tf_op jit(solution)/shard_map/grad_mm/pallas_call | solution.py:266
  611.0 1.7 slice.31
  612.7 1.6 collective-permute-start.12
  614.3 1.1 collective-permute-start.13
  615.8 17.1 %add_convert_fusion.1 = bf16[512,4096]{1,0:T(8,128)(2,1)} fusion(f32[512,4096]{1,0:T(8,128)} %fusion.7, bf16[2048,512]{1,0:T(8,128)(2,1)S(1)} %bitcast.52, bf16[2048,4096]{1,0:T(8,128)(2,1)} %all-gather.8.cloned.1.call-done), kind=kOutput, calls=%fused_computation.6 | convolution fusion | flops 8594128896 | bytes 31457280 | tf_op jit(solution)/shard_map/dot_general | solution.py:228
  632.9 2.3 fusion.4
  635.2 23.2 %grad_mm.2.own_ref = f32[512,4096]{1,0:T(8,128)} custom-call(s32[4]{0:T(128)} %pad_add_fusion.owner_ref, bf16[2,512,768]{2,1,0:T(8,128)(2,1)} %get-tuple-element.112.refs_0_, bf16[2,512,768]{2,1,0:T(8,128)(2,1)} %copy-done.4, bf16[2,512,768]{2,1,0:T(8,128)(2,1)} %collective-permute-done.1.refs_2_, bf16[2,512,768]{2,1,0:T(8,128)(2,1)} %collective-permute-done.2.refs_3_, ...), custom_call_target="tpu_custom_call" | custom-call | flops 12884901888 | bytes 33554432 | tf_op jit(solution)/shard_map/grad_mm/pallas_call | solution.py:266
  658.4 16.9 %mix_mm.3 = f32[512,4096]{1,0:T(8,128)} custom-call(bf16[2,512,512]{2,1,0:T(8,128)(2,1)} %get-tuple-element.103.refs_0_, bf16[2,512,512]{2,1,0:T(8,128)(2,1)} %collective-permute-done.3.refs_1_, bf16[2,512,512]{2,1,0:T(8,128)(2,1)} %collective-permute-done.4.refs_2_, bf16[2,512,512]{2,1,0:T(8,128)(2,1)} %copy-done.5, bf16[512,4096]{1,0:T(8,128)(2,1)} %refs_4_.3, ...), custom_call_target="tpu_custom_call" | custom-call | flops 8589934592 | bytes 25165824 | tf_op jit(solution)/shard_map/mix_mm/pallas_call | solution.py:302
  675.2 7.8 %shard_map.137 = (bf16[512,4096]{1,0:T(8,128)(2,1)}, f32[1,4096]{1,0:T(1,128)}) custom-call(f32[512,4096]{1,0:T(8,128)} %grad_mm.2.own_ref, bf16[256,4096]{1,0:T(8,128)(2,1)} %collective-permute-done.12.got_ref, bf16[512,4096]{1,0:T(8,128)(2,1)} %x_ref.3, bf16[512,4096]{1,0:T(8,128)(2,1)} %dy_ref.3, f32[1,4096]{1,0:T(1,128)} %bitcast.54), custom_call_target="tpu_custom_call" | custom-call | flops 20971520 | bytes 12582912 | tf_op jit(solution)/shard_map/pallas_call | solution.py:346
  683.1 24.0 %collective-permute-done.13 = bf16[512,4096]{1,0:T(8,128)(2,1)} collective-permute-done((bf16[512,4096]{1,0:T(8,128)(2,1)}, bf16[512,4096]{1,0:T(8,128)(2,1)}, u32[]{:S(2)}, u32[]{:S(2)}) %collective-permute-start.13) | collective-permute-done | bytes 4194336 | tf_op jit(solution)/shard_map/ppermute | solution.py:359
  707.1 8.0 %add_convert_fusion = bf16[512,4096]{1,0:T(8,128)(2,1)} fusion(f32[512,4096]{1,0:T(8,128)} %mix_mm.3, bf16[512,4096]{1,0:T(8,128)(2,1)} %collective-permute-done.13), kind=kLoop, calls=%fused_computation.5 | loop fusion | flops 6291456 | bytes 16777216 | tf_op jit(solution)/shard_map/convert_element_type | solution.py:470
  715.1 1.3 copy-done.3
  716.4 7.9 %shard_map.138 = (bf16[512,4096]{1,0:T(8,128)(2,1)}, f32[1,4096]{1,0:T(1,128)}) custom-call(f32[512,4096]{1,0:T(8,128)} %grad_mm.2.own_ref, bf16[256,4096]{1,0:T(8,128)(2,1)} %copy-done.3, bf16[512,4096]{1,0:T(8,128)(2,1)} %x_ref.3, bf16[512,4096]{1,0:T(8,128)(2,1)} %dy_ref.3, f32[1,4096]{1,0:T(1,128)} %bitcast.55, ...), custom_call_target="tpu_custom_call", output_to_operand_aliasing={{0}: (5, {})} | custom-call | flops 20971520 | bytes 12582912 | tf_op jit(solution)/shard_map/pallas_call | solution.py:346
  724.3 1.4 collective-permute-done.15
  727.0 3.1 collective-permute-done.16
  730.1 1.1 collective-permute-start.17
  731.2 2.7 collective-permute-done.17
  (55 shorter events, 10.6 us)
Async XLA Ops:
  7.2 167.7 %all-gather.4.cloned.1.call-start = ((), (), s32[]{:S(2)}) async-start(), calls=%async_computation | async-start | bytes 37748736 | tf_op jit(solution)/shard_map/all_gather | solution.py:411
  7.2 3.5 copy-start
  15.0 5.0 copy-start.7
  15.1 257.8 %all-gather.6.cloned.1.call-start = ((), (), s32[]{:S(2)}) async-start(), calls=%async_computation.1 | async-start | bytes 18874368 | tf_op jit(solution)/shard_map/all_gather | solution.py:416
  19.9 333.0 %all-gather.8.cloned.1.call-start = ((), (), s32[]{:S(2)}) async-start(), calls=%async_computation.2 | async-start | bytes 18874368 | tf_op jit(solution)/shard_map/all_gather | solution.py:426
  20.1 187.7 %copy-start.6 = (s32[4096]{0:T(1024)}, s32[4096]{0:T(1024)S(1)}, u32[]{:S(2)}) copy-start(s32[4096]{0:T(1024)S(1)} %get-tuple-element.81) | copy-start | bytes 49156
  367.5 92.9 %collective-permute-start.6 = (bf16[4096,512]{1,0:T(8,128)(2,1)}, bf16[4096,512]{1,0:T(8,128)(2,1)}, u32[]{:S(2)}, u32[]{:S(2)}) collective-permute-start(bf16[4096,512]{1,0:T(8,128)(2,1)} %refs_4_.2), channel_id=1, source_target_pairs={{0,4},{1,5},{2,6},{3,7},{4,0},{5,1},{6,2},{7,3},{8,12},{9,13},{10,... | collective-permute-start | bytes 12582920 | tf_op jit(solution)/shard_map/ppermute | solution.py:359
  368.4 92.7 %collective-permute-start.7 = (bf16[512,4096]{1,0:T(8,128)(2,1)}, bf16[512,4096]{1,0:T(8,128)(2,1)}, u32[]{:S(2)}, u32[]{:S(2)}) collective-permute-start(bf16[512,4096]{1,0:T(8,128)(2,1)} %refs_4_.3), channel_id=1, source_target_pairs={{0,2},{1,3},{2,0},{3,1},{4,6},{5,7},{6,4},{7,5},{8,10},{9,11},{10,... | collective-permute-start | bytes 12582920 | tf_op jit(solution)/shard_map/ppermute | solution.py:359
  461.1 58.0 %collective-permute-start.8 = (bf16[512,4096]{1,0:T(8,128)(2,1)}, bf16[512,4096]{1,0:T(8,128)(2,1)}, u32[]{:S(2)}, u32[]{:S(2)}) collective-permute-start(bf16[512,4096]{1,0:T(8,128)(2,1)} %refs_4_.3), channel_id=1, source_target_pairs={{0,1},{1,0},{2,3},{3,2},{4,5},{5,4},{6,7},{7,6},{8,9},{9,8},{10,11... | collective-permute-start | bytes 12582920 | tf_op jit(solution)/shard_map/ppermute | solution.py:359
  461.1 59.0 %collective-permute-start.9 = (bf16[512,4096]{1,0:T(8,128)(2,1)}, bf16[512,4096]{1,0:T(8,128)(2,1)}, u32[]{:S(2)}, u32[]{:S(2)}) collective-permute-start(bf16[512,4096]{1,0:T(8,128)(2,1)} %collective-permute-done.7.refs_6_), channel_id=1, source_target_pairs={{0,1},{1,0},{2,3},{3,2},{4,5},{5,4},{6,7},{7,6},{8,9},{9,8},{10,11... | collective-permute-start | bytes 12582920 | tf_op jit(solution)/shard_map/ppermute | solution.py:359
  466.5 9.5 %collective-permute-start.3 = (bf16[2,512,512]{2,1,0:T(8,128)(2,1)}, bf16[2,512,512]{2,1,0:T(8,128)(2,1)}, u32[]{:S(2)}, u32[]{:S(2)}) collective-permute-start(bf16[2,512,512]{2,1,0:T(8,128)(2,1)} %get-tuple-element.104), channel_id=1, source_target_pairs={{0,1},{1,0},{2,3},{3,2},{4,5},{5,4},{6,7},{7,6},{8,9},{9,8},{10,11... | collective-permute-start | bytes 3145736 | tf_op jit(solution)/shard_map/ppermute | solution.py:359
  466.5 25.9 %collective-permute-start.4 = (bf16[2,512,512]{2,1,0:T(8,128)(2,1)}, bf16[2,512,512]{2,1,0:T(8,128)(2,1)}, u32[]{:S(2)}, u32[]{:S(2)}) collective-permute-start(bf16[2,512,512]{2,1,0:T(8,128)(2,1)} %get-tuple-element.105), channel_id=1, source_target_pairs={{0,2},{1,3},{2,0},{3,1},{4,6},{5,7},{6,4},{7,5},{8,10},{9,11},{10,... | collective-permute-start | bytes 3145736 | tf_op jit(solution)/shard_map/ppermute | solution.py:359
  468.1 121.2 %collective-permute-start.10 = (bf16[4096,512]{1,0:T(8,128)(2,1)}, bf16[4096,512]{1,0:T(8,128)(2,1)}, u32[]{:S(2)}, u32[]{:S(2)}) collective-permute-start(bf16[4096,512]{1,0:T(8,128)(2,1)} %refs_4_.2), channel_id=1, source_target_pairs={{0,1},{1,0},{2,3},{3,2},{4,5},{5,4},{6,7},{7,6},{8,9},{9,8},{10,11... | collective-permute-start | bytes 12582920 | tf_op jit(solution)/shard_map/ppermute | solution.py:359
  476.1 113.2 %collective-permute-start.11 = (bf16[4096,512]{1,0:T(8,128)(2,1)}, bf16[4096,512]{1,0:T(8,128)(2,1)}, u32[]{:S(2)}, u32[]{:S(2)}) collective-permute-start(bf16[4096,512]{1,0:T(8,128)(2,1)} %collective-permute-done.6.refs_6_), channel_id=1, source_target_pairs={{0,1},{1,0},{2,3},{3,2},{4,5},{5,4},{6,7},{7,6},{8,9},{9,8},{10,11... | collective-permute-start | bytes 12582920 | tf_op jit(solution)/shard_map/ppermute | solution.py:359
  492.4 25.6 %collective-permute-start.5 = (bf16[2,512,512]{2,1,0:T(8,128)(2,1)}, bf16[2,512,512]{2,1,0:T(8,128)(2,1)S(1)}, u32[]{:S(2)}, u32[]{:S(2)}) collective-permute-start(bf16[2,512,512]{2,1,0:T(8,128)(2,1)} %get-tuple-element.106), channel_id=1, source_target_pairs={{0,3},{1,2},{2,1},{3,0},{4,7},{5,6},{6,5},{7,4},{8,11},{9,10},{10,... | collective-permute-start | bytes 3145736 | tf_op jit(solution)/shard_map/ppermute | solution.py:359
  494.4 26.5 %copy-start.1 = (bf16[4096,256]{1,0:T(8,128)(2,1)S(1)}, bf16[4096,256]{1,0:T(8,128)(2,1)}, u32[]{:S(2)}) copy-start(bf16[4096,256]{1,0:T(8,128)(2,1)} %get-tuple-element.94) | copy-start | bytes 6291460
  518.0 1.0 copy-start.5
  519.0 34.8 %collective-permute-start = (bf16[2,512,768]{2,1,0:T(8,128)(2,1)}, bf16[2,512,768]{2,1,0:T(8,128)(2,1)S(1)}, u32[]{:S(2)}, u32[]{:S(2)}) collective-permute-start(bf16[2,512,768]{2,1,0:T(8,128)(2,1)} %get-tuple-element.96), channel_id=1, source_target_pairs={{0,1},{1,0},{2,3},{3,2},{4,5},{5,4},{6,7},{7,6},{8,9},{9,8},{10,11... | collective-permute-start | bytes 4718600 | tf_op jit(solution)/shard_map/ppermute | solution.py:359
  519.1 37.6 %collective-permute-start.1 = (bf16[2,512,768]{2,1,0:T(8,128)(2,1)}, bf16[2,512,768]{2,1,0:T(8,128)(2,1)}, u32[]{:S(2)}, u32[]{:S(2)}) collective-permute-start(bf16[2,512,768]{2,1,0:T(8,128)(2,1)} %get-tuple-element.97), channel_id=1, source_target_pairs={{0,4},{1,5},{2,6},{3,7},{4,0},{5,1},{6,2},{7,3},{8,12},{9,13},{10,... | collective-permute-start | bytes 4718600 | tf_op jit(solution)/shard_map/ppermute | solution.py:359
  520.1 69.1 %collective-permute-start.2 = (bf16[2,512,768]{2,1,0:T(8,128)(2,1)}, bf16[2,512,768]{2,1,0:T(8,128)(2,1)}, u32[]{:S(2)}, u32[]{:S(2)}) collective-permute-start(bf16[2,512,768]{2,1,0:T(8,128)(2,1)} %get-tuple-element.98), channel_id=1, source_target_pairs={{0,5},{1,4},{2,7},{3,6},{4,1},{5,0},{6,3},{7,2},{8,13},{9,12},{10,... | collective-permute-start | bytes 4718600 | tf_op jit(solution)/shard_map/ppermute | solution.py:359
  553.8 35.5 %copy-start.4 = (bf16[2,512,768]{2,1,0:T(8,128)(2,1)}, bf16[2,512,768]{2,1,0:T(8,128)(2,1)S(1)}, u32[]{:S(2)}) copy-start(bf16[2,512,768]{2,1,0:T(8,128)(2,1)S(1)} %collective-permute-done.refs_1_) | copy-start | bytes 4718596
  612.7 62.5 %collective-permute-start.12 = (bf16[256,4096]{1,0:T(8,128)(2,1)}, bf16[256,4096]{1,0:T(8,128)(2,1)}, u32[]{:S(2)}, u32[]{:S(2)}) collective-permute-start(bf16[256,4096]{1,0:T(8,128)(2,1)} %get-tuple-element.120), channel_id=1, source_target_pairs={{0,2},{1,3},{2,0},{3,1},{4,6},{5,7},{6,4},{7,5},{8,10},{9,11},{10,... | collective-permute-start | bytes 6291464 | tf_op jit(solution)/shard_map/ppermute | solution.py:359
  614.3 92.8 %collective-permute-start.13 = (bf16[512,4096]{1,0:T(8,128)(2,1)}, bf16[512,4096]{1,0:T(8,128)(2,1)}, u32[]{:S(2)}, u32[]{:S(2)}) collective-permute-start(bf16[512,4096]{1,0:T(8,128)(2,1)} %mix_mm.2), channel_id=1, source_target_pairs={{0,4},{1,5},{2,6},{3,7},{4,0},{5,1},{6,2},{7,3},{8,12},{9,13},{10,... | collective-permute-start | bytes 12582920 | tf_op jit(solution)/shard_map/ppermute | solution.py:359
  615.3 99.7 %collective-permute-start.14 = (bf16[256,4096]{1,0:T(8,128)(2,1)}, bf16[256,4096]{1,0:T(8,128)(2,1)S(1)}, u32[]{:S(2)}, u32[]{:S(2)}) collective-permute-start(bf16[256,4096]{1,0:T(8,128)(2,1)} %get-tuple-element.126), channel_id=1, source_target_pairs={{0,2},{1,3},{2,0},{3,1},{4,6},{5,7},{6,4},{7,5},{8,10},{9,11},{10,... | collective-permute-start | bytes 6291464 | tf_op jit(solution)/shard_map/ppermute | solution.py:359
  615.8 17.1 %copy-start.2 = (f32[4096,256]{1,0:T(8,128)S(1)}, f32[4096,256]{1,0:T(8,128)}, u32[]{:S(2)}) copy-start(f32[4096,256]{1,0:T(8,128)} %fusion.8) | copy-start | bytes 12582916
  715.1 1.3 copy-start.3
  724.3 1.4 collective-permute-start.15
  726.4 3.7 collective-permute-start.16
  730.1 3.7 collective-permute-start.17
Sparse Core Ops, SparseCore 0:
  15.2 159.6 all-gather.3
  177.3 85.9 all-gather.5
  265.8 85.9 all-gather.7
